TPU v7x, 32 devices: a whole 2x2x4 slice. The times are simulated.
32 devices in a mesh: dp: 2 (over x), tx: 4 (over z), ty: 4 (over y, core).
Axes of the slice: x: 2, y: 2, z: 4, core: 2. Of those that a mesh axis runs over, the one named last changes fastest.
Arguments:
- x_in: bfloat16 [64, 256, 1152], P('dp', None, 'tx'), parts along dimension 0
- ln1_gain: float32 [2, 1152], P(None, 'tx')
- ln1_bias: float32 [2, 1152], P(None, 'tx')
- w_q: bfloat16 [2, 1152, 16, 72], P(None, 'tx', 'ty')
- b_q: float32 [2, 16, 72], P(None, 'ty')
- w_k: bfloat16 [2, 1152, 16, 72], P(None, 'tx', 'ty')
- w_v: bfloat16 [2, 1152, 16, 72], P(None, 'tx', 'ty')
- b_v: float32 [2, 16, 72], P(None, 'ty')
- w_o: bfloat16 [2, 16, 72, 1152], P(None, 'ty', None, 'tx')
- b_o: float32 [2, 1152], P(None, 'tx')
- ln2_gain: float32 [2, 1152], P(None, 'tx')
- ln2_bias: float32 [2, 1152], P(None, 'tx')
- w_up: bfloat16 [2, 1152, 4304], P(None, 'tx', 'ty')
- b_up: float32 [2, 4304], P(None, 'ty')
- w_down: bfloat16 [2, 4304, 1152], P(None, 'ty', 'tx')
- b_down: float32 [2, 1152], P(None, 'tx')
Outputs:
- output: bfloat16 [64, 256, 1152], P('dp', None, 'tx'), parts along dimension 0
There are 2 independent parts. A program takes and returns all parts, laid end to end along the dimension named above; an argument that names none is the same for every part.
All inputs are finite; a program needn't handle non-finite values.
Results may differ from a plain program's by a relative error of at most 0.02.
Values are sent between devices in bfloat16 or wider.
A program may use at most 1 GiB of HBM per device.

v0:
```python
import jax
import jax.numpy as jnp
from jax import lax
from jax.sharding import PartitionSpec as P

EPS = 1e-6


def split_norm(x_f, gain, shift, width):
    moments = lax.psum(jnp.stack([jnp.sum(x_f, axis=-1), jnp.sum(x_f * x_f, axis=-1)]), "tx")
    mean = (moments[0] / width)[..., None]
    variance = (moments[1] / width)[..., None] - mean * mean
    return ((x_f - mean) * lax.rsqrt(variance + EPS) * gain + shift).astype(jnp.bfloat16)


def solution(mesh):
    tx_size = mesh.shape["tx"]
    act_spec = P("dp", None, "tx")
    vec_tx = P(None, "tx")
    proj_spec = P(None, "tx", "ty", None)
    head_vec = P(None, "ty", None)
    in_specs = (act_spec, vec_tx, vec_tx, proj_spec, head_vec, proj_spec, proj_spec, head_vec,
                P(None, "ty", None, "tx"), vec_tx, vec_tx, vec_tx,
                P(None, "tx", "ty"), P(None, "ty"), P(None, "ty", "tx"), vec_tx)

    def local_fn(x_in, ln1_gain, ln1_bias, w_q, b_q, w_k, w_v, b_v, w_o, b_o, ln2_gain, ln2_bias, w_up, b_up, w_down, b_down):
        width = x_in.shape[-1] * tx_size
        scale = w_q.shape[-1] ** -0.5
        residual = x_in
        for layer in range(w_q.shape[0]):
            x_f = residual.astype(jnp.float32)
            normed = split_norm(x_f, ln1_gain[layer], ln1_bias[layer], width)
            part_q = jnp.einsum("bnw,whd->bnhd", normed, w_q[layer], preferred_element_type=jnp.float32).astype(jnp.bfloat16)
            part_k = jnp.einsum("bnw,whd->bnhd", normed, w_k[layer], preferred_element_type=jnp.float32).astype(jnp.bfloat16)
            part_v = jnp.einsum("bnw,whd->bnhd", normed, w_v[layer], preferred_element_type=jnp.float32).astype(jnp.bfloat16)
            sum_q, k_proj, sum_v = lax.psum((part_q, part_k, part_v), "tx")
            q_proj = (sum_q.astype(jnp.float32) + b_q[layer]).astype(jnp.bfloat16)
            v_proj = (sum_v.astype(jnp.float32) + b_v[layer]).astype(jnp.bfloat16)
            scores = jnp.einsum("bqhd,bkhd->bhqk", q_proj, k_proj, preferred_element_type=jnp.float32) * scale
            attn_prob = jax.nn.softmax(scores, axis=-1).astype(jnp.bfloat16)
            attended = jnp.einsum("bhqk,bkhd->bqhd", attn_prob, v_proj, preferred_element_type=jnp.float32).astype(jnp.bfloat16)
            part_o = jnp.einsum("bqhd,hdw->bqw", attended, w_o[layer], preferred_element_type=jnp.float32).astype(jnp.bfloat16)
            x_mid = (x_f + lax.psum(part_o, "ty").astype(jnp.float32) + b_o[layer]).astype(jnp.bfloat16)
            mid_f = x_mid.astype(jnp.float32)
            normed2 = split_norm(mid_f, ln2_gain[layer], ln2_bias[layer], width)
            part_up = jnp.einsum("bnw,wf->bnf", normed2, w_up[layer], preferred_element_type=jnp.float32).astype(jnp.bfloat16)
            hidden = jax.nn.gelu(lax.psum(part_up, "tx").astype(jnp.float32) + b_up[layer], approximate=True).astype(jnp.bfloat16)
            part_down = jnp.einsum("bnf,fw->bnw", hidden, w_down[layer], preferred_element_type=jnp.float32).astype(jnp.bfloat16)
            residual = (mid_f + lax.psum(part_down, "ty").astype(jnp.float32) + b_down[layer]).astype(jnp.bfloat16)
        return residual

    return jax.shard_map(local_fn, mesh=mesh, in_specs=in_specs, out_specs=act_spec, check_vma=False)
```

profile of v0, /device:TPU:0, one launch (start us, length us, event | category | flops | bytes accessed | tf_op | source)
XLA Modules:
  0.0 2943.2 jit_solution(10310846510854568515)
XLA Ops:
  12.7 35.8 %all-reduce.15.cloned.1.call-done = f32[2,32,256]{2,1,0:T(8,128)} async-done(((f32[2,32,256]{2,1,0:T(8,128)}), f32[2,32,256]{2,1,0:T(8,128)}) %all-reduce.15.cloned.1.call-update) | async-done | bytes 65552 | tf_op jit(solution)/shard_map/psum | solution.py:10
  69.5 473.2 %all-reduce.37.cloned.1.call-done = (bf16[32,256,4,72]{1,3,2,0:T(8,128)(2,1)}, bf16[32,256,4,72]{1,3,2,0:T(8,128)(2,1)}, bf16[32,256,4,72]{1,3,2,0:T(8,128)(2,1)}) async-done(((bf16[32,256,4,72]{1,3,2,0:T(8,128)(2,1)}, bf16[32,256,4,72]{1,3,2,0:T(8,128)(2,1)}, bf16[32,256,4,72]{1,3,2,0:T(8,128)(2,1)}), (bf16[32,256,4,72]{1,3,2,0:T(8,128)(2,1)}, bf16[32,256,4,72]{1,3,2,0:T(8,128)(2,1)}, ...) | async-done | bytes 14155792 | tf_op jit(solution)/shard_map/psum | solution.py:36
  542.6 16.2 fusion.60
  558.9 34.8 %fusion.159 = (f32[32,4,256]{2,1,0:T(4,128)S(1)}, f32[32,4,256,256]{2,3,1,0:T(8,128)}) fusion(f32[32,4,256,256]{2,3,1,0:T(8,128)} %fusion.60), kind=kOutput, calls=%fused_computation.200 | output fusion | flops 33554688 | bytes 67239936 | tf_op jit(solution)/shard_map/sub | solution.py:40
  593.7 16.7 bitcast_convert_fusion.1
  611.1 92.2 %all-reduce.17.cloned.1.call-done = bf16[32,256,288]{1,2,0:T(8,128)(2,1)} async-done(((bf16[32,256,288]{1,2,0:T(8,128)(2,1)}), bf16[32,256,288]{1,2,0:T(8,128)(2,1)}) %all-reduce.17.cloned.1.call-update) | async-done | bytes 4718608 | tf_op jit(solution)/shard_map/psum | solution.py:43
  703.4 8.9 convert_reduce_fusion.2
  713.8 33.7 %all-reduce.19.cloned.1.call-done = f32[2,32,256]{2,1,0:T(8,128)} async-done(((f32[2,32,256]{2,1,0:T(8,128)}), f32[2,32,256]{2,1,0:T(8,128)}) %all-reduce.19.cloned.1.call-update) | async-done | bytes 65552 | tf_op jit(solution)/shard_map/psum | solution.py:10
  749.1 16.1 convolution_convert_fusion.1
  766.5 587.2 %all-reduce.21.cloned.1.call-done = bf16[32,256,1076]{1,2,0:T(8,128)(2,1)} async-done(((bf16[32,256,1076]{1,2,0:T(8,128)(2,1)}), bf16[32,256,1076]{1,2,0:T(8,128)(2,1)}) %all-reduce.21.cloned.1.call-update) | async-done | bytes 17629200 | tf_op jit(solution)/shard_map/psum | solution.py:47
  1353.8 19.6 fusion.90
  1374.0 92.2 %all-reduce.23.cloned.1.call-done = bf16[32,256,288]{1,2,0:T(8,128)(2,1)} async-done(((bf16[32,256,288]{1,2,0:T(8,128)(2,1)}), bf16[32,256,288]{1,2,0:T(8,128)(2,1)}) %all-reduce.23.cloned.1.call-update) | async-done | bytes 4718608 | tf_op jit(solution)/shard_map/psum | solution.py:49
  1476.3 34.2 %all-reduce.25.cloned.1.call-done = f32[2,32,256]{2,1,0:T(8,128)} async-done(((f32[2,32,256]{2,1,0:T(8,128)}), f32[2,32,256]{2,1,0:T(8,128)}) %all-reduce.25.cloned.1.call-update) | async-done | bytes 65552 | tf_op jit(solution)/shard_map/psum | solution.py:10
  1530.0 474.8 %all-reduce.35.cloned.1.call-done = (bf16[32,256,4,72]{1,3,2,0:T(8,128)(2,1)}, bf16[32,256,4,72]{1,3,2,0:T(8,128)(2,1)}, bf16[32,256,4,72]{1,3,2,0:T(8,128)(2,1)}) async-done(((bf16[32,256,4,72]{1,3,2,0:T(8,128)(2,1)}, bf16[32,256,4,72]{1,3,2,0:T(8,128)(2,1)}, bf16[32,256,4,72]{1,3,2,0:T(8,128)(2,1)}), (bf16[32,256,4,72]{1,3,2,0:T(8,128)(2,1)}, bf16[32,256,4,72]{1,3,2,0:T(8,128)(2,1)}, ...) | async-done | bytes 14155792 | tf_op jit(solution)/shard_map/psum | solution.py:36
  2004.8 16.2 fusion.61
  2021.0 34.8 %fusion.160 = (f32[32,4,256]{2,1,0:T(4,128)S(1)}, f32[32,4,256,256]{2,3,1,0:T(8,128)}) fusion(f32[32,4,256,256]{2,3,1,0:T(8,128)} %fusion.61), kind=kOutput, calls=%fused_computation.201 | output fusion | flops 33554688 | bytes 67239936 | tf_op jit(solution)/shard_map/sub | solution.py:40
  2055.8 16.8 bitcast_convert_fusion
  2072.8 92.8 %all-reduce.27.cloned.1.call-done = bf16[32,256,288]{1,2,0:T(8,128)(2,1)} async-done(((bf16[32,256,288]{1,2,0:T(8,128)(2,1)}), bf16[32,256,288]{1,2,0:T(8,128)(2,1)}) %all-reduce.27.cloned.1.call-update) | async-done | bytes 4718608 | tf_op jit(solution)/shard_map/psum | solution.py:43
  2165.6 8.9 convert_reduce_fusion
  2175.4 34.4 %all-reduce.29.cloned.1.call-done = f32[2,32,256]{2,1,0:T(8,128)} async-done(((f32[2,32,256]{2,1,0:T(8,128)}), f32[2,32,256]{2,1,0:T(8,128)}) %all-reduce.29.cloned.1.call-update) | async-done | bytes 65552 | tf_op jit(solution)/shard_map/psum | solution.py:10
  2211.4 16.1 convolution_convert_fusion
  2227.6 588.5 %all-reduce.31.cloned.1.call-done = bf16[32,256,1076]{1,2,0:T(8,128)(2,1)} async-done(((bf16[32,256,1076]{1,2,0:T(8,128)(2,1)}), bf16[32,256,1076]{1,2,0:T(8,128)(2,1)}) %all-reduce.31.cloned.1.call-update) | async-done | bytes 17629200 | tf_op jit(solution)/shard_map/psum | solution.py:47
  2816.0 19.5 fusion.93
  2835.6 92.9 %all-reduce.33.cloned.1.call-done = bf16[32,256,288]{1,2,0:T(8,128)(2,1)} async-done(((bf16[32,256,288]{1,2,0:T(8,128)(2,1)}), bf16[32,256,288]{1,2,0:T(8,128)(2,1)}) %all-reduce.33.cloned.1.call-update) | async-done | bytes 4718608 | tf_op jit(solution)/shard_map/psum | solution.py:49
  (112 shorter events, 72.5 us)
Async XLA Ops:
  6.5 41.9 %all-reduce.15.cloned.1.call-start = ((), (), s32[]{:S(2)}) async-start(), calls=%async_computation | async-start | bytes 131072 | tf_op jit(solution)/shard_map/psum | solution.py:10
  11.3 531.4 %all-reduce.37.cloned.1.call-start = ((), (), s32[]{:S(2)}) async-start(), calls=%async_computation.11 | async-start | bytes 28311552 | tf_op jit(solution)/shard_map/psum | solution.py:36
  67.6 635.7 %all-reduce.17.cloned.1.call-start = ((), (), s32[]{:S(2)}) async-start(), calls=%async_computation.1 | async-start | bytes 9437184 | tf_op jit(solution)/shard_map/psum | solution.py:43
  610.4 138.7 %copy-start.16 = (bf16[2,288,1076]{2,1,0:T(8,128)(2,1)S(1)}, bf16[2,288,1076]{2,1,0:T(8,128)(2,1)}, u32[]{:S(2)}) copy-start(bf16[2,288,1076]{2,1,0:T(8,128)(2,1)} %param.28) | copy-start | bytes 3718660
  610.5 137.1 %all-reduce.19.cloned.1.call-start = ((), (), s32[]{:S(2)}) async-start(), calls=%async_computation.2 | async-start | bytes 131072 | tf_op jit(solution)/shard_map/psum | solution.py:10
  712.9 640.9 %all-reduce.21.cloned.1.call-start = ((), (), s32[]{:S(2)}) async-start(), calls=%async_computation.3 | async-start | bytes 35389440 | tf_op jit(solution)/shard_map/psum | solution.py:47
  765.2 588.6 %copy-start.18 = (bf16[2,1076,288]{1,2,0:T(8,128)(2,1)S(1)}, bf16[2,1076,288]{1,2,0:T(8,128)(2,1)}, u32[]{:S(2)}) copy-start(bf16[2,1076,288]{1,2,0:T(8,128)(2,1)} %param.30) | copy-start | bytes 3718660
  765.3 701.0 %all-reduce.23.cloned.1.call-start = ((), (), s32[]{:S(2)}) async-start(), calls=%async_computation.4 | async-start | bytes 9437184 | tf_op jit(solution)/shard_map/psum | solution.py:49
  1373.3 138.7 %copy-start.11 = (f32[288]{0:T(512)S(1)}, f32[288]{0:T(512)}, u32[]{:S(2)}) copy-start(f32[288]{0:T(512)} %get-tuple-element.25) | copy-start | bytes 3460
  1373.3 138.7 %copy-start.12 = (f32[288]{0:T(512)S(1)}, f32[288]{0:T(512)}, u32[]{:S(2)}) copy-start(f32[288]{0:T(512)} %get-tuple-element.45) | copy-start | bytes 3460
  1373.4 138.7 %copy-start.19 = (bf16[2,288,4,72]{1,3,2,0:T(8,128)(2,1)S(1)}, bf16[2,288,4,72]{1,3,2,0:T(8,128)(2,1)}, u32[]{:S(2)}) copy-start(bf16[2,288,4,72]{1,3,2,0:T(8,128)(2,1)} %param.19) | copy-start | bytes 995332
  1373.4 137.1 %all-reduce.25.cloned.1.call-start = ((), (), s32[]{:S(2)}) async-start(), calls=%async_computation.5 | async-start | bytes 131072 | tf_op jit(solution)/shard_map/psum | solution.py:10
  1475.8 528.9 %all-reduce.35.cloned.1.call-start = ((), (), s32[]{:S(2)}) async-start(), calls=%async_computation.10 | async-start | bytes 28311552 | tf_op jit(solution)/shard_map/psum | solution.py:36
  1529.7 475.0 %copy-start = (f32[4,72]{1,0:T(4,128)S(1)}, f32[4,72]{1,0:T(4,128)}, u32[]{:S(2)}) copy-start(f32[4,72]{1,0:T(4,128)} %get-tuple-element.38) | copy-start | bytes 3460
  1529.8 635.8 %all-reduce.27.cloned.1.call-start = ((), (), s32[]{:S(2)}) async-start(), calls=%async_computation.6 | async-start | bytes 9437184 | tf_op jit(solution)/shard_map/psum | solution.py:43
  2055.8 109.7 %copy-start.3 = (f32[288]{0:T(512)S(1)}, f32[288]{0:T(512)}, u32[]{:S(2)}) copy-start(f32[288]{0:T(512)} %get-tuple-element.21) | copy-start | bytes 3460
  2072.7 138.7 %copy-start.13 = (f32[288]{0:T(512)S(1)}, f32[288]{0:T(512)}, u32[]{:S(2)}) copy-start(f32[288]{0:T(512)} %get-tuple-element.19) | copy-start | bytes 3460
  2072.7 138.7 %copy-start.14 = (f32[288]{0:T(512)S(1)}, f32[288]{0:T(512)}, u32[]{:S(2)}) copy-start(f32[288]{0:T(512)} %get-tuple-element.47) | copy-start | bytes 3460
  2072.7 138.7 %copy-start.17 = (bf16[2,288,1076]{2,1,0:T(8,128)(2,1)S(1)}, bf16[2,288,1076]{2,1,0:T(8,128)(2,1)}, u32[]{:S(2)}) copy-start(bf16[2,288,1076]{2,1,0:T(8,128)(2,1)} %param.28) | copy-start | bytes 3718660
  2072.7 137.1 %all-reduce.29.cloned.1.call-start = ((), (), s32[]{:S(2)}) async-start(), calls=%async_computation.7 | async-start | bytes 131072 | tf_op jit(solution)/shard_map/psum | solution.py:10
  2175.2 640.9 %all-reduce.31.cloned.1.call-start = ((), (), s32[]{:S(2)}) async-start(), calls=%async_computation.8 | async-start | bytes 35389440 | tf_op jit(solution)/shard_map/psum | solution.py:47
  2227.5 588.6 %copy-start.2 = (f32[1076]{0:T(1024)S(1)}, f32[1076]{0:T(1024)}, u32[]{:S(2)}) copy-start(f32[1076]{0:T(1024)} %get-tuple-element.13) | copy-start | bytes 12916
  2227.5 701.0 %all-reduce.33.cloned.1.call-start = ((), (), s32[]{:S(2)}) async-start(), calls=%async_computation.9 | async-start | bytes 9437184 | tf_op jit(solution)/shard_map/psum | solution.py:49
  2816.0 112.5 %copy-start.4 = (f32[288]{0:T(512)S(1)}, f32[288]{0:T(512)}, u32[]{:S(2)}) copy-start(f32[288]{0:T(512)} %get-tuple-element.15) | copy-start | bytes 3460
  (17 other events, 523.9 us)
Sparse Core Ops, SparseCore 0:
  11.4 37.0 all-reduce.14
  67.8 474.7 all-reduce.36
  610.6 92.7 all-reduce.16
  713.1 34.4 all-reduce.18
  765.4 588.3 all-reduce.20
  1373.5 92.7 all-reduce.22
  1476.0 34.4 all-reduce.24
  1529.9 474.8 all-reduce.34
  2072.8 92.7 all-reduce.26
  2175.3 34.4 all-reduce.28
  2227.6 588.3 all-reduce.30
  2835.7 92.7 all-reduce.32
where the time goes:
time: 2950 us; the launch traced here: 2940 us
  waiting for transfers between devices  2630 us (89%)
  matrix products  173 us (6%)
  other arithmetic  117 us (4%)
    psum x2, waiting for transfers between devices, local_fn(): lax.psum(part_up, 'tx').astype(jnp.float32) + b_up[layer]  1180 us
    psum x2, waiting for transfers between devices, local_fn(): sum_q, k_proj, sum_v = lax.psum((part_q, part_k, part_v), 'tx')  948 us
    psum x2, waiting for transfers between devices, local_fn(): lax.psum(part_down, 'ty').astype(jnp.float32)  185 us
    psum x2, waiting for transfers between devices, local_fn(): lax.psum(part_o, 'ty').astype(jnp.float32)  185 us
    psum x4, waiting for transfers between devices, split_norm(): lax.psum(jnp.stack([jnp.sum(x_f, axis=-1), jnp.sum(x_f * x_f, axis=-1)]),...  138 us
    sub x2, other arithmetic, local_fn(): attn_prob = jax.nn.softmax(scores, axis=-1).astype(jnp.bfloat16)  69.7 us
  transfers between devices with their start and end apart: 12, of which 12 were waited for; matrix products, arithmetic and copies ran while one was open for 0% of the time, Pallas kernels for 0%

commit v1 on v0

v1 whole, which is shorter than its diff:
```python
import jax
import jax.numpy as jnp
from jax import lax
from jax.experimental import pallas as pl
from jax.experimental.pallas import tpu as pltpu
from jax.sharding import PartitionSpec as P

EPS = 1e-6
BF = jnp.bfloat16
F32 = jnp.float32
LANES = 128
VMEM_BYTES = 60 * 1024 * 1024


def norm_rows(x_f, gain, shift):
    mean = jnp.mean(x_f, axis=-1, keepdims=True)
    centred = x_f - mean
    variance = jnp.mean(centred * centred, axis=-1, keepdims=True)
    return (centred * lax.rsqrt(variance + EPS) * gain + shift).astype(BF)


def dot_nn(a, b):
    return lax.dot_general(a, b, (((1,), (0,)), ((), ())), preferred_element_type=F32)


def dot_nt(a, b):
    return lax.dot_general(a, b, (((1,), (1,)), ((), ())), preferred_element_type=F32)


def attention_kernel(heads, dim, toks, x_ref, gain_ref, shift_ref, bias_ref, bo_ref, w_ref, out_ref, h_ref, acc_ref):
    step = pl.program_id(0)
    width = x_ref.shape[-1]
    hd = heads * dim
    span = -(-hd // LANES) * LANES

    @pl.when(step == 0)
    def _():
        h_ref[...] = norm_rows(x_ref[...].astype(F32), gain_ref[...], shift_ref[...])
        acc_ref[...] = jnp.zeros_like(acc_ref)

    w = w_ref[...].reshape(width, w_ref.shape[-1])
    cols = w.shape[-1]
    qkv = dot_nn(h_ref[...], w) + bias_ref[0]
    q_f = qkv[:, :span]
    k = pltpu.roll(qkv, cols - hd, 1)[:, :span].astype(BF)
    v = pltpu.roll(qkv, hd, 1)[:, cols - span:].astype(BF)
    lane = lax.broadcasted_iota(jnp.int32, (toks, span), 1)
    outs = []
    for img in range(x_ref.shape[0] // toks):
        rows = slice(img * toks, (img + 1) * toks)
        q_i, k_i, v_i = q_f[rows], k[rows], v[rows]
        o_i = jnp.zeros((toks, span), F32)
        for head in range(heads):
            q_h = jnp.where((lane >= head * dim) & (lane < (head + 1) * dim), q_i, 0.0).astype(BF)
            s = dot_nt(q_h, k_i) * (dim ** -0.5)
            e = jnp.exp(s - jnp.max(s, axis=-1, keepdims=True))
            p = (e / jnp.sum(e, axis=-1, keepdims=True)).astype(BF)
            lo = span - hd + head * dim
            o_i = jnp.where((lane >= lo) & (lane < lo + dim), dot_nn(p, v_i), o_i)
        outs.append(o_i)
    acc_ref[...] += dot_nt(jnp.concatenate(outs, axis=0).astype(BF), w[:, cols - span:])

    @pl.when(step == pl.num_programs(0) - 1)
    def _():
        out_ref[...] = (x_ref[...].astype(F32) + acc_ref[...] + bo_ref[...]).astype(BF)


def mlp_kernel(toks, x_ref, gain_ref, shift_ref, bias_ref, bd_ref, up_ref, down_ref, out_ref, h_ref, acc_ref):
    step = pl.program_id(0)
    width = x_ref.shape[-1]

    @pl.when(step == 0)
    def _():
        h_ref[...] = norm_rows(x_ref[...].astype(F32), gain_ref[...], shift_ref[...])
        acc_ref[...] = jnp.zeros_like(acc_ref)

    up = up_ref[...].reshape(width, up_ref.shape[-1])
    down = down_ref[...].reshape(width, down_ref.shape[-1])
    u = jax.nn.gelu(dot_nn(h_ref[...], up) + bias_ref[0], approximate=True).astype(BF)
    acc_ref[...] += dot_nt(u, down)

    @pl.when(step == pl.num_programs(0) - 1)
    def _():
        y = x_ref[...].astype(F32) + acc_ref[...] + bd_ref[...]
        if out_ref.shape == x_ref.shape:
            out_ref[...] = y.astype(BF)
        else:
            wl = out_ref.shape[2]
            y_t = y.T.astype(BF)
            for c in range(out_ref.shape[0]):
                for img in range(out_ref.shape[1]):
                    out_ref[c, img] = y_t[c * wl:(c + 1) * wl, img * toks:(img + 1) * toks]


def solution(mesh):
    tx, ty = mesh.shape["tx"], mesh.shape["ty"]
    act_spec = P("dp", None, "tx")
    vec_tx = P(None, "tx")
    proj_spec = P(None, "tx", "ty", None)
    head_vec = P(None, "ty", None)
    in_specs = (act_spec, vec_tx, vec_tx, proj_spec, head_vec, proj_spec, proj_spec, head_vec,
                P(None, "ty", None, "tx"), vec_tx, vec_tx, vec_tx,
                P(None, "tx", "ty"), P(None, "ty"), P(None, "ty", "tx"), vec_tx)

    def local_fn(x_in, ln1_gain, ln1_bias, w_q, b_q, w_k, w_v, b_v, w_o, b_o, ln2_gain, ln2_bias, w_up, b_up, w_down, b_down):
        layers, wl, hl, dim = w_q.shape
        fl = w_up.shape[-1]
        imgs, toks, _ = x_in.shape
        hd = hl * dim
        width = wl * tx
        cols = max(4 * hd, -(-fl // LANES) * LANES)
        per = imgs // ty
        nb = per // tx
        n = nb * toks

        def proj_block(l):
            rows = [w[l].transpose(1, 2, 0).reshape(hd, wl) for w in (w_q, w_k, w_v)] + [w_o[l].reshape(hd, wl)]
            return jnp.pad(jnp.concatenate(rows, axis=0).T, ((0, 0), (0, cols - 4 * hd)))

        def up_block(l):
            return jnp.pad(w_up[l], ((0, 0), (0, cols - fl)))

        def down_block(l):
            return jnp.pad(w_down[l].T, ((0, 0), (0, cols - fl)))

        blocks = []
        for l in range(layers):
            blocks += [("a", l, proj_block), ("u", l, up_block), ("d", l, down_block)]
        where = {}
        gathered = []
        for i in range(0, len(blocks), 2):
            pair = blocks[i:i + 2]
            for j, (kind, l, _) in enumerate(pair):
                where[kind, l] = (len(gathered), j)
            with jax.named_scope(f"gather{i // 2}"):
                local = jnp.stack([make(l) for _, l, make in pair])
                full = lax.all_gather(local.reshape(len(pair) * wl, cols), ("tx", "ty"), axis=0)
            gathered.append(full.reshape(tx, ty, len(pair), wl, cols))

        with jax.named_scope("entry"):
            mine = lax.dynamic_slice_in_dim(x_in.transpose(0, 2, 1), lax.axis_index("ty") * per, per, axis=0)
            x_t = lax.all_to_all(mine, "tx", split_axis=0, concat_axis=0, tiled=True)
            x = x_t.reshape(tx, nb, wl, toks).transpose(1, 3, 0, 2).reshape(n, width)
        with jax.named_scope("vectors"):
            on_tx = [ln1_gain, ln1_bias, ln2_gain, ln2_bias, b_o, b_down]
            on_ty = [b_q.reshape(layers, hd), b_v.reshape(layers, hd), b_up]
            vec = lax.all_gather(jnp.concatenate([a.reshape(1, -1) for a in on_tx + on_ty], axis=1), ("tx", "ty"), axis=0)
            vec = vec.reshape(tx, ty, -1)
            at = len(on_tx) * layers * wl
            vt = vec[:, 0, :at].reshape(tx, len(on_tx), layers, wl).transpose(1, 2, 0, 3).reshape(len(on_tx), layers, 1, width)
            vq = vec[0, :, at:at + layers * hd].reshape(ty, layers, hd)
            vv = vec[0, :, at + layers * hd:at + 2 * layers * hd].reshape(ty, layers, hd)
            vu = vec[0, :, at + 2 * layers * hd:].reshape(ty, layers, fl)
            gap = jnp.zeros_like(vq)
            tail = jnp.zeros((ty, layers, cols - 4 * hd), F32)
            bias_a = jnp.concatenate([vq, gap, vv, gap, tail], axis=2).transpose(1, 0, 2).reshape(layers, ty, 1, cols)
            bias_u = jnp.pad(vu, ((0, 0), (0, 0), (0, cols - fl))).transpose(1, 0, 2).reshape(layers, ty, 1, cols)

        whole = pl.BlockSpec((n, width), lambda i: (0, 0))
        row = pl.BlockSpec((1, width), lambda i: (0, 0))
        bias = pl.BlockSpec((1, 1, cols), lambda i: (i, 0, 0))
        scratch = [pltpu.VMEM((n, width), BF), pltpu.VMEM((n, width), F32)]
        params = pltpu.CompilerParams(vmem_limit_bytes=VMEM_BYTES, dimension_semantics=("arbitrary",))

        def weight(kind, l):
            g, j = where[kind, l]
            return gathered[g], pl.BlockSpec((tx, 1, 1, wl, cols), lambda i: (0, i, j, 0, 0))

        for l in range(layers):
            w_a, spec_a = weight("a", l)
            with jax.named_scope(f"attention{l}"):
                x = pl.pallas_call(
                    lambda *refs: attention_kernel(hl, dim, toks, *refs),
                    grid=(ty,),
                    in_specs=[whole, row, row, bias, row, spec_a],
                    out_specs=whole,
                    out_shape=jax.ShapeDtypeStruct((n, width), BF),
                    scratch_shapes=scratch,
                    compiler_params=params,
                    name="attention",
                    cost_estimate=pl.CostEstimate(flops=2 * n * width * width * 5, bytes_accessed=2 * width * width * 4, transcendentals=n * toks * 16),
                )(x, vt[0, l], vt[1, l], bias_a[l], vt[4, l], w_a)
            w_u, spec_u = weight("u", l)
            w_d, spec_d = weight("d", l)
            last = l == layers - 1
            out = (tx, nb, wl, toks) if last else (n, width)
            with jax.named_scope(f"mlp{l}"):
                x = pl.pallas_call(
                    lambda *refs: mlp_kernel(toks, *refs),
                    grid=(ty,),
                    in_specs=[whole, row, row, bias, row, spec_u, spec_d],
                    out_specs=pl.BlockSpec(out, lambda i, r=len(out): (0,) * r),
                    out_shape=jax.ShapeDtypeStruct(out, BF),
                    scratch_shapes=scratch,
                    compiler_params=params,
                    name="mlp",
                    cost_estimate=pl.CostEstimate(flops=2 * n * width * cols * ty * 2, bytes_accessed=4 * width * cols * ty, transcendentals=n * cols * ty),
                )(x, vt[2, l], vt[3, l], bias_u[l], vt[5, l], w_u, w_d)
        with jax.named_scope("exit"):
            y = lax.all_to_all(x.reshape(tx * nb, wl, toks), "tx", split_axis=0, concat_axis=0, tiled=True)
            y = lax.all_gather(y, "ty", axis=0, tiled=True)
        return y.transpose(0, 2, 1)

    return jax.shard_map(local_fn, mesh=mesh, in_specs=in_specs, out_specs=act_spec, check_vma=False)
```

time: 2950 us -> 477 us (0.16)
  waiting for transfers between devices: 2630 us -> 255 us
  matrix products: 173 us -> 0 us
  other arithmetic: 117 us -> 3.13 us
  blocking collectives: 0 us -> 92.2 us
  Pallas kernels: 0 us -> 82 us
    psum x12 -> x0, waiting for transfers between devices: 2630 us -> none  [the longest x2 1180 us: local_fn(): lax.psum(part_up, 'tx').astype(jnp.float32) + b_up[layer]]
    all_gather x0 -> x4, waiting for transfers between devices: none -> 255 us  [the longest x3 220 us: local_fn(): lax.all_gather(local.reshape(len(pair) * wl, cols), ('tx', 'ty'), axis=0)]
    dot_general x14 -> x0, matrix products: 173 us -> none  [the longest x2 39.1 us: local_fn(): jnp.einsum('bnf,fw->bnw', hidden, w_down[layer], preferred_element_type=j...]
    pallas_call x0 -> x4, Pallas kernels: none -> 82 us  [the longest x2 42.4 us: local_fn(): pl.pallas_call(lambda *refs: attention_kernel(hl, dim, toks, *refs), grid...]
    sub x2 -> x0, other arithmetic: 69.7 us -> none  [local_fn(): attn_prob = jax.nn.softmax(scores, axis=-1).astype(jnp.bfloat16)]
    all_gather x0 -> x1, blocking collectives: none -> 56.8 us  [local_fn(): lax.all_gather(jnp.concatenate([a.reshape(1, -1) for a in on_tx + on_ty],...]
    all_to_all x0 -> x1, blocking collectives: none -> 35.4 us  [local_fn(): lax.all_to_all(x.reshape(tx * nb, wl, toks), 'tx', split_axis=0, concat_a...]
    reduce_sum x4 -> x0, other arithmetic: 30.8 us -> none  [split_norm(): jnp.sum(x_f, axis=-1)]
  transfers between devices with their start and end apart: 12 -> 5, of which waited for: 12 -> 4; matrix products, arithmetic and copies ran while one was open for 0% -> 3% of each run, Pallas kernels for 0% -> 13%
where the time goes in v1:
time: 477 us; the launch traced here: 476 us
  waiting for transfers between devices  255 us (53%)
  blocking collectives  92.2 us (19%)
  Pallas kernels  82 us (17%)
  local copies, waits for them, and re-layouts  24.1 us (5%)
  between operations  13.4 us (3%)
  starting transfers between devices  6.61 us (1%)
    all_gather x3, waiting for transfers between devices, local_fn(): lax.all_gather(local.reshape(len(pair) * wl, cols), ('tx', 'ty'), axis=0)  220 us
    all_gather x1, blocking collectives, local_fn(): lax.all_gather(jnp.concatenate([a.reshape(1, -1) for a in on_tx + on_ty],...  56.8 us
    pallas_call x2, Pallas kernels, local_fn(): pl.pallas_call(lambda *refs: attention_kernel(hl, dim, toks, *refs), grid...  42.4 us
    pallas_call x2, Pallas kernels, local_fn(): pl.pallas_call(lambda *refs: mlp_kernel(toks, *refs), grid=(ty,), in_spec...  39.6 us
    all_to_all x1, blocking collectives, local_fn(): lax.all_to_all(x.reshape(tx * nb, wl, toks), 'tx', split_axis=0, concat_a...  35.4 us
    all_gather x1, waiting for transfers between devices, local_fn(): y = lax.all_gather(y, 'ty', axis=0, tiled=True)  34.7 us
  transfers between devices with their start and end apart: 5, of which 4 were waited for; matrix products, arithmetic and copies ran while one was open for 3% of the time, Pallas kernels for 13%

profile of v1, /device:TPU:0, one launch (start us, length us, event | category | flops | bytes accessed | tf_op | source)
XLA Modules:
  0.0 476.3 jit_solution(4545640373467264489)
XLA Ops:
  6.5 1.4 slice_bitcast_fusion.1
  9.7 0.7 fusion
  10.8 1.6 copy.47
  12.5 1.4 slice_bitcast_fusion
  14.4 0.8 copy-done
  15.7 1.7 copy.50
  17.5 1.2 pad_maximum_fusion.2
  18.8 2.4 dynamic-slice_bitcast_fusion
  21.2 6.5 %all-to-all-start = ((bf16[8,288,256]{2,1,0:T(8,128)(2,1)}), bf16[8,288,256]{2,1,0:T(8,128)(2,1)S(1)}, u32[]{:S(2)}, u32[]{:S(2)}) async-start(bf16[8,288,256]{2,1,0:T(8,128)(2,1)} %dynamic-slice_bitcast_fusion), calls=%async_computation | async-start | bytes 2359296 | tf_op jit(solution)/shard_map/entry/all_to_all | solution.py:142
  28.7 56.8 %all-gather.1 = f32[16,1,6760]{2,1,0:T(1,128)S(1)} all-gather(f32[1,1,6760]{2,1,0:T(1,128)S(1)} %bitcast.138), channel_id=2, replica_groups=mesh['dp'=2,'tx'=4,'ty'=4] {'tx','ty'}, dimensions={0}, use_global_device_ids=true | all-gather | bytes 459680 | tf_op jit(solution)/shard_map/vectors/all_gather | solution.py:147
  85.5 1.0 reduce
  87.7 0.7 slice_bitcast_fusion.6
  89.7 1.2 copy.44
  91.2 1.6 copy.48.refs_0_
  92.8 53.1 %all-gather.7.cloned.1.call-done = bf16[16,576,1152]{2,1,0:T(8,128)(2,1)} async-done(((bf16[1,576,1152]{2,1,0:T(8,128)(2,1)}), bf16[16,576,1152]{2,1,0:T(8,128)(2,1)}) %all-gather.7.cloned.1.call-update) | async-done | bytes 21233680 | tf_op jit(solution)/shard_map/gather0/all_gather | solution.py:137
  145.9 21.1 %attention.2.refs_0_ = bf16[512,1152]{1,0:T(8,128)(2,1)} custom-call(bf16[512,1152]{1,0:T(8,128)(2,1)} %copy.48.refs_0_, f32[1,1152]{1,0:T(1,128)} %get-tuple-element.30.refs_1_, f32[1,1152]{1,0:T(1,128)} %get-tuple-element.29.refs_2_, f32[4,1,1152]{2,1,0:T(1,128)} %get-tuple-element.34.refs_3_, f32[1,1152]{1,0:T(1,128)} %get-tuple-element.28.refs_4_, ...), custom_call_target="tpu_custom_call" | custom-call | flops 6794772480 | bytes 10616832 | tf_op jit(solution)/shard_map/attention0/attention/pallas_call | solution.py:172
  166.9 96.5 %all-gather.9.cloned.1.call-done = bf16[16,576,1152]{2,1,0:T(8,128)(2,1)} async-done(((bf16[1,576,1152]{2,1,0:T(8,128)(2,1)}), bf16[16,576,1152]{2,1,0:T(8,128)(2,1)}) %all-gather.9.cloned.1.call-update) | async-done | bytes 21233680 | tf_op jit(solution)/shard_map/gather1/all_gather | solution.py:137
  263.5 19.7 %mlp.2.refs_0_ = bf16[512,1152]{1,0:T(8,128)(2,1)} custom-call(bf16[512,1152]{1,0:T(8,128)(2,1)} %attention.2.refs_0_, f32[1,1152]{1,0:T(1,128)} %get-tuple-element.27.refs_1_, f32[1,1152]{1,0:T(1,128)} %get-tuple-element.26.refs_2_, f32[4,1,1152]{2,1,0:T(1,128)} %get-tuple-element.32.refs_3_, f32[1,1152]{1,0:T(1,128)} %get-tuple-element.25.refs_4_, ...), custom_call_target="tpu_custom_call" | custom-call | flops 10871635968 | bytes 21233664 | tf_op jit(solution)/shard_map/mlp0/mlp/pallas_call | solution.py:188
  283.2 21.3 %attention.3.refs_0_ = bf16[512,1152]{1,0:T(8,128)(2,1)} custom-call(bf16[512,1152]{1,0:T(8,128)(2,1)} %mlp.2.refs_0_, f32[1,1152]{1,0:T(1,128)} %get-tuple-element.24.refs_1_, f32[1,1152]{1,0:T(1,128)} %get-tuple-element.23.refs_2_, f32[4,1,1152]{2,1,0:T(1,128)} %get-tuple-element.33.refs_3_, f32[1,1152]{1,0:T(1,128)} %get-tuple-element.22.refs_4_, ...), custom_call_target="tpu_custom_call" | custom-call | flops 6794772480 | bytes 10616832 | tf_op jit(solution)/shard_map/attention1/attention/pallas_call | solution.py:172
  304.5 70.5 %all-gather.11.cloned.1.call-done = bf16[16,576,1152]{2,1,0:T(8,128)(2,1)} async-done(((bf16[1,576,1152]{2,1,0:T(8,128)(2,1)}), bf16[16,576,1152]{2,1,0:T(8,128)(2,1)}) %all-gather.11.cloned.1.call-update) | async-done | bytes 21233680 | tf_op jit(solution)/shard_map/gather2/all_gather | solution.py:137
  375.0 19.9 %mlp.3 = bf16[4,2,288,256]{3,2,1,0:T(8,128)(2,1)} custom-call(bf16[512,1152]{1,0:T(8,128)(2,1)} %attention.3.refs_0_, f32[1,1152]{1,0:T(1,128)} %get-tuple-element.21.refs_1_, f32[1,1152]{1,0:T(1,128)} %get-tuple-element.20.refs_2_, f32[4,1,1152]{2,1,0:T(1,128)} %get-tuple-element.31.refs_3_, f32[1,1152]{1,0:T(1,128)} %get-tuple-element.19.refs_4_, ...), custom_call_target="tpu_custom_call" | custom-call | flops 10871635968 | bytes 21233664 | tf_op jit(solution)/shard_map/mlp1/mlp/pallas_call | solution.py:188
  394.9 35.4 %all_to_all.10 = bf16[8,288,256]{2,1,0:T(8,128)(2,1)} all-to-all(bf16[8,288,256]{2,1,0:T(8,128)(2,1)} %bitcast.121), channel_id=1, replica_groups=mesh['dp'=2,'tx'=4,'ty'=4] {'tx'}, dimensions={0} | all-to-all | bytes 2359296 | tf_op jit(solution)/shard_map/exit/all_to_all | solution.py:200
  430.3 34.7 %all-gather.13.cloned.1.call-done = bf16[32,288,256]{2,1,0:T(8,128)(2,1)} async-done(((bf16[8,288,256]{2,1,0:T(8,128)(2,1)}), bf16[32,288,256]{2,1,0:T(8,128)(2,1)}) %all-gather.13.cloned.1.call-update) | async-done | bytes 4718608 | tf_op jit(solution)/shard_map/exit/all_gather | solution.py:201
  465.0 4.8 %copy.56 = bf16[32,256,288]{1,2,0:T(8,128)(2,1)} copy(bf16[32,256,288]{1,2,0:T(8,128)(2,1)} %bitcast.122) | data formatting | bytes 9437184
  (74 shorter events, 6.9 us)
Async XLA Ops:
  6.5 139.3 %all-gather.7.cloned.1.call-start = ((), (), s32[]{:S(2)}) async-start(), calls=%async_computation.2 | async-start | bytes 22560768 | tf_op jit(solution)/shard_map/gather0/all_gather | solution.py:137
  7.9 1.0 copy-start.1
  8.3 1.0 copy-start.2
  8.4 1.2 copy-start.3
  8.4 1.3 copy-start.4
  12.5 251.0 %all-gather.9.cloned.1.call-start = ((), (), s32[]{:S(2)}) async-start(), calls=%async_computation.3 | async-start | bytes 22560768 | tf_op jit(solution)/shard_map/gather1/all_gather | solution.py:137
  14.3 0.9 copy-start
  17.4 357.6 %all-gather.11.cloned.1.call-start = ((), (), s32[]{:S(2)}) async-start(), calls=%async_computation.4 | async-start | bytes 22560768 | tf_op jit(solution)/shard_map/gather2/all_gather | solution.py:137
  21.2 6.6 %copy-start.8 = (f32[2,288]{1,0:T(2,128)S(1)}, f32[2,288]{1,0:T(2,128)}, u32[]{:S(2)}) copy-start(f32[2,288]{1,0:T(2,128)} %param.17) | copy-start | bytes 6916
  21.2 6.7 %copy-start.9 = (f32[2,288]{1,0:T(2,128)S(1)}, f32[2,288]{1,0:T(2,128)}, u32[]{:S(2)}) copy-start(f32[2,288]{1,0:T(2,128)} %param.18) | copy-start | bytes 6916
  21.2 6.8 %copy-start.10 = (f32[2,288]{1,0:T(2,128)S(1)}, f32[2,288]{1,0:T(2,128)}, u32[]{:S(2)}) copy-start(f32[2,288]{1,0:T(2,128)} %param.26) | copy-start | bytes 6916
  21.2 6.9 %copy-start.11 = (f32[2,288]{1,0:T(2,128)S(1)}, f32[2,288]{1,0:T(2,128)}, u32[]{:S(2)}) copy-start(f32[2,288]{1,0:T(2,128)} %param.27) | copy-start | bytes 6916
  21.2 6.9 %copy-start.12 = (f32[2,288]{1,0:T(2,128)S(1)}, f32[2,288]{1,0:T(2,128)}, u32[]{:S(2)}) copy-start(f32[2,288]{1,0:T(2,128)} %param.25) | copy-start | bytes 6916
  21.2 7.0 %copy-start.13 = (f32[2,288]{1,0:T(2,128)S(1)}, f32[2,288]{1,0:T(2,128)}, u32[]{:S(2)}) copy-start(f32[2,288]{1,0:T(2,128)} %param.31) | copy-start | bytes 6916
  21.2 7.1 %copy-start.6 = (f32[2,4,72]{2,1,0:T(4,128)S(1)}, f32[2,4,72]{2,1,0:T(4,128)}, u32[]{:S(2)}) copy-start(f32[2,4,72]{2,1,0:T(4,128)} %param.20) | copy-start | bytes 6916
  21.2 7.2 %copy-start.7 = (f32[2,4,72]{2,1,0:T(4,128)S(1)}, f32[2,4,72]{2,1,0:T(4,128)}, u32[]{:S(2)}) copy-start(f32[2,4,72]{2,1,0:T(4,128)} %param.23) | copy-start | bytes 6916
  21.2 7.3 %copy-start.5 = (f32[2,1076]{1,0:T(2,128)S(1)}, f32[2,1076]{1,0:T(2,128)}, u32[]{:S(2)}) copy-start(f32[2,1076]{1,0:T(2,128)} %param.29) | copy-start | bytes 25828
  21.2 68.4 %all-to-all-start = ((bf16[8,288,256]{2,1,0:T(8,128)(2,1)}), bf16[8,288,256]{2,1,0:T(8,128)(2,1)S(1)}, u32[]{:S(2)}, u32[]{:S(2)}) async-start(bf16[8,288,256]{2,1,0:T(8,128)(2,1)} %dynamic-slice_bitcast_fusion), calls=%async_computation | async-start | bytes 2359296 | tf_op jit(solution)/shard_map/entry/all_to_all | solution.py:142
  27.8 437.2 %all-gather.13.cloned.1.call-start = ((), (), s32[]{:S(2)}) async-start(), calls=%async_computation.5 | async-start | bytes 5898240 | tf_op jit(solution)/shard_map/exit/all_gather | solution.py:201
Sparse Core Ops, SparseCore 0:
  12.6 133.2 all-gather.6
  147.4 115.9 all-gather.8
  265.1 109.8 all-gather.10
  430.4 34.5 all-gather.12

commit v2 on v1

v2 whole, which is shorter than its diff:
```python
import jax
import jax.numpy as jnp
from jax import lax
from jax.experimental import pallas as pl
from jax.experimental.pallas import tpu as pltpu
from jax.sharding import PartitionSpec as P


EPS = 1e-6
BF = jnp.bfloat16
F32 = jnp.float32
LANES = 128
VMEM_BYTES = 60 * 1024 * 1024
RING_ROWS = 456


def norm_rows(x_f, gain, shift):
    mean = jnp.mean(x_f, axis=-1, keepdims=True)
    centred = x_f - mean
    variance = jnp.mean(centred * centred, axis=-1, keepdims=True)
    return (centred * lax.rsqrt(variance + EPS) * gain + shift).astype(BF)


def dot_nn(a, b):
    return lax.dot_general(a, b, (((1,), (0,)), ((), ())), preferred_element_type=F32)


def dot_nt(a, b):
    return lax.dot_general(a, b, (((1,), (1,)), ((), ())), preferred_element_type=F32)


def attention_kernel(heads, dim, toks, x_ref, gain_ref, shift_ref, bias_ref, bo_ref, w_ref, out_ref, h_ref, acc_ref):
    step = pl.program_id(0)
    width = x_ref.shape[-1]
    hd = heads * dim
    span = -(-hd // LANES) * LANES

    @pl.when(step == 0)
    def _():
        h_ref[...] = norm_rows(x_ref[...].astype(F32), gain_ref[...], shift_ref[...])
        acc_ref[...] = jnp.zeros_like(acc_ref)

    w = w_ref[...].reshape(width, w_ref.shape[-1])
    cols = w.shape[-1]
    qkv = dot_nn(h_ref[...], w) + bias_ref[0]
    q_f = qkv[:, :span]
    k = pltpu.roll(qkv, cols - hd, 1)[:, :span].astype(BF)
    v = pltpu.roll(qkv, hd, 1)[:, cols - span:].astype(BF)
    lane = lax.broadcasted_iota(jnp.int32, (toks, span), 1)
    outs = []
    for img in range(x_ref.shape[0] // toks):
        rows = slice(img * toks, (img + 1) * toks)
        q_i, k_i, v_i = q_f[rows], k[rows], v[rows]
        o_i = jnp.zeros((toks, span), F32)
        for head in range(heads):
            q_h = jnp.where((lane >= head * dim) & (lane < (head + 1) * dim), q_i, 0.0).astype(BF)
            s = dot_nt(q_h, k_i) * (dim ** -0.5)
            e = jnp.exp(s - jnp.max(s, axis=-1, keepdims=True))
            p = (e / jnp.sum(e, axis=-1, keepdims=True)).astype(BF)
            lo = span - hd + head * dim
            o_i = jnp.where((lane >= lo) & (lane < lo + dim), dot_nn(p, v_i), o_i)
        outs.append(o_i)
    acc_ref[...] += dot_nt(jnp.concatenate(outs, axis=0).astype(BF), w[:, cols - span:])

    @pl.when(step == pl.num_programs(0) - 1)
    def _():
        out_ref[...] = (x_ref[...].astype(F32) + acc_ref[...] + bo_ref[...]).astype(BF)


def mlp_kernel(toks, up_kind, down_kind, x_ref, gain_ref, shift_ref, bias_ref, bd_ref, *rest):
    counts = [1 if kind is None else 3 for kind in (up_kind, down_kind)]
    srcs = (rest[:counts[0]], rest[counts[0]:sum(counts)])
    out_ref, h_ref, acc_ref, up_buf, down_buf, sems = rest[sum(counts):]
    step = pl.program_id(0)
    steps = pl.num_programs(0)
    width = x_ref.shape[-1]
    plane = lax.axis_index("dp")
    core = lax.rem(lax.axis_index("ty"), 2)

    def loads(i, slot):
        copies = []
        for w, (kind, refs, buf) in enumerate(zip((up_kind, down_kind), srcs, (up_buf, down_buf))):
            if kind is None:
                parts = [(refs[0].at[:, i], buf.at[slot])]
            else:
                half, pair = buf.shape[3], refs[1].shape[0]
                parts = [(refs[0].at[:, i, pl.ds(kind * half, half)], buf.at[slot, :, plane]),
                         (refs[1].at[:, i], buf.at[slot, pl.ds(core * pair, pair), 1 - plane]),
                         (refs[2].at[:, i], buf.at[slot, pl.ds((1 - core) * pair, pair), 1 - plane])]
            copies += [pltpu.make_async_copy(src, dst, sems.at[slot, w, j]) for j, (src, dst) in enumerate(parts)]
        return copies

    slot = lax.rem(step, 2)

    @pl.when(step == 0)
    def _():
        for copy in loads(step, slot):
            copy.start()
        h_ref[...] = norm_rows(x_ref[...].astype(F32), gain_ref[...], shift_ref[...])
        acc_ref[...] = jnp.zeros_like(acc_ref)

    @pl.when(step + 1 < steps)
    def _():
        for copy in loads(step + 1, 1 - slot):
            copy.start()

    for copy in loads(step, slot):
        copy.wait()
    up = up_buf[slot].reshape(width, up_buf.shape[-1])
    down = down_buf[slot].reshape(width, down_buf.shape[-1])
    u = jax.nn.gelu(dot_nn(h_ref[...], up) + bias_ref[0], approximate=True).astype(BF)
    acc_ref[...] += dot_nt(u, down)

    @pl.when(step == steps - 1)
    def _():
        y = x_ref[...].astype(F32) + acc_ref[...] + bd_ref[...]
        if out_ref.shape == x_ref.shape:
            out_ref[...] = y.astype(BF)
        else:
            wl = out_ref.shape[2]
            y_t = y.T.astype(BF)
            for c in range(out_ref.shape[0]):
                for img in range(out_ref.shape[1]):
                    out_ref[c, img] = y_t[c * wl:(c + 1) * wl, img * toks:(img + 1) * toks]


def solution(mesh):
    tx, ty = mesh.shape["tx"], mesh.shape["ty"]
    act_spec = P("dp", None, "tx")
    vec_tx = P(None, "tx")
    proj_spec = P(None, "tx", "ty", None)
    head_vec = P(None, "ty", None)
    in_specs = (act_spec, vec_tx, vec_tx, proj_spec, head_vec, proj_spec, proj_spec, head_vec,
                P(None, "ty", None, "tx"), vec_tx, vec_tx, vec_tx,
                P(None, "tx", "ty"), P(None, "ty"), P(None, "ty", "tx"), vec_tx)

    def local_fn(x_in, ln1_gain, ln1_bias, w_q, b_q, w_k, w_v, b_v, w_o, b_o, ln2_gain, ln2_bias, w_up, b_up, w_down, b_down):
        layers, wl, hl, dim = w_q.shape
        fl = w_up.shape[-1]
        imgs, toks, _ = x_in.shape
        hd = hl * dim
        width = wl * tx
        cols = max(4 * hd, -(-fl // LANES) * LANES)
        per = imgs // ty
        nb = per // tx
        n = nb * toks

        def proj_block(l):
            rows = [w[l].transpose(1, 2, 0).reshape(hd, wl) for w in (w_q, w_k, w_v)] + [w_o[l].reshape(hd, wl)]
            return jnp.pad(jnp.concatenate(rows, axis=0).T, ((0, 0), (0, cols - 4 * hd)))

        def up_block(l):
            return jnp.pad(w_up[l], ((0, 0), (0, cols - fl)))

        def down_block(l):
            return jnp.pad(w_down[l].T, ((0, 0), (0, cols - fl)))

        plane = lax.axis_index("dp")
        core = lax.axis_index("ty") % 2
        half = wl // 2

        def gather(parts):
            rows = sum(p.shape[0] for p in parts)
            full = lax.all_gather(jnp.concatenate(parts, axis=0), ("tx", "ty"), axis=0)
            return full.reshape(tx, ty, rows, cols)

        halves = [("u", 0), ("d", 0), ("u", 1)]
        makers = {"u": up_block, "d": down_block}
        fill = max(0, RING_ROWS - half * len(halves))
        mine = [lax.dynamic_slice_in_dim(makers[kind](l), plane * half, half, axis=0) for kind, l in halves]
        split = gather(mine + [jnp.zeros((fill, cols), BF)])
        both = gather([proj_block(0), proj_block(1)]).reshape(tx, ty, 2, wl, cols)
        last_down = gather([down_block(1)])
        images = lax.dynamic_slice_in_dim(x_in.transpose(0, 2, 1), lax.axis_index("ty") * per, per, axis=0)
        x_t = lax.all_to_all(images, "tx", split_axis=0, concat_axis=0, tiled=True)
        x = x_t.reshape(tx, nb, wl, toks).transpose(1, 3, 0, 2).reshape(n, width)
        on_tx = [ln1_gain, ln1_bias, ln2_gain, ln2_bias, b_o, b_down]
        on_ty = [b_q.reshape(layers, hd), b_v.reshape(layers, hd), b_up]
        vec = lax.all_gather(jnp.concatenate([a.reshape(1, -1) for a in on_tx + on_ty], axis=1), ("tx", "ty"), axis=0)
        vec = vec.reshape(tx, ty, -1)
        at = len(on_tx) * layers * wl
        vt = vec[:, 0, :at].reshape(tx, len(on_tx), layers, wl).transpose(1, 2, 0, 3).reshape(len(on_tx), layers, 1, width)
        vq = vec[0, :, at:at + layers * hd].reshape(ty, layers, hd)
        vv = vec[0, :, at + layers * hd:at + 2 * layers * hd].reshape(ty, layers, hd)
        vu = vec[0, :, at + 2 * layers * hd:].reshape(ty, layers, fl)
        gap = jnp.zeros_like(vq)
        tail = jnp.zeros((ty, layers, cols - 4 * hd), F32)
        bias_a = jnp.concatenate([vq, gap, vv, gap, tail], axis=2).transpose(1, 0, 2).reshape(layers, ty, 1, cols)
        bias_u = jnp.pad(vu, ((0, 0), (0, 0), (0, cols - fl))).transpose(1, 0, 2).reshape(layers, ty, 1, cols)

        swap = [(i, i ^ 1) for i in range(ty)]
        split, x, vt, bias_a, bias_u = lax.optimization_barrier((split, x, vt, bias_a, bias_u))
        got = {}
        for j, key in enumerate(halves):
            sent = lax.dynamic_slice(split, (core * (tx // 2), 0, j * half, 0), (tx // 2, ty, half, cols))
            if j:
                sent, got[halves[0]] = lax.optimization_barrier((sent, got[halves[0]]))
            got[key] = lax.ppermute(sent, "dp", [(0, 1), (1, 0)])
        crossed = {}

        def cross_core(key):
            crossed[key] = (got[key], lax.ppermute(got[key], "ty", swap))

        cross_core(halves[0])

        whole = pl.BlockSpec((n, width), lambda i: (0, 0))
        row = pl.BlockSpec((1, width), lambda i: (0, 0))
        bias = pl.BlockSpec((1, 1, cols), lambda i: (i, 0, 0))
        scratch = [pltpu.VMEM((n, width), BF), pltpu.VMEM((n, width), F32)]
        params = pltpu.CompilerParams(vmem_limit_bytes=VMEM_BYTES, dimension_semantics=("arbitrary",))

        anywhere = pl.BlockSpec(memory_space=pl.ANY)

        for l in range(layers):
            x = pl.pallas_call(
                lambda *refs: attention_kernel(hl, dim, toks, *refs),
                grid=(ty,),
                in_specs=[whole, row, row, bias, row, pl.BlockSpec((tx, 1, 1, wl, cols), lambda i, l=l: (0, i, l, 0, 0))],
                out_specs=whole,
                out_shape=jax.ShapeDtypeStruct((n, width), BF),
                scratch_shapes=scratch,
                compiler_params=params,
                name="attention",
                cost_estimate=pl.CostEstimate(flops=2 * n * width * width * 12, bytes_accessed=2 * width * width * 4, transcendentals=n * toks * 16),
            )(x, vt[0, l], vt[1, l], bias_a[l], vt[4, l], both)
            late = halves[l + 1]
            got[late], x = lax.optimization_barrier((got[late], x))
            cross_core(late)
            last = l == layers - 1
            out = (tx, nb, wl, toks) if last else (n, width)
            kinds, operands, bufs = [], [], []
            for key in (("u", l), ("d", l)):
                if key in crossed:
                    kinds.append(halves.index(key))
                    operands += [split, *crossed[key]]
                    bufs.append(pltpu.VMEM((2, tx, 2, half, cols), BF))
                else:
                    kinds.append(None)
                    operands.append(last_down)
                    bufs.append(pltpu.VMEM((2, tx, wl, cols), BF))
            x = pl.pallas_call(
                lambda *refs, k=tuple(kinds): mlp_kernel(toks, *k, *refs),
                grid=(ty,),
                in_specs=[whole, row, row, bias, row] + [anywhere] * len(operands),
                out_specs=pl.BlockSpec(out, lambda i, r=len(out): (0,) * r),
                out_shape=jax.ShapeDtypeStruct(out, BF),
                scratch_shapes=scratch + bufs + [pltpu.SemaphoreType.DMA((2, 2, 3))],
                compiler_params=params,
                name="mlp",
                cost_estimate=pl.CostEstimate(flops=2 * n * width * cols * ty * 4, bytes_accessed=4 * width * cols * ty, transcendentals=n * cols * ty),
            )(x, vt[2, l], vt[3, l], bias_u[l], vt[5, l], *operands)
        y = lax.all_to_all(x.reshape(tx * nb, wl, toks), "tx", split_axis=0, concat_axis=0, tiled=True)
        y = lax.all_gather(y, "ty", axis=0, tiled=True)
        return y.transpose(0, 2, 1)

    return jax.shard_map(local_fn, mesh=mesh, in_specs=in_specs, out_specs=act_spec, check_vma=False)
```

time: 477 us -> 434 us (0.910)
  waiting for transfers between devices: 255 us -> 203 us
    all_gather x3, waiting for transfers between devices: 220 us -> 91.9 us  [gather(): full = lax.all_gather(jnp.concatenate(parts, axis=0), ('tx', 'ty'), axis=0)]
    ppermute x0 -> x6, waiting for transfers between devices: none -> 75.5 us  [the longest x3 72.5 us: local_fn(): got[key] = lax.ppermute(sent, 'dp', [(0, 1), (1, 0)])]
    dynamic_slice x0 -> x3, local copies, waits for them, and re-layouts: none -> 6.41 us  [the longest x1 6.3 us: local_fn(): lax.dynamic_slice(split, (core * (tx // 2), 0, j * half, 0), (tx // 2, ty...]
  transfers between devices with their start and end apart: 5 -> 11, of which waited for: 4 -> 7; matrix products, arithmetic and copies ran while one was open for 3% -> 5% of each run, Pallas kernels for 13% -> 14%
where the time goes in v2:
time: 434 us; the launch traced here: 433 us
  waiting for transfers between devices  203 us (47%)
  blocking collectives  91.1 us (21%)
  Pallas kernels  82.6 us (19%)
  local copies, waits for them, and re-layouts  28.1 us (6%)
  between operations  13.5 us (3%)
  starting transfers between devices  11.2 us (3%)
    all_gather x3, waiting for transfers between devices, gather(): full = lax.all_gather(jnp.concatenate(parts, axis=0), ('tx', 'ty'), axis=0)  91.9 us
    ppermute x3, waiting for transfers between devices, local_fn(): got[key] = lax.ppermute(sent, 'dp', [(0, 1), (1, 0)])  72.5 us
    all_gather x1, blocking collectives, local_fn(): lax.all_gather(jnp.concatenate([a.reshape(1, -1) for a in on_tx + on_ty],...  57.5 us
    pallas_call x2, Pallas kernels, local_fn(): pl.pallas_call(lambda *refs: attention_kernel(hl, dim, toks, *refs), grid...  42.6 us
    pallas_call x2, Pallas kernels, local_fn(): pl.pallas_call(lambda *refs, k=tuple(kinds): mlp_kernel(toks, *k, *refs),...  39.9 us
    all_gather x1, waiting for transfers between devices, local_fn(): y = lax.all_gather(y, 'ty', axis=0, tiled=True)  35.7 us
    all_to_all x1, blocking collectives, local_fn(): lax.all_to_all(x.reshape(tx * nb, wl, toks), 'tx', split_axis=0, concat_a...  33.6 us
  transfers between devices with their start and end apart: 11, of which 7 were waited for; matrix products, arithmetic and copies ran while one was open for 5% of the time, Pallas kernels for 14%

profile of v2, /device:TPU:0, one launch (start us, length us, event | category | flops | bytes accessed | tf_op | source)
XLA Modules:
  0.0 433.1 jit_solution(1910674814322661870)
XLA Ops:
  6.5 1.5 slice_bitcast_fusion.3
  13.3 1.2 pad_maximum_fusion
  15.6 2.4 dynamic-slice_bitcast_fusion
  18.0 6.3 %all-to-all-start = ((bf16[8,288,256]{2,1,0:T(8,128)(2,1)}), bf16[8,288,256]{2,1,0:T(8,128)(2,1)S(1)}, u32[]{:S(2)}, u32[]{:S(2)}) async-start(bf16[8,288,256]{2,1,0:T(8,128)(2,1)} %dynamic-slice_bitcast_fusion), calls=%async_computation | async-start | bytes 2359296 | tf_op jit(solution)/shard_map/all_to_all | solution.py:175
  25.3 57.5 %all-gather.4 = f32[16,1,6760]{2,1,0:T(1,128)S(1)} all-gather(f32[1,1,6760]{2,1,0:T(1,128)S(1)} %bitcast.120), channel_id=3, replica_groups=mesh['dp'=2,'tx'=4,'ty'=4] {'tx','ty'}, dimensions={0}, use_global_device_ids=true | all-gather | bytes 459680 | tf_op jit(solution)/shard_map/all_gather | solution.py:179
  86.6 36.3 %all-gather.12.cloned.1.call-done = bf16[7296,1152]{1,0:T(8,128)(2,1)} async-done(((bf16[456,1152]{1,0:T(8,128)(2,1)}), bf16[7296,1152]{1,0:T(8,128)(2,1)}) %all-gather.12.cloned.1.call-update) | async-done | bytes 16810000 | tf_op jit(solution)/shard_map/all_gather | solution.py:164
  122.9 6.3 %constant_dynamic-slice_fusion = (bf16[2,4,144,1152]{3,2,1,0:T(8,128)(2,1)S(1)}, bf16[2,4,144,1152]{3,2,1,0:T(8,128)(2,1)}, bf16[2,4,144,1152]{3,2,1,0:T(8,128)(2,1)}) fusion(bf16[4,4,456,1152]{3,2,1,0:T(8,128)(2,1)} %bitcast.103, s32[]{:T(128)S(6)} %select_n.23), kind=kLoop, calls=%fused_computation.29 | loop fusion | bytes 15925252 | tf_op jit(solution)/shard_map/dynamic_slice | solution.py:195
  129.2 1.5 collective-permute-start
  130.7 58.4 %collective-permute-done.refs_6_ = bf16[2,4,144,1152]{3,2,1,0:T(8,128)(2,1)} collective-permute-done((bf16[2,4,144,1152]{3,2,1,0:T(8,128)(2,1)S(1)}, bf16[2,4,144,1152]{3,2,1,0:T(8,128)(2,1)}, u32[]{:S(2)}, u32[]{:S(2)}) %collective-permute-start) | collective-permute-done | bytes 2654240 | tf_op jit(solution)/shard_map/ppermute | solution.py:198
  189.0 1.5 collective-permute-start.2
  190.5 1.4 copy.53.refs_0_
  193.2 46.9 %all-gather.14.cloned.1.call-done = bf16[9216,1152]{1,0:T(8,128)(2,1)} async-done(((bf16[576,1152]{1,0:T(8,128)(2,1)}), bf16[9216,1152]{1,0:T(8,128)(2,1)}) %all-gather.14.cloned.1.call-update) | async-done | bytes 21233680 | tf_op jit(solution)/shard_map/all_gather | solution.py:164
  240.2 21.3 %attention.2.refs_0_ = bf16[512,1152]{1,0:T(8,128)(2,1)} custom-call(bf16[512,1152]{1,0:T(8,128)(2,1)} %copy.53.refs_0_, f32[1,1152]{1,0:T(1,128)} %get-tuple-element.59.refs_1_, f32[1,1152]{1,0:T(1,128)} %get-tuple-element.58.refs_2_, f32[4,1,1152]{2,1,0:T(1,128)} %get-tuple-element.63.refs_3_, f32[1,1152]{1,0:T(1,128)} %get-tuple-element.57.refs_4_, ...), custom_call_target="tpu_custom_call" | custom-call | flops 16307453952 | bytes 10616832 | tf_op jit(solution)/shard_map/attention/pallas_call | solution.py:215
  262.3 1.5 collective-permute-start.1
  263.8 3.0 collective-permute-done.4.refs_10_
  266.7 19.9 %mlp.2.refs_0_ = bf16[512,1152]{1,0:T(8,128)(2,1)} custom-call(bf16[512,1152]{1,0:T(8,128)(2,1)} %attention.2.refs_0_, f32[1,1152]{1,0:T(1,128)} %get-tuple-element.56.refs_1_, f32[1,1152]{1,0:T(1,128)} %get-tuple-element.55.refs_2_, f32[4,1,1152]{2,1,0:T(1,128)} %get-tuple-element.61.refs_3_, f32[1,1152]{1,0:T(1,128)} %get-tuple-element.54.refs_4_, ...), custom_call_target="tpu_custom_call" | custom-call | flops 21743271936 | bytes 21233664 | tf_op jit(solution)/shard_map/mlp/pallas_call | solution.py:241
  286.6 21.4 %attention.3.refs_0_ = bf16[512,1152]{1,0:T(8,128)(2,1)} custom-call(bf16[512,1152]{1,0:T(8,128)(2,1)} %mlp.2.refs_0_, f32[1,1152]{1,0:T(1,128)} %get-tuple-element.53.refs_1_, f32[1,1152]{1,0:T(1,128)} %get-tuple-element.52.refs_2_, f32[4,1,1152]{2,1,0:T(1,128)} %get-tuple-element.62.refs_3_, f32[1,1152]{1,0:T(1,128)} %get-tuple-element.51.refs_4_, ...), custom_call_target="tpu_custom_call" | custom-call | flops 16307453952 | bytes 10616832 | tf_op jit(solution)/shard_map/attention/pallas_call | solution.py:215
  308.0 14.2 %collective-permute-done.1.refs_6_ = bf16[2,4,144,1152]{3,2,1,0:T(8,128)(2,1)} collective-permute-done((bf16[2,4,144,1152]{3,2,1,0:T(8,128)(2,1)S(1)}, bf16[2,4,144,1152]{3,2,1,0:T(8,128)(2,1)}, u32[]{:S(2)}, u32[]{:S(2)}) %collective-permute-start.1) | collective-permute-done | bytes 2654240 | tf_op jit(solution)/shard_map/ppermute | solution.py:198
  322.1 8.7 %all-gather.16.cloned.1.call-done = bf16[4608,1152]{1,0:T(8,128)(2,1)} async-done(((bf16[288,1152]{1,0:T(8,128)(2,1)}), bf16[4608,1152]{1,0:T(8,128)(2,1)}) %all-gather.16.cloned.1.call-update) | async-done | bytes 10616848 | tf_op jit(solution)/shard_map/all_gather | solution.py:164
  330.8 1.5 copy-done.15
  332.3 20.1 %mlp.3 = bf16[4,2,288,256]{3,2,1,0:T(8,128)(2,1)} custom-call(bf16[512,1152]{1,0:T(8,128)(2,1)} %attention.3.refs_0_, f32[1,1152]{1,0:T(1,128)} %get-tuple-element.50.refs_1_, f32[1,1152]{1,0:T(1,128)} %get-tuple-element.49.refs_2_, f32[4,1,1152]{2,1,0:T(1,128)} %get-tuple-element.60.refs_3_, f32[1,1152]{1,0:T(1,128)} %get-tuple-element.48.refs_4_, ...), custom_call_target="tpu_custom_call" | custom-call | flops 21743271936 | bytes 21233664 | tf_op jit(solution)/shard_map/mlp/pallas_call | solution.py:241
  352.4 33.6 %all_to_all.10 = bf16[8,288,256]{2,1,0:T(8,128)(2,1)} all-to-all(bf16[8,288,256]{2,1,0:T(8,128)(2,1)} %bitcast.109), channel_id=1, replica_groups=mesh['dp'=2,'tx'=4,'ty'=4] {'tx'}, dimensions={0} | all-to-all | bytes 2359296 | tf_op jit(solution)/shard_map/all_to_all | solution.py:252
  386.0 35.7 %all-gather.10.cloned.1.call-done = bf16[32,288,256]{2,1,0:T(8,128)(2,1)} async-done(((bf16[8,288,256]{2,1,0:T(8,128)(2,1)}), bf16[32,288,256]{2,1,0:T(8,128)(2,1)}) %all-gather.10.cloned.1.call-update) | async-done | bytes 4718608 | tf_op jit(solution)/shard_map/all_gather | solution.py:253
  421.7 4.8 %copy.59 = bf16[32,256,288]{1,2,0:T(8,128)(2,1)} copy(bf16[32,256,288]{1,2,0:T(8,128)(2,1)} %bitcast.99) | data formatting | bytes 9437184
  (101 shorter events, 12.9 us)
Async XLA Ops:
  6.5 116.4 %all-gather.12.cloned.1.call-start = ((), (), s32[]{:S(2)}) async-start(), calls=%async_computation.3 | async-start | bytes 17860608 | tf_op jit(solution)/shard_map/all_gather | solution.py:164
  6.5 1.7 copy-start.1
  8.6 1.6 copy-start.3
  9.8 230.3 %all-gather.14.cloned.1.call-start = ((), (), s32[]{:S(2)}) async-start(), calls=%async_computation.4 | async-start | bytes 22560768 | tf_op jit(solution)/shard_map/all_gather | solution.py:164
  14.5 316.3 %all-gather.16.cloned.1.call-start = ((), (), s32[]{:S(2)}) async-start(), calls=%async_computation.5 | async-start | bytes 11280384 | tf_op jit(solution)/shard_map/all_gather | solution.py:164
  15.5 8.9 %copy-start.9 = (f32[2,288]{1,0:T(2,128)S(1)}, f32[2,288]{1,0:T(2,128)}, u32[]{:S(2)}) copy-start(f32[2,288]{1,0:T(2,128)} %param.17) | copy-start | bytes 6916
  15.5 8.9 %copy-start.10 = (f32[2,288]{1,0:T(2,128)S(1)}, f32[2,288]{1,0:T(2,128)}, u32[]{:S(2)}) copy-start(f32[2,288]{1,0:T(2,128)} %param.18) | copy-start | bytes 6916
  15.6 9.0 %copy-start.11 = (f32[2,288]{1,0:T(2,128)S(1)}, f32[2,288]{1,0:T(2,128)}, u32[]{:S(2)}) copy-start(f32[2,288]{1,0:T(2,128)} %param.26) | copy-start | bytes 6916
  15.6 9.1 %copy-start.12 = (f32[2,288]{1,0:T(2,128)S(1)}, f32[2,288]{1,0:T(2,128)}, u32[]{:S(2)}) copy-start(f32[2,288]{1,0:T(2,128)} %param.27) | copy-start | bytes 6916
  15.6 9.2 %copy-start.13 = (f32[2,288]{1,0:T(2,128)S(1)}, f32[2,288]{1,0:T(2,128)}, u32[]{:S(2)}) copy-start(f32[2,288]{1,0:T(2,128)} %param.25) | copy-start | bytes 6916
  15.6 9.2 %copy-start.14 = (f32[2,288]{1,0:T(2,128)S(1)}, f32[2,288]{1,0:T(2,128)}, u32[]{:S(2)}) copy-start(f32[2,288]{1,0:T(2,128)} %param.31) | copy-start | bytes 6916
  15.6 9.3 %copy-start.7 = (f32[2,4,72]{2,1,0:T(4,128)S(1)}, f32[2,4,72]{2,1,0:T(4,128)}, u32[]{:S(2)}) copy-start(f32[2,4,72]{2,1,0:T(4,128)} %param.20) | copy-start | bytes 6916
  15.6 9.4 %copy-start.8 = (f32[2,4,72]{2,1,0:T(4,128)S(1)}, f32[2,4,72]{2,1,0:T(4,128)}, u32[]{:S(2)}) copy-start(f32[2,4,72]{2,1,0:T(4,128)} %param.23) | copy-start | bytes 6916
  15.6 9.5 %copy-start.6 = (f32[2,1076]{1,0:T(2,128)S(1)}, f32[2,1076]{1,0:T(2,128)}, u32[]{:S(2)}) copy-start(f32[2,1076]{1,0:T(2,128)} %param.29) | copy-start | bytes 25828
  18.0 67.0 %all-to-all-start = ((bf16[8,288,256]{2,1,0:T(8,128)(2,1)}), bf16[8,288,256]{2,1,0:T(8,128)(2,1)S(1)}, u32[]{:S(2)}, u32[]{:S(2)}) async-start(bf16[8,288,256]{2,1,0:T(8,128)(2,1)} %dynamic-slice_bitcast_fusion), calls=%async_computation | async-start | bytes 2359296 | tf_op jit(solution)/shard_map/all_to_all | solution.py:175
  24.4 397.3 %all-gather.10.cloned.1.call-start = ((), (), s32[]{:S(2)}) async-start(), calls=%async_computation.2 | async-start | bytes 5898240 | tf_op jit(solution)/shard_map/all_gather | solution.py:253
  129.2 59.8 %collective-permute-start = (bf16[2,4,144,1152]{3,2,1,0:T(8,128)(2,1)S(1)}, bf16[2,4,144,1152]{3,2,1,0:T(8,128)(2,1)}, u32[]{:S(2)}, u32[]{:S(2)}) collective-permute-start(bf16[2,4,144,1152]{3,2,1,0:T(8,128)(2,1)S(1)} %get-tuple-element.31), channel_id=1, source_target_pairs={{0,16},{16,0},{1,17},{17,1},{2,18},{18,2},{3,19},{19,3},{4,20},{20... | collective-permute-start | bytes 7962632 | tf_op jit(solution)/shard_map/ppermute | solution.py:198
  189.0 72.4 %collective-permute-start.2 = (bf16[2,4,144,1152]{3,2,1,0:T(8,128)(2,1)}, bf16[2,4,144,1152]{3,2,1,0:T(8,128)(2,1)}, u32[]{:S(2)}, u32[]{:S(2)}) collective-permute-start(bf16[2,4,144,1152]{3,2,1,0:T(8,128)(2,1)} %get-tuple-element.21), channel_id=1, source_target_pairs={{0,16},{16,0},{1,17},{17,1},{2,18},{18,2},{3,19},{19,3},{4,20},{20... | collective-permute-start | bytes 7962632 | tf_op jit(solution)/shard_map/ppermute | solution.py:198
  193.2 70.6 %collective-permute-start.3 = (bf16[2,4,144,1152]{3,2,1,0:T(8,128)(2,1)}, bf16[2,4,144,1152]{3,2,1,0:T(8,128)(2,1)}, u32[]{:S(2)}, u32[]{:S(2)}) collective-permute-start(bf16[2,4,144,1152]{3,2,1,0:T(8,128)(2,1)} %collective-permute-done.refs_6_), channel_id=1, source_target_pairs={{0,1},{1,0},{2,3},{3,2},{4,5},{5,4},{6,7},{7,6},{8,9},{9,8},{10,11... | collective-permute-start | bytes 7962632 | tf_op jit(solution)/shard_map/ppermute | solution.py:202
  240.2 22.1 %copy-start = (bf16[2,4,144,1152]{3,2,1,0:T(8,128)(2,1)S(1)}, bf16[2,4,144,1152]{3,2,1,0:T(8,128)(2,1)}, u32[]{:S(2)}) copy-start(bf16[2,4,144,1152]{3,2,1,0:T(8,128)(2,1)} %get-tuple-element.20) | copy-start | bytes 7962628
  261.4 5.3 %collective-permute-start.4 = (bf16[2,4,144,1152]{3,2,1,0:T(8,128)(2,1)}, bf16[2,4,144,1152]{3,2,1,0:T(8,128)(2,1)}, u32[]{:S(2)}, u32[]{:S(2)}) collective-permute-start(bf16[2,4,144,1152]{3,2,1,0:T(8,128)(2,1)} %collective-permute-done.2.refs_9_), channel_id=1, source_target_pairs={{0,1},{1,0},{2,3},{3,2},{4,5},{5,4},{6,7},{7,6},{8,9},{9,8},{10,11... | collective-permute-start | bytes 7962632 | tf_op jit(solution)/shard_map/ppermute | solution.py:202
  262.3 59.8 %collective-permute-start.1 = (bf16[2,4,144,1152]{3,2,1,0:T(8,128)(2,1)S(1)}, bf16[2,4,144,1152]{3,2,1,0:T(8,128)(2,1)}, u32[]{:S(2)}, u32[]{:S(2)}) collective-permute-start(bf16[2,4,144,1152]{3,2,1,0:T(8,128)(2,1)S(1)} %copy-done), channel_id=1, source_target_pairs={{0,16},{16,0},{1,17},{17,1},{2,18},{18,2},{3,19},{19,3},{4,20},{20... | collective-permute-start | bytes 7962632 | tf_op jit(solution)/shard_map/ppermute | solution.py:198
  322.1 8.7 %collective-permute-start.5 = (bf16[2,4,144,1152]{3,2,1,0:T(8,128)(2,1)}, bf16[2,4,144,1152]{3,2,1,0:T(8,128)(2,1)S(1)}, u32[]{:S(2)}, u32[]{:S(2)}) collective-permute-start(bf16[2,4,144,1152]{3,2,1,0:T(8,128)(2,1)} %collective-permute-done.1.refs_6_), channel_id=1, source_target_pairs={{0,1},{1,0},{2,3},{3,2},{4,5},{5,4},{6,7},{7,6},{8,9},{9,8},{10,11... | collective-permute-start | bytes 7962632 | tf_op jit(solution)/shard_map/ppermute | solution.py:202
  330.8 1.5 copy-start.15
  (3 other events, 3.7 us)
Sparse Core Ops, SparseCore 0:
  9.9 112.9 all-gather.11
  124.5 115.6 all-gather.13
  242.4 88.3 all-gather.15
  386.1 35.5 all-gather.9

commit v3 on v2

v3 whole, which is shorter than its diff:
```python
import jax
import jax.numpy as jnp
from jax import lax
from jax.experimental import pallas as pl
from jax.experimental.pallas import tpu as pltpu
from jax.sharding import PartitionSpec as P


EPS = 1e-6
BF = jnp.bfloat16
F32 = jnp.float32
LANES = 128
VMEM_BYTES = 60 * 1024 * 1024


def norm_rows(x_f, gain, shift):
    mean = jnp.mean(x_f, axis=-1, keepdims=True)
    centred = x_f - mean
    variance = jnp.mean(centred * centred, axis=-1, keepdims=True)
    return (centred * lax.rsqrt(variance + EPS) * gain + shift).astype(BF)


def dot_nn(a, b):
    return lax.dot_general(a, b, (((1,), (0,)), ((), ())), preferred_element_type=F32)


def dot_nt(a, b):
    return lax.dot_general(a, b, (((1,), (1,)), ((), ())), preferred_element_type=F32)


def attention_kernel(heads, dim, toks, x_ref, gain_ref, shift_ref, bias_ref, bo_ref, w_ref, out_ref, h_ref, acc_ref):
    step = pl.program_id(0)
    width = x_ref.shape[-1]
    hd = heads * dim
    span = -(-hd // LANES) * LANES

    @pl.when(step == 0)
    def _():
        h_ref[...] = norm_rows(x_ref[...].astype(F32), gain_ref[...], shift_ref[...])
        acc_ref[...] = jnp.zeros_like(acc_ref)

    w = w_ref[...].reshape(width, w_ref.shape[-1])
    cols = w.shape[-1]
    qkv = dot_nn(h_ref[...], w) + bias_ref[0]
    q_f = qkv[:, :span]
    k = pltpu.roll(qkv, cols - hd, 1)[:, :span].astype(BF)
    v = pltpu.roll(qkv, hd, 1)[:, cols - span:].astype(BF)
    lane = lax.broadcasted_iota(jnp.int32, (toks, span), 1)
    outs = []
    for img in range(x_ref.shape[0] // toks):
        rows = slice(img * toks, (img + 1) * toks)
        q_i, k_i, v_i = q_f[rows], k[rows], v[rows]
        o_i = jnp.zeros((toks, span), F32)
        for head in range(heads):
            q_h = jnp.where((lane >= head * dim) & (lane < (head + 1) * dim), q_i, 0.0).astype(BF)
            s = dot_nt(q_h, k_i) * (dim ** -0.5)
            e = jnp.exp(s - jnp.max(s, axis=-1, keepdims=True))
            p = (e / jnp.sum(e, axis=-1, keepdims=True)).astype(BF)
            lo = span - hd + head * dim
            o_i = jnp.where((lane >= lo) & (lane < lo + dim), dot_nn(p, v_i), o_i)
        outs.append(o_i)
    acc_ref[...] += dot_nt(jnp.concatenate(outs, axis=0).astype(BF), w[:, cols - span:])

    @pl.when(step == pl.num_programs(0) - 1)
    def _():
        out_ref[...] = (x_ref[...].astype(F32) + acc_ref[...] + bo_ref[...]).astype(BF)


def load_ahead(loads, first=lambda: None):
    step = pl.program_id(0)
    slot = lax.rem(step, 2)

    @pl.when(step == 0)
    def _():
        for copy in loads(step, slot):
            copy.start()
        first()

    @pl.when(step + 1 < pl.num_programs(0))
    def _():
        for copy in loads(step + 1, 1 - slot):
            copy.start()

    for copy in loads(step, slot):
        copy.wait()
    return slot


def half_loads(srcs, bufs, sems):
    plane = lax.axis_index("dp")
    core = lax.rem(lax.axis_index("ty"), 2)

    def loads(i, slot):
        copies = []
        for w, buf in enumerate(bufs):
            own, same, other = srcs[3 * w:3 * w + 3]
            pair = same.shape[0]
            parts = [(own.at[:, i], buf.at[slot, :, plane]),
                     (same.at[:, i], buf.at[slot, pl.ds(core * pair, pair), 1 - plane]),
                     (other.at[:, i], buf.at[slot, pl.ds((1 - core) * pair, pair), 1 - plane])]
            copies += [pltpu.make_async_copy(src, dst, sems.at[slot, w, j]) for j, (src, dst) in enumerate(parts)]
        return copies

    return loads


def mlp_kernel(x_ref, gain_ref, shift_ref, bias_ref, bd_ref, u0, u1, u2, d0, d1, d2, out_ref, h_ref, acc_ref, up_buf, down_buf, sems):
    step = pl.program_id(0)
    width = x_ref.shape[-1]

    def first():
        h_ref[...] = norm_rows(x_ref[...].astype(F32), gain_ref[...], shift_ref[...])
        acc_ref[...] = jnp.zeros_like(acc_ref)

    slot = load_ahead(half_loads((u0, u1, u2, d0, d1, d2), (up_buf, down_buf), sems), first)
    up = up_buf[slot].reshape(width, up_buf.shape[-1])
    down = down_buf[slot].reshape(width, down_buf.shape[-1])
    u = jax.nn.gelu(dot_nn(h_ref[...], up) + bias_ref[0], approximate=True).astype(BF)
    acc_ref[...] += dot_nt(u, down)

    @pl.when(step == pl.num_programs(0) - 1)
    def _():
        out_ref[...] = (x_ref[...].astype(F32) + acc_ref[...] + bd_ref[...]).astype(BF)


def up_kernel(x_ref, gain_ref, shift_ref, bias_ref, u0, u1, u2, out_ref, h_ref, up_buf, sems):
    width = x_ref.shape[-1]

    def first():
        h_ref[...] = norm_rows(x_ref[...].astype(F32), gain_ref[...], shift_ref[...])

    slot = load_ahead(half_loads((u0, u1, u2), (up_buf,), sems), first)
    up = up_buf[slot].reshape(width, up_buf.shape[-1])
    out_ref[0] = jax.nn.gelu(dot_nn(h_ref[...], up) + bias_ref[0], approximate=True).astype(BF)


def down_kernel(order, toks, x_ref, bd_ref, u_ref, down_ref, out_ref, acc_ref):
    step = pl.program_id(0)
    width = x_ref.shape[-1]

    @pl.when(step == 0)
    def _():
        acc_ref[...] = x_ref[...].astype(F32) + bd_ref[...]

    acc_ref[...] += dot_nt(u_ref[0], down_ref[...].reshape(width, down_ref.shape[-1]))

    @pl.when(step == pl.num_programs(0) - 1)
    def _():
        wl = out_ref.shape[2]
        y_t = acc_ref[...].T.astype(BF)
        for i, block in enumerate(order):
            for img in range(out_ref.shape[1]):
                out_ref[block, img] = y_t[i * wl:(i + 1) * wl, img * toks:(img + 1) * toks]


def solution(mesh):
    tx, ty = mesh.shape["tx"], mesh.shape["ty"]
    act_spec = P("dp", None, "tx")
    vec_tx = P(None, "tx")
    proj_spec = P(None, "tx", "ty", None)
    head_vec = P(None, "ty", None)
    in_specs = (act_spec, vec_tx, vec_tx, proj_spec, head_vec, proj_spec, proj_spec, head_vec,
                P(None, "ty", None, "tx"), vec_tx, vec_tx, vec_tx,
                P(None, "tx", "ty"), P(None, "ty"), P(None, "ty", "tx"), vec_tx)

    def local_fn(x_in, ln1_gain, ln1_bias, w_q, b_q, w_k, w_v, b_v, w_o, b_o, ln2_gain, ln2_bias, w_up, b_up, w_down, b_down):
        layers, wl, hl, dim = w_q.shape
        fl = w_up.shape[-1]
        imgs, toks, _ = x_in.shape
        hd = hl * dim
        width = wl * tx
        cols = max(4 * hd, -(-fl // LANES) * LANES)
        per = imgs // ty
        nb = per // tx
        n = nb * toks

        def proj_block(l):
            rows = [w[l].transpose(1, 2, 0).reshape(hd, wl) for w in (w_q, w_k, w_v)] + [w_o[l].reshape(hd, wl)]
            return jnp.pad(jnp.concatenate(rows, axis=0).T, ((0, 0), (0, cols - 4 * hd)))

        def up_block(l):
            return jnp.pad(w_up[l], ((0, 0), (0, cols - fl)))

        def down_block(l):
            return jnp.pad(w_down[l].T, ((0, 0), (0, cols - fl)))

        plane = lax.axis_index("dp")
        core = lax.axis_index("ty") % 2
        half = wl // 2

        order = [1, 0] + list(range(2, tx))
        groups = [[t * ty + i for t in order for i in range(ty)]]

        def blocks(a):
            return jnp.concatenate([a[i:i + 1] for i in order], axis=0)

        def gather(block):
            full = lax.all_gather(block, ("tx", "ty"), axis=0, axis_index_groups=groups)
            return full.reshape(tx, ty, *block.shape)

        halves = [("u", 0), ("d", 0), ("u", 1)]
        makers = {"u": up_block, "d": down_block}
        split = {(kind, l): gather(lax.dynamic_slice_in_dim(makers[kind](l), plane * half, half, axis=0)) for kind, l in halves}
        proj = [gather(proj_block(0)), gather(proj_block(1))]
        last_down = gather(down_block(1))

        images = lax.dynamic_slice_in_dim(x_in.transpose(0, 2, 1), lax.axis_index("ty") * per, per, axis=0)
        x_t = lax.all_to_all(images, "tx", split_axis=0, concat_axis=0, tiled=True)
        x = blocks(x_t.reshape(tx, nb, wl, toks)).transpose(1, 3, 0, 2).reshape(n, width)
        swap = [(i, i ^ 1) for i in range(ty)]
        got, crossed = {}, {}

        def to_send(key):
            return lax.dynamic_slice_in_dim(split[key], core * (tx // 2), tx // 2, axis=0)

        def cross_plane(key, sent):
            got[key] = lax.ppermute(sent, "dp", [(0, 1), (1, 0)])

        def cross_core(key):
            crossed[key] = (got[key], lax.ppermute(got[key], "ty", swap))

        split[halves[0]], x = lax.optimization_barrier((split[halves[0]], x))
        on_tx = [ln1_gain, ln1_bias, ln2_gain, ln2_bias, b_o, b_down]
        on_ty = [b_q.reshape(layers, hd), b_v.reshape(layers, hd), b_up]
        own = jnp.concatenate([a.reshape(1, -1) for a in on_tx + on_ty], axis=1)
        own, sent = lax.optimization_barrier((own, to_send(halves[0])))
        vec = lax.all_gather(own, ("tx", "ty"), axis=0)
        vec = blocks(vec.reshape(tx, ty, -1))
        at = len(on_tx) * layers * wl
        vt = vec[:, 0, :at].reshape(tx, len(on_tx), layers, wl).transpose(1, 2, 0, 3).reshape(len(on_tx), layers, 1, width)
        vq = vec[0, :, at:at + layers * hd].reshape(ty, layers, hd)
        vv = vec[0, :, at + layers * hd:at + 2 * layers * hd].reshape(ty, layers, hd)
        vu = vec[0, :, at + 2 * layers * hd:].reshape(ty, layers, fl)
        gap = jnp.zeros_like(vq)
        tail = jnp.zeros((ty, layers, cols - 4 * hd), F32)
        bias_a = jnp.concatenate([vq, gap, vv, gap, tail], axis=2).transpose(1, 0, 2).reshape(layers, ty, 1, cols)
        bias_u = jnp.pad(vu, ((0, 0), (0, 0), (0, cols - fl))).transpose(1, 0, 2).reshape(layers, ty, 1, cols)

        cross_plane(halves[0], sent)
        for key in halves[1:]:
            split[key], vec = lax.optimization_barrier((split[key], vec))
            cross_plane(key, to_send(key))
        cross_core(halves[0])

        whole = pl.BlockSpec((n, width), lambda i: (0, 0))
        row = pl.BlockSpec((1, width), lambda i: (0, 0))
        bias = pl.BlockSpec((1, 1, cols), lambda i: (i, 0, 0))
        scratch = [pltpu.VMEM((n, width), BF), pltpu.VMEM((n, width), F32)]
        params = pltpu.CompilerParams(vmem_limit_bytes=VMEM_BYTES, dimension_semantics=("arbitrary",))

        anywhere = pl.BlockSpec(memory_space=pl.ANY)
        rows_bf, rows_f = scratch
        half_buf = pltpu.VMEM((2, tx, 2, half, cols), BF)
        act = jax.ShapeDtypeStruct((n, width), BF)
        dot_flops = 2 * n * width * cols * ty

        def kernel(fn, in_specs, out_spec, out_shape, scratch_shapes, flops):
            return pl.pallas_call(fn, grid=(ty,), in_specs=in_specs, out_specs=out_spec, out_shape=out_shape,
                                  scratch_shapes=scratch_shapes, compiler_params=params,
                                  cost_estimate=pl.CostEstimate(flops=flops, bytes_accessed=width * cols * ty * 4, transcendentals=n * cols * ty))

        for l in range(layers):
            x = kernel(lambda *refs: attention_kernel(hl, dim, toks, *refs),
                       [whole, row, row, bias, row, pl.BlockSpec((tx, 1, wl, cols), lambda i: (0, i, 0, 0))],
                       whole, act, scratch, 4 * dot_flops)(x, vt[0, l], vt[1, l], bias_a[l], vt[4, l], proj[l])
            late = halves[l + 1]
            got[late], x = lax.optimization_barrier((got[late], x))
            cross_core(late)
            up = (split["u", l], *crossed["u", l])
            if l < layers - 1:
                down = (split["d", l], *crossed["d", l])
                x = kernel(mlp_kernel, [whole, row, row, bias, row] + [anywhere] * 6, whole, act,
                           scratch + [half_buf, half_buf, pltpu.SemaphoreType.DMA((2, 2, 3))], 4 * dot_flops,
                           )(x, vt[2, l], vt[3, l], bias_u[l], vt[5, l], *up, *down)
            else:
                hidden = pl.BlockSpec((1, n, cols), lambda i: (i, 0, 0))
                u = kernel(up_kernel, [whole, row, row, bias] + [anywhere] * 3, hidden,
                           jax.ShapeDtypeStruct((ty, n, cols), BF), [rows_bf, half_buf, pltpu.SemaphoreType.DMA((2, 1, 3))],
                           2 * dot_flops)(x, vt[2, l], vt[3, l], bias_u[l], *up)
                out = (tx, nb, wl, toks)
                x = kernel(lambda *refs: down_kernel(order, toks, *refs),
                           [whole, row, hidden, pl.BlockSpec((tx, 1, wl, cols), lambda i: (0, i, 0, 0))],
                           pl.BlockSpec(out, lambda i: (0, 0, 0, 0)), jax.ShapeDtypeStruct(out, BF), [rows_f],
                           2 * dot_flops)(x, vt[5, l], u, last_down)
        y = lax.all_to_all(x.reshape(tx * nb, wl, toks), "tx", split_axis=0, concat_axis=0, tiled=True)
        y = lax.all_gather(y, "ty", axis=0, tiled=True)
        return y.transpose(0, 2, 1)

    return jax.shard_map(local_fn, mesh=mesh, in_specs=in_specs, out_specs=act_spec, check_vma=False)
```

time: 434 us -> 428 us (0.986)
  blocking collectives: 91.1 us -> 55.3 us
  waiting for transfers between devices: 203 us -> 224 us
  local copies, waits for them, and re-layouts: 28.1 us -> 35.6 us
    ppermute x3, waiting for transfers between devices: 72.5 us -> 16.6 us  [cross_plane(): got[key] = lax.ppermute(sent, 'dp', [(0, 1), (1, 0)])]
    all_to_all x1, waiting for transfers between devices: 0.01 us -> 41 us  [local_fn(): x_t = lax.all_to_all(images, 'tx', split_axis=0, concat_axis=0, tiled=True)]
    all_gather x1, blocking collectives: 57.5 us -> 21.7 us  [local_fn(): vec = lax.all_gather(own, ('tx', 'ty'), axis=0)]
    all_gather x3 -> x6, waiting for transfers between devices: 91.9 us -> 124 us  [gather(): full = lax.all_gather(block, ('tx', 'ty'), axis=0, axis_index_groups=groups)]
    pallas_call x4 -> x5, Pallas kernels: 82.6 us -> 86.7 us  [the longest x2 42.2 us: local_fn(): kernel(lambda *refs: attention_kernel(hl, dim, toks, *refs), [whole, row,...]
    dynamic_slice x1 -> x3, local copies, waits for them, and re-layouts: 6.3 us -> 8.87 us  [to_send(): lax.dynamic_slice_in_dim(split[key], core * (tx // 2), tx // 2, axis=0)]
  transfers between devices with their start and end apart: 11 -> 14, of which waited for: 7 -> 10; matrix products, arithmetic and copies ran while one was open for 5% -> 6% of each run, Pallas kernels for 14% -> 18%
where the time goes in v3:
time: 428 us; the launch traced here: 427 us
  waiting for transfers between devices  224 us (52%)
  Pallas kernels  86.7 us (20%)
  blocking collectives  55.3 us (13%)
  local copies, waits for them, and re-layouts  35.6 us (8%)
  between operations  13.8 us (3%)
  starting transfers between devices  11.6 us (3%)
    all_gather x6, waiting for transfers between devices, gather(): full = lax.all_gather(block, ('tx', 'ty'), axis=0, axis_index_groups=groups)  124 us
    pallas_call x2, Pallas kernels, local_fn(): kernel(lambda *refs: attention_kernel(hl, dim, toks, *refs), [whole, row,...  42.2 us
    all_to_all x1, waiting for transfers between devices, local_fn(): x_t = lax.all_to_all(images, 'tx', split_axis=0, concat_axis=0, tiled=True)  41 us
    all_gather x1, waiting for transfers between devices, local_fn(): y = lax.all_gather(y, 'ty', axis=0, tiled=True)  36.4 us
    all_to_all x1, blocking collectives, local_fn(): lax.all_to_all(x.reshape(tx * nb, wl, toks), 'tx', split_axis=0, concat_a...  33.6 us
    all_gather x1, blocking collectives, local_fn(): vec = lax.all_gather(own, ('tx', 'ty'), axis=0)  21.7 us
    pallas_call x1, Pallas kernels, local_fn(): kernel(mlp_kernel, [whole, row, row, bias, row] + [anywhere] * 6, whole,...  20.3 us
    ppermute x3, waiting for transfers between devices, cross_plane(): got[key] = lax.ppermute(sent, 'dp', [(0, 1), (1, 0)])  16.6 us
  transfers between devices with their start and end apart: 14, of which 10 were waited for; matrix products, arithmetic and copies ran while one was open for 6% of the time, Pallas kernels for 18%

profile of v3, /device:TPU:0, one launch (start us, length us, event | category | flops | bytes accessed | tf_op | source)
XLA Modules:
  0.0 427.2 jit_solution(14249984641066623668)
XLA Ops:
  18.3 2.4 dynamic-slice_bitcast_fusion
  20.7 6.3 %all-to-all-start = ((bf16[8,288,256]{2,1,0:T(8,128)(2,1)}), bf16[8,288,256]{2,1,0:T(8,128)(2,1)S(1)}, u32[]{:S(2)}, u32[]{:S(2)}) async-start(bf16[8,288,256]{2,1,0:T(8,128)(2,1)} %dynamic-slice_bitcast_fusion), calls=%async_computation | async-start | bytes 2359296 | tf_op jit(solution)/shard_map/all_to_all | solution.py:208
  27.9 41.0 %all-to-all-done = bf16[8,288,256]{2,1,0:T(8,128)(2,1)S(1)} async-done(((bf16[8,288,256]{2,1,0:T(8,128)(2,1)}), bf16[8,288,256]{2,1,0:T(8,128)(2,1)S(1)}, u32[]{:S(2)}, u32[]{:S(2)}) %all-to-all-start) | async-done | bytes 1179680 | tf_op jit(solution)/shard_map/all_to_all | solution.py:208
  70.6 2.8 all-gather.22.cloned.1.call-done
  73.5 3.5 constant_dynamic-slice_fusion.1
  78.4 21.7 %all-gather.7 = f32[16,1,6760]{2,1,0:T(1,128)S(1)} all-gather(f32[1,1,6760]{2,1,0:T(1,128)S(1)} %bitcast.140), channel_id=5, replica_groups=mesh['dp'=2,'tx'=4,'ty'=4] {'tx','ty'}, dimensions={0}, use_global_device_ids=true | all-gather | bytes 459680 | tf_op jit(solution)/shard_map/all_gather | solution.py:227
  100.9 12.1 %all-gather.20.cloned.1.call-done = bf16[2304,1152]{1,0:T(8,128)(2,1)} async-done(((bf16[144,1152]{1,0:T(8,128)(2,1)}), bf16[2304,1152]{1,0:T(8,128)(2,1)}) %all-gather.20.cloned.1.call-update) | async-done | bytes 5308432 | tf_op jit(solution)/shard_map/all_gather | solution.py:198
  113.0 3.5 constant_dynamic-slice_fusion
  121.1 16.6 %collective-permute-done.2.u1 = bf16[2,4,144,1152]{3,2,1,0:T(8,128)(2,1)} collective-permute-done((bf16[2,4,144,1152]{3,2,1,0:T(8,128)(2,1)}, bf16[2,4,144,1152]{3,2,1,0:T(8,128)(2,1)}, u32[]{:S(2)}, u32[]{:S(2)}) %collective-permute-start.2) | collective-permute-done | bytes 2654240 | tf_op jit(solution)/shard_map/ppermute | solution.py:217
  137.7 35.9 %all-gather.24.cloned.1.call-done = bf16[4608,1152]{1,0:T(8,128)(2,1)} async-done(((bf16[288,1152]{1,0:T(8,128)(2,1)}), bf16[4608,1152]{1,0:T(8,128)(2,1)}) %all-gather.24.cloned.1.call-update) | async-done | bytes 10616848 | tf_op jit(solution)/shard_map/all_gather | solution.py:198
  173.6 21.1 %shard_map.154.x_ref = bf16[512,1152]{1,0:T(8,128)(2,1)} custom-call(bf16[512,1152]{1,0:T(8,128)(2,1)} %copy.53.refs_0_, f32[1,1152]{1,0:T(1,128)} %get-tuple-element.56.refs_1_, f32[1,1152]{1,0:T(1,128)} %get-tuple-element.55.refs_2_, f32[4,1,1152]{2,1,0:T(1,128)} %get-tuple-element.60.refs_3_, f32[1,1152]{1,0:T(1,128)} %get-tuple-element.54.refs_4_, ...), custom_call_target="tpu_custom_call" | custom-call | flops 21743271936 | bytes 21233664 | tf_op jit(solution)/shard_map/pallas_call | solution.py:263
  195.1 16.6 %all-gather.18.cloned.1.call-done = bf16[2304,1152]{1,0:T(8,128)(2,1)} async-done(((bf16[144,1152]{1,0:T(8,128)(2,1)}), bf16[2304,1152]{1,0:T(8,128)(2,1)}) %all-gather.18.cloned.1.call-update) | async-done | bytes 5308432 | tf_op jit(solution)/shard_map/all_gather | solution.py:198
  211.8 2.0 constant_dynamic-slice_fusion.2
  215.9 20.3 %shard_map.155.refs_0_ = bf16[512,1152]{1,0:T(8,128)(2,1)} custom-call(bf16[512,1152]{1,0:T(8,128)(2,1)} %shard_map.154.x_ref, f32[1,1152]{1,0:T(1,128)} %get-tuple-element.53.gain_ref, f32[1,1152]{1,0:T(1,128)} %get-tuple-element.52.shift_ref, f32[4,1,1152]{2,1,0:T(1,128)} %get-tuple-element.58.bias_ref, f32[1,1152]{1,0:T(1,128)} %get-tuple-element.51.bd_ref, ...), custom_call_target="tpu_custom_call" | custom-call | flops 21743271936 | bytes 21233664 | tf_op jit(solution)/shard_map/pallas_call | solution.py:272
  236.2 35.9 %all-gather.26.cloned.1.call-done = bf16[4608,1152]{1,0:T(8,128)(2,1)} async-done(((bf16[288,1152]{1,0:T(8,128)(2,1)}), bf16[4608,1152]{1,0:T(8,128)(2,1)}) %all-gather.26.cloned.1.call-update) | async-done | bytes 10616848 | tf_op jit(solution)/shard_map/all_gather | solution.py:198
  272.1 21.1 %shard_map.156.x_ref.refs_0_ = bf16[512,1152]{1,0:T(8,128)(2,1)} custom-call(bf16[512,1152]{1,0:T(8,128)(2,1)} %shard_map.155.refs_0_, f32[1,1152]{1,0:T(1,128)} %get-tuple-element.50.refs_1_, f32[1,1152]{1,0:T(1,128)} %get-tuple-element.49.refs_2_, f32[4,1,1152]{2,1,0:T(1,128)} %get-tuple-element.59.refs_3_, f32[1,1152]{1,0:T(1,128)} %get-tuple-element.48.refs_4_, ...), custom_call_target="tpu_custom_call" | custom-call | flops 21743271936 | bytes 21233664 | tf_op jit(solution)/shard_map/pallas_call | solution.py:263
  293.5 5.5 %collective-permute-done.5.u2 = bf16[2,4,144,1152]{3,2,1,0:T(8,128)(2,1)S(1)} collective-permute-done((bf16[2,4,144,1152]{3,2,1,0:T(8,128)(2,1)}, bf16[2,4,144,1152]{3,2,1,0:T(8,128)(2,1)S(1)}, u32[]{:S(2)}, u32[]{:S(2)}) %collective-permute-start.5) | collective-permute-done | bytes 2654240 | tf_op jit(solution)/shard_map/ppermute | solution.py:220
  298.9 1.5 copy-done.12
  300.5 12.3 %shard_map.157.refs_2_ = bf16[4,512,1152]{2,1,0:T(8,128)(2,1)} custom-call(bf16[512,1152]{1,0:T(8,128)(2,1)} %shard_map.156.x_ref.refs_0_, f32[1,1152]{1,0:T(1,128)} %get-tuple-element.46.gain_ref, f32[1,1152]{1,0:T(1,128)} %get-tuple-element.45.shift_ref, f32[4,1,1152]{2,1,0:T(1,128)} %get-tuple-element.57.bias_ref, bf16[4,4,144,1152]{3,2,1,0:T(8,128)(2,1)} %bitcast.128, ...), custom_call_target="tpu_custom_call" | custom-call | flops 10871635968 | bytes 21233664 | tf_op jit(solution)/shard_map/pallas_call | solution.py:277
  312.8 20.8 %all-gather.28.cloned.1.call-done = bf16[4608,1152]{1,0:T(8,128)(2,1)} async-done(((bf16[288,1152]{1,0:T(8,128)(2,1)}), bf16[4608,1152]{1,0:T(8,128)(2,1)}) %all-gather.28.cloned.1.call-update) | async-done | bytes 10616848 | tf_op jit(solution)/shard_map/all_gather | solution.py:198
  333.6 11.8 %shard_map.158 = bf16[4,2,288,256]{3,2,1,0:T(8,128)(2,1)} custom-call(bf16[512,1152]{1,0:T(8,128)(2,1)} %shard_map.156.x_ref.refs_0_, f32[1,1152]{1,0:T(1,128)} %get-tuple-element.47.refs_1_, bf16[4,512,1152]{2,1,0:T(8,128)(2,1)} %shard_map.157.refs_2_, bf16[4,4,288,1152]{3,2,1,0:T(8,128)(2,1)} %bitcast.141), custom_call_target="tpu_custom_call" | custom-call | flops 10871635968 | bytes 21233664 | tf_op jit(solution)/shard_map/pallas_call | solution.py:281
  345.4 33.6 %all_to_all.10 = bf16[8,288,256]{2,1,0:T(8,128)(2,1)} all-to-all(bf16[8,288,256]{2,1,0:T(8,128)(2,1)} %bitcast.129), channel_id=1, replica_groups=mesh['dp'=2,'tx'=4,'ty'=4] {'tx'}, dimensions={0} | all-to-all | bytes 2359296 | tf_op jit(solution)/shard_map/all_to_all | solution.py:285
  379.1 36.4 %all-gather.16.cloned.1.call-done = bf16[32,288,256]{2,1,0:T(8,128)(2,1)} async-done(((bf16[8,288,256]{2,1,0:T(8,128)(2,1)}), bf16[32,288,256]{2,1,0:T(8,128)(2,1)}) %all-gather.16.cloned.1.call-update) | async-done | bytes 4718608 | tf_op jit(solution)/shard_map/all_gather | solution.py:286
  415.5 4.8 %copy.60 = bf16[32,256,288]{1,2,0:T(8,128)(2,1)} copy(bf16[32,256,288]{1,2,0:T(8,128)(2,1)} %bitcast.118) | data formatting | bytes 9437184
  (101 shorter events, 23.9 us)
Async XLA Ops:
  6.5 2.4 copy-start
  6.5 67.0 %all-gather.22.cloned.1.call-start = ((), (), s32[]{:S(2)}) async-start(), calls=%async_computation.5 | async-start | bytes 5640192 | tf_op jit(solution)/shard_map/all_gather | solution.py:198
  8.9 104.1 %all-gather.20.cloned.1.call-start = ((), (), s32[]{:S(2)}) async-start(), calls=%async_computation.4 | async-start | bytes 5640192 | tf_op jit(solution)/shard_map/all_gather | solution.py:198
  9.8 163.8 %all-gather.24.cloned.1.call-start = ((), (), s32[]{:S(2)}) async-start(), calls=%async_computation.6 | async-start | bytes 11280384 | tf_op jit(solution)/shard_map/all_gather | solution.py:198
  14.2 197.5 %all-gather.18.cloned.1.call-start = ((), (), s32[]{:S(2)}) async-start(), calls=%async_computation.3 | async-start | bytes 5640192 | tf_op jit(solution)/shard_map/all_gather | solution.py:198
  15.1 257.0 %all-gather.26.cloned.1.call-start = ((), (), s32[]{:S(2)}) async-start(), calls=%async_computation.7 | async-start | bytes 11280384 | tf_op jit(solution)/shard_map/all_gather | solution.py:198
  17.2 316.4 %all-gather.28.cloned.1.call-start = ((), (), s32[]{:S(2)}) async-start(), calls=%async_computation.8 | async-start | bytes 11280384 | tf_op jit(solution)/shard_map/all_gather | solution.py:198
  18.2 8.9 %copy-start.3 = (f32[2,1076]{1,0:T(2,128)S(1)}, f32[2,1076]{1,0:T(2,128)}, u32[]{:S(2)}) copy-start(f32[2,1076]{1,0:T(2,128)} %param.29) | copy-start | bytes 25828
  18.2 8.9 %copy-start.6 = (f32[2,288]{1,0:T(2,128)S(1)}, f32[2,288]{1,0:T(2,128)}, u32[]{:S(2)}) copy-start(f32[2,288]{1,0:T(2,128)} %param.17) | copy-start | bytes 6916
  18.2 9.0 %copy-start.7 = (f32[2,288]{1,0:T(2,128)S(1)}, f32[2,288]{1,0:T(2,128)}, u32[]{:S(2)}) copy-start(f32[2,288]{1,0:T(2,128)} %param.18) | copy-start | bytes 6916
  18.2 9.1 %copy-start.8 = (f32[2,288]{1,0:T(2,128)S(1)}, f32[2,288]{1,0:T(2,128)}, u32[]{:S(2)}) copy-start(f32[2,288]{1,0:T(2,128)} %param.26) | copy-start | bytes 6916
  18.2 9.2 %copy-start.9 = (f32[2,288]{1,0:T(2,128)S(1)}, f32[2,288]{1,0:T(2,128)}, u32[]{:S(2)}) copy-start(f32[2,288]{1,0:T(2,128)} %param.27) | copy-start | bytes 6916
  18.2 9.3 %copy-start.10 = (f32[2,288]{1,0:T(2,128)S(1)}, f32[2,288]{1,0:T(2,128)}, u32[]{:S(2)}) copy-start(f32[2,288]{1,0:T(2,128)} %param.25) | copy-start | bytes 6916
  18.2 9.3 %copy-start.11 = (f32[2,288]{1,0:T(2,128)S(1)}, f32[2,288]{1,0:T(2,128)}, u32[]{:S(2)}) copy-start(f32[2,288]{1,0:T(2,128)} %param.31) | copy-start | bytes 6916
  18.2 9.4 %copy-start.4 = (f32[2,4,72]{2,1,0:T(4,128)S(1)}, f32[2,4,72]{2,1,0:T(4,128)}, u32[]{:S(2)}) copy-start(f32[2,4,72]{2,1,0:T(4,128)} %param.20) | copy-start | bytes 6916
  18.2 9.5 %copy-start.5 = (f32[2,4,72]{2,1,0:T(4,128)S(1)}, f32[2,4,72]{2,1,0:T(4,128)}, u32[]{:S(2)}) copy-start(f32[2,4,72]{2,1,0:T(4,128)} %param.23) | copy-start | bytes 6916
  20.7 48.3 %all-to-all-start = ((bf16[8,288,256]{2,1,0:T(8,128)(2,1)}), bf16[8,288,256]{2,1,0:T(8,128)(2,1)S(1)}, u32[]{:S(2)}, u32[]{:S(2)}) async-start(bf16[8,288,256]{2,1,0:T(8,128)(2,1)} %dynamic-slice_bitcast_fusion), calls=%async_computation | async-start | bytes 2359296 | tf_op jit(solution)/shard_map/all_to_all | solution.py:208
  27.0 388.5 %all-gather.16.cloned.1.call-start = ((), (), s32[]{:S(2)}) async-start(), calls=%async_computation.2 | async-start | bytes 5898240 | tf_op jit(solution)/shard_map/all_gather | solution.py:286
  76.9 60.8 %collective-permute-start.2 = (bf16[2,4,144,1152]{3,2,1,0:T(8,128)(2,1)}, bf16[2,4,144,1152]{3,2,1,0:T(8,128)(2,1)}, u32[]{:S(2)}, u32[]{:S(2)}) collective-permute-start(bf16[2,4,144,1152]{3,2,1,0:T(8,128)(2,1)} %constant_dynamic-slice_fusion.1), channel_id=1, source_target_pairs={{0,16},{16,0},{1,17},{17,1},{2,18},{18,2},{3,19},{19,3},{4,20},{20... | collective-permute-start | bytes 7962632 | tf_op jit(solution)/shard_map/ppermute | solution.py:217
  116.4 78.3 %collective-permute-start.1 = (bf16[2,4,144,1152]{3,2,1,0:T(8,128)(2,1)}, bf16[2,4,144,1152]{3,2,1,0:T(8,128)(2,1)}, u32[]{:S(2)}, u32[]{:S(2)}) collective-permute-start(bf16[2,4,144,1152]{3,2,1,0:T(8,128)(2,1)} %constant_dynamic-slice_fusion), channel_id=1, source_target_pairs={{0,16},{16,0},{1,17},{17,1},{2,18},{18,2},{3,19},{19,3},{4,20},{20... | collective-permute-start | bytes 7962632 | tf_op jit(solution)/shard_map/ppermute | solution.py:217
  137.7 78.2 %collective-permute-start.3 = (bf16[2,4,144,1152]{3,2,1,0:T(8,128)(2,1)}, bf16[2,4,144,1152]{3,2,1,0:T(8,128)(2,1)}, u32[]{:S(2)}, u32[]{:S(2)}) collective-permute-start(bf16[2,4,144,1152]{3,2,1,0:T(8,128)(2,1)} %collective-permute-done.2.u1), channel_id=1, source_target_pairs={{0,1},{1,0},{2,3},{3,2},{4,5},{5,4},{6,7},{7,6},{8,9},{9,8},{10,11... | collective-permute-start | bytes 7962632 | tf_op jit(solution)/shard_map/ppermute | solution.py:220
  194.7 21.2 %collective-permute-start.4 = (bf16[2,4,144,1152]{3,2,1,0:T(8,128)(2,1)}, bf16[2,4,144,1152]{3,2,1,0:T(8,128)(2,1)}, u32[]{:S(2)}, u32[]{:S(2)}) collective-permute-start(bf16[2,4,144,1152]{3,2,1,0:T(8,128)(2,1)} %collective-permute-done.1.d1), channel_id=1, source_target_pairs={{0,1},{1,0},{2,3},{3,2},{4,5},{5,4},{6,7},{7,6},{8,9},{9,8},{10,11... | collective-permute-start | bytes 7962632 | tf_op jit(solution)/shard_map/ppermute | solution.py:220
  213.7 79.5 %collective-permute-start = (bf16[2,4,144,1152]{3,2,1,0:T(8,128)(2,1)S(1)}, bf16[2,4,144,1152]{3,2,1,0:T(8,128)(2,1)}, u32[]{:S(2)}, u32[]{:S(2)}) collective-permute-start(bf16[2,4,144,1152]{3,2,1,0:T(8,128)(2,1)S(1)} %constant_dynamic-slice_fusion.2), channel_id=1, source_target_pairs={{0,16},{16,0},{1,17},{17,1},{2,18},{18,2},{3,19},{19,3},{4,20},{20... | collective-permute-start | bytes 7962632 | tf_op jit(solution)/shard_map/ppermute | solution.py:217
  293.2 5.7 %collective-permute-start.5 = (bf16[2,4,144,1152]{3,2,1,0:T(8,128)(2,1)}, bf16[2,4,144,1152]{3,2,1,0:T(8,128)(2,1)S(1)}, u32[]{:S(2)}, u32[]{:S(2)}) collective-permute-start(bf16[2,4,144,1152]{3,2,1,0:T(8,128)(2,1)} %collective-permute-done.u1), channel_id=1, source_target_pairs={{0,1},{1,0},{2,3},{3,2},{4,5},{5,4},{6,7},{7,6},{8,9},{9,8},{10,11... | collective-permute-start | bytes 7962632 | tf_op jit(solution)/shard_map/ppermute | solution.py:220
  (3 other events, 4.6 us)
Sparse Core Ops, SparseCore 0:
  9.0 64.4 all-gather.21
  75.1 37.8 all-gather.19
  114.6 58.9 all-gather.23
  175.0 36.6 all-gather.17
  213.2 58.8 all-gather.25
  273.6 59.9 all-gather.27
  379.2 36.2 all-gather.15

commit v4 on v3

--- a/solution.py
+++ b/solution.py
@@ -86,7 +86,7 @@
     return slot
 
 
-def half_loads(srcs, bufs, sems):
+def half_loads(offsets, srcs, bufs, sems):
     plane = lax.axis_index("dp")
     core = lax.rem(lax.axis_index("ty"), 2)
 
@@ -95,7 +95,7 @@
         for w, buf in enumerate(bufs):
             own, same, other = srcs[3 * w:3 * w + 3]
             pair = same.shape[0]
-            parts = [(own.at[:, i], buf.at[slot, :, plane]),
+            parts = [(own.at[:, i, pl.ds(offsets[w], buf.shape[3])], buf.at[slot, :, plane]),
                      (same.at[:, i], buf.at[slot, pl.ds(core * pair, pair), 1 - plane]),
                      (other.at[:, i], buf.at[slot, pl.ds((1 - core) * pair, pair), 1 - plane])]
             copies += [pltpu.make_async_copy(src, dst, sems.at[slot, w, j]) for j, (src, dst) in enumerate(parts)]
@@ -104,7 +104,7 @@
     return loads
 
 
-def mlp_kernel(x_ref, gain_ref, shift_ref, bias_ref, bd_ref, u0, u1, u2, d0, d1, d2, out_ref, h_ref, acc_ref, up_buf, down_buf, sems):
+def mlp_kernel(offsets, x_ref, gain_ref, shift_ref, bias_ref, bd_ref, u0, u1, u2, d0, d1, d2, out_ref, h_ref, acc_ref, up_buf, down_buf, sems):
     step = pl.program_id(0)
     width = x_ref.shape[-1]
 
@@ -112,7 +112,7 @@
         h_ref[...] = norm_rows(x_ref[...].astype(F32), gain_ref[...], shift_ref[...])
         acc_ref[...] = jnp.zeros_like(acc_ref)
 
-    slot = load_ahead(half_loads((u0, u1, u2, d0, d1, d2), (up_buf, down_buf), sems), first)
+    slot = load_ahead(half_loads(offsets, (u0, u1, u2, d0, d1, d2), (up_buf, down_buf), sems), first)
     up = up_buf[slot].reshape(width, up_buf.shape[-1])
     down = down_buf[slot].reshape(width, down_buf.shape[-1])
     u = jax.nn.gelu(dot_nn(h_ref[...], up) + bias_ref[0], approximate=True).astype(BF)
@@ -123,18 +123,18 @@
         out_ref[...] = (x_ref[...].astype(F32) + acc_ref[...] + bd_ref[...]).astype(BF)
 
 
-def up_kernel(x_ref, gain_ref, shift_ref, bias_ref, u0, u1, u2, out_ref, h_ref, up_buf, sems):
+def up_kernel(offsets, x_ref, gain_ref, shift_ref, bias_ref, u0, u1, u2, out_ref, h_ref, up_buf, sems):
     width = x_ref.shape[-1]
 
     def first():
         h_ref[...] = norm_rows(x_ref[...].astype(F32), gain_ref[...], shift_ref[...])
 
-    slot = load_ahead(half_loads((u0, u1, u2), (up_buf,), sems), first)
+    slot = load_ahead(half_loads(offsets, (u0, u1, u2), (up_buf,), sems), first)
     up = up_buf[slot].reshape(width, up_buf.shape[-1])
     out_ref[0] = jax.nn.gelu(dot_nn(h_ref[...], up) + bias_ref[0], approximate=True).astype(BF)
 
 
-def down_kernel(order, toks, x_ref, bd_ref, u_ref, down_ref, out_ref, acc_ref):
+def down_kernel(order, x_ref, bd_ref, u_ref, down_ref, out_ref, acc_ref):
     step = pl.program_id(0)
     width = x_ref.shape[-1]
 
@@ -146,11 +146,26 @@
 
     @pl.when(step == pl.num_programs(0) - 1)
     def _():
-        wl = out_ref.shape[2]
+        wl = out_ref.shape[1]
         y_t = acc_ref[...].T.astype(BF)
         for i, block in enumerate(order):
-            for img in range(out_ref.shape[1]):
-                out_ref[block, img] = y_t[i * wl:(i + 1) * wl, img * toks:(img + 1) * toks]
+            out_ref[block] = y_t[i * wl:(i + 1) * wl]
+
+
+def place_kernel(tx, ty, per, nb, *refs):
+    *srcs, out_ref, sems = refs
+    t, y = lax.axis_index("tx"), lax.axis_index("ty")
+    copies = []
+    for j, src in enumerate(srcs):
+        img, dist = divmod(j, ty)
+        group = y + dist - 2 * sum(bit * lax.rem(y // bit, 2) for bit in (1, 2) if dist & bit)
+        for k in range(tx):
+            index = group * per + lax.rem(t - k + tx, tx) * nb + img
+            copies.append(pltpu.make_async_copy(src.at[k], out_ref.at[index], sems.at[j, k]))
+    for copy in copies:
+        copy.start()
+    for copy in copies:
+        copy.wait()
 
 
 def solution(mesh):
@@ -199,10 +214,16 @@
             return full.reshape(tx, ty, *block.shape)
 
         halves = [("u", 0), ("d", 0), ("u", 1)]
-        makers = {"u": up_block, "d": down_block}
-        split = {(kind, l): gather(lax.dynamic_slice_in_dim(makers[kind](l), plane * half, half, axis=0)) for kind, l in halves}
-        proj = [gather(proj_block(0)), gather(proj_block(1))]
+
+        def half_block(block):
+            return lax.dynamic_slice_in_dim(block, plane * half, half, axis=0)
+
+        first = gather(jnp.concatenate([half_block(up_block(0)), half_block(down_block(0))], axis=0))
+        second = gather(jnp.concatenate([proj_block(0), half_block(up_block(1))], axis=0))
+        third = gather(proj_block(1))
         last_down = gather(down_block(1))
+        proj = [second, third]
+        split = {("u", 0): (first, 0), ("d", 0): (first, half), ("u", 1): (second, wl)}
 
         images = lax.dynamic_slice_in_dim(x_in.transpose(0, 2, 1), lax.axis_index("ty") * per, per, axis=0)
         x_t = lax.all_to_all(images, "tx", split_axis=0, concat_axis=0, tiled=True)
@@ -211,7 +232,8 @@
         got, crossed = {}, {}
 
         def to_send(key):
-            return lax.dynamic_slice_in_dim(split[key], core * (tx // 2), tx // 2, axis=0)
+            full, at = split[key]
+            return lax.dynamic_slice(full, (core * (tx // 2), 0, at, 0), (tx // 2, ty, half, cols))
 
         def cross_plane(key, sent):
             got[key] = lax.ppermute(sent, "dp", [(0, 1), (1, 0)])
@@ -219,7 +241,8 @@
         def cross_core(key):
             crossed[key] = (got[key], lax.ppermute(got[key], "ty", swap))
 
-        split[halves[0]], x = lax.optimization_barrier((split[halves[0]], x))
+        first, x = lax.optimization_barrier((first, x))
+        split["u", 0] = (first, 0)
         on_tx = [ln1_gain, ln1_bias, ln2_gain, ln2_bias, b_o, b_down]
         on_ty = [b_q.reshape(layers, hd), b_v.reshape(layers, hd), b_up]
         own = jnp.concatenate([a.reshape(1, -1) for a in on_tx + on_ty], axis=1)
@@ -238,8 +261,8 @@
 
         cross_plane(halves[0], sent)
         for key in halves[1:]:
-            split[key], vec = lax.optimization_barrier((split[key], vec))
-            cross_plane(key, to_send(key))
+            sent, vec = lax.optimization_barrier((to_send(key), vec))
+            cross_plane(key, sent)
         cross_core(halves[0])
 
         whole = pl.BlockSpec((n, width), lambda i: (0, 0))
@@ -249,7 +272,7 @@
         params = pltpu.CompilerParams(vmem_limit_bytes=VMEM_BYTES, dimension_semantics=("arbitrary",))
 
         anywhere = pl.BlockSpec(memory_space=pl.ANY)
-        rows_bf, rows_f = scratch
+        rows_bf, _ = scratch
         half_buf = pltpu.VMEM((2, tx, 2, half, cols), BF)
         act = jax.ShapeDtypeStruct((n, width), BF)
         dot_flops = 2 * n * width * cols * ty
@@ -266,24 +289,45 @@
             late = halves[l + 1]
             got[late], x = lax.optimization_barrier((got[late], x))
             cross_core(late)
-            up = (split["u", l], *crossed["u", l])
+            up = (split["u", l][0], *crossed["u", l])
             if l < layers - 1:
-                down = (split["d", l], *crossed["d", l])
-                x = kernel(mlp_kernel, [whole, row, row, bias, row] + [anywhere] * 6, whole, act,
+                down = (split["d", l][0], *crossed["d", l])
+                offsets = (split["u", l][1], split["d", l][1])
+                x = kernel(lambda *refs, o=offsets: mlp_kernel(o, *refs), [whole, row, row, bias, row] + [anywhere] * 6, whole, act,
                            scratch + [half_buf, half_buf, pltpu.SemaphoreType.DMA((2, 2, 3))], 4 * dot_flops,
                            )(x, vt[2, l], vt[3, l], bias_u[l], vt[5, l], *up, *down)
             else:
                 hidden = pl.BlockSpec((1, n, cols), lambda i: (i, 0, 0))
-                u = kernel(up_kernel, [whole, row, row, bias] + [anywhere] * 3, hidden,
+                u = kernel(lambda *refs, o=(split["u", l][1],): up_kernel(o, *refs), [whole, row, row, bias] + [anywhere] * 3, hidden,
                            jax.ShapeDtypeStruct((ty, n, cols), BF), [rows_bf, half_buf, pltpu.SemaphoreType.DMA((2, 1, 3))],
                            2 * dot_flops)(x, vt[2, l], vt[3, l], bias_u[l], *up)
-                out = (tx, nb, wl, toks)
-                x = kernel(lambda *refs: down_kernel(order, toks, *refs),
-                           [whole, row, hidden, pl.BlockSpec((tx, 1, wl, cols), lambda i: (0, i, 0, 0))],
-                           pl.BlockSpec(out, lambda i: (0, 0, 0, 0)), jax.ShapeDtypeStruct(out, BF), [rows_f],
-                           2 * dot_flops)(x, vt[5, l], u, last_down)
-        y = lax.all_to_all(x.reshape(tx * nb, wl, toks), "tx", split_axis=0, concat_axis=0, tiled=True)
-        y = lax.all_gather(y, "ty", axis=0, tiled=True)
+                outs = []
+                for img in range(nb):
+                    outs.append(kernel(lambda *refs: down_kernel(order, *refs),
+                                       [pl.BlockSpec((toks, width), lambda i, m=img: (m, 0)), row,
+                                        pl.BlockSpec((1, toks, cols), lambda i, m=img: (i, m, 0)),
+                                        pl.BlockSpec((tx, 1, wl, cols), lambda i: (0, i, 0, 0))],
+                                       pl.BlockSpec((tx, wl, toks), lambda i: (0, 0, 0)),
+                                       jax.ShapeDtypeStruct((tx, wl, toks), BF), [pltpu.VMEM((toks, width), F32)],
+                                       2 * dot_flops // nb)(x, vt[5, l], u, last_down))
+        me = lax.axis_index("tx")
+        pieces = []
+        for y_i in outs:
+            moved = []
+            for k in range(tx):
+                part = lax.dynamic_index_in_dim(y_i, (me + k) % tx, keepdims=False)
+                moved.append(lax.ppermute(part, "tx", [(i, (i + k) % tx) for i in range(tx)]) if k else part)
+            by_group = [jnp.stack(moved)]
+            for dist in range(1, ty):
+                bit = dist & -dist
+                by_group.append(lax.ppermute(by_group[dist - bit], "ty", [(i, i ^ bit) for i in range(ty)]))
+            pieces += by_group
+        y = pl.pallas_call(lambda *refs: place_kernel(tx, ty, per, nb, *refs),
+                           in_specs=[pl.BlockSpec(memory_space=pltpu.VMEM)] * len(pieces),
+                           out_specs=pl.BlockSpec(memory_space=pl.ANY),
+                           out_shape=jax.ShapeDtypeStruct((imgs, wl, toks), BF),
+                           scratch_shapes=[pltpu.SemaphoreType.DMA((len(pieces), tx))],
+                           compiler_params=pltpu.CompilerParams(vmem_limit_bytes=VMEM_BYTES // 2), name="place")(*pieces)
         return y.transpose(0, 2, 1)
 
     return jax.shard_map(local_fn, mesh=mesh, in_specs=in_specs, out_specs=act_spec, check_vma=False)

time: 428 us -> 377 us (0.88)
  waiting for transfers between devices: 224 us -> 189 us
  blocking collectives: 55.3 us -> 24.5 us
  starting transfers between devices: 11.6 us -> 22.5 us
  Pallas kernels: 86.7 us -> 93.9 us
  local copies, waits for them, and re-layouts: 35.6 us -> 30.4 us
    all_gather x6 -> x4, waiting for transfers between devices: 124 us -> 65.7 us  [gather(): full = lax.all_gather(block, ('tx', 'ty'), axis=0, axis_index_groups=groups)]
    all_gather x1 -> x0, waiting for transfers between devices: 36.4 us -> none  [local_fn(): y = lax.all_gather(y, 'ty', axis=0, tiled=True)]
    all_to_all x1 -> x0, blocking collectives: 33.6 us -> none  [local_fn(): lax.all_to_all(x.reshape(tx * nb, wl, toks), 'tx', split_axis=0, concat_a...]
    ppermute x3, waiting for transfers between devices: 16.6 us -> 50.1 us  [cross_plane(): got[key] = lax.ppermute(sent, 'dp', [(0, 1), (1, 0)])]
    ppermute x0 -> x12, waiting for transfers between devices: none -> 25.3 us  [the longest x6 17.3 us: local_fn(): lax.ppermute(by_group[dist - bit], 'ty', [(i, i ^ bit) for i in range(ty)])]
    ppermute x0 -> x12, starting transfers between devices: none -> 12.7 us  [the longest x6 9.27 us: local_fn(): lax.ppermute(part, 'tx', [(i, (i + k) % tx) for i in range(tx)])]
    pallas_call x3 -> x5, Pallas kernels: 44.4 us -> 51.7 us  [the longest x1 19.9 us: local_fn(): kernel(lambda *refs, o=offsets: mlp_kernel(o, *refs), [whole, row, row, b...]
    unnamed x28 -> x27, local copies, waits for them, and re-layouts: 6.7 us -> 2.15 us
  transfers between devices with their start and end apart: 14 -> 23, of which waited for: 10 -> 15; matrix products, arithmetic and copies ran while one was open for 6% -> 7% of each run, Pallas kernels for 18% -> 22%
where the time goes in v4:
time: 377 us; the launch traced here: 376 us
  waiting for transfers between devices  189 us (50%)
  Pallas kernels  93.9 us (25%)
  local copies, waits for them, and re-layouts  30.4 us (8%)
  blocking collectives  24.5 us (6%)
  starting transfers between devices  22.5 us (6%)
  between operations  13.5 us (4%)
    all_gather x4, waiting for transfers between devices, gather(): full = lax.all_gather(block, ('tx', 'ty'), axis=0, axis_index_groups=groups)  65.7 us
    ppermute x3, waiting for transfers between devices, cross_plane(): got[key] = lax.ppermute(sent, 'dp', [(0, 1), (1, 0)])  50.1 us
    pallas_call x2, Pallas kernels, local_fn(): kernel(lambda *refs: attention_kernel(hl, dim, toks, *refs), [whole, row,...  42.2 us
    all_to_all x1, waiting for transfers between devices, local_fn(): x_t = lax.all_to_all(images, 'tx', split_axis=0, concat_axis=0, tiled=True)  40.6 us
    all_gather x1, blocking collectives, local_fn(): vec = lax.all_gather(own, ('tx', 'ty'), axis=0)  24.5 us
    pallas_call x1, Pallas kernels, local_fn(): kernel(lambda *refs, o=offsets: mlp_kernel(o, *refs), [whole, row, row, b...  19.9 us
    ppermute x6, waiting for transfers between devices, local_fn(): lax.ppermute(by_group[dist - bit], 'ty', [(i, i ^ bit) for i in range(ty)])  17.3 us
    pallas_call x2, Pallas kernels, local_fn(): kernel(lambda *refs: down_kernel(order, *refs), [pl.BlockSpec((toks, widt...  17 us
  transfers between devices with their start and end apart: 23, of which 15 were waited for; matrix products, arithmetic and copies ran while one was open for 7% of the time, Pallas kernels for 22%

profile of v4, /device:TPU:0, one launch (start us, length us, event | category | flops | bytes accessed | tf_op | source)
XLA Modules:
  0.0 376.4 jit_solution(10873896933555383064)
XLA Ops:
  21.3 6.3 %all-to-all-start = ((bf16[8,288,256]{2,1,0:T(8,128)(2,1)}), bf16[8,288,256]{2,1,0:T(8,128)(2,1)S(1)}, u32[]{:S(2)}, u32[]{:S(2)}) async-start(bf16[8,288,256]{2,1,0:T(8,128)(2,1)} %dynamic-slice_bitcast_fusion), calls=%async_computation | async-start | bytes 2359296 | tf_op jit(solution)/shard_map/all_to_all | solution.py:229
  28.6 40.6 %all-to-all-done = bf16[8,288,256]{2,1,0:T(8,128)(2,1)S(1)} async-done(((bf16[8,288,256]{2,1,0:T(8,128)(2,1)}), bf16[8,288,256]{2,1,0:T(8,128)(2,1)S(1)}, u32[]{:S(2)}, u32[]{:S(2)}) %all-to-all-start) | async-done | bytes 1179680 | tf_op jit(solution)/shard_map/all_to_all | solution.py:229
  70.9 24.1 %all-gather.13.cloned.1.call-done = bf16[4608,1152]{1,0:T(8,128)(2,1)} async-done(((bf16[288,1152]{1,0:T(8,128)(2,1)}), bf16[4608,1152]{1,0:T(8,128)(2,1)}) %all-gather.13.cloned.1.call-update) | async-done | bytes 10616848 | tf_op jit(solution)/shard_map/all_gather | solution.py:213
  95.0 5.3 %constant_dynamic-slice_fusion.2 = (bf16[2,4,144,1152]{3,2,1,0:T(8,128)(2,1)}, bf16[2,4,144,1152]{3,2,1,0:T(8,128)(2,1)}) fusion(bf16[4,4,288,1152]{3,2,1,0:T(8,128)(2,1)} %bitcast.135, s32[]{:T(128)S(6)} %select_n.63), kind=kLoop, calls=%fused_computation.50 | loop fusion | bytes 10616836 | tf_op jit(solution)/shard_map/dynamic_slice | solution.py:236
  101.8 24.5 %all-gather.5 = f32[16,1,6760]{2,1,0:T(1,128)S(1)} all-gather(f32[1,1,6760]{2,1,0:T(1,128)S(1)} %bitcast.159), channel_id=4, replica_groups=mesh['dp'=2,'tx'=4,'ty'=4] {'tx','ty'}, dimensions={0}, use_global_device_ids=true | all-gather | bytes 459680 | tf_op jit(solution)/shard_map/all_gather | solution.py:250
  130.5 30.5 %collective-permute-done.2.refs_6_ = bf16[2,4,144,1152]{3,2,1,0:T(8,128)(2,1)} collective-permute-done((bf16[2,4,144,1152]{3,2,1,0:T(8,128)(2,1)}, bf16[2,4,144,1152]{3,2,1,0:T(8,128)(2,1)}, u32[]{:S(2)}, u32[]{:S(2)}) %collective-permute-start.2) | collective-permute-done | bytes 2654240 | tf_op jit(solution)/shard_map/ppermute | solution.py:239
  161.1 26.1 %all-gather.11.cloned.1.call-done = bf16[6912,1152]{1,0:T(8,128)(2,1)} async-done(((bf16[432,1152]{1,0:T(8,128)(2,1)}), bf16[6912,1152]{1,0:T(8,128)(2,1)}) %all-gather.11.cloned.1.call-update) | async-done | bytes 15925264 | tf_op jit(solution)/shard_map/all_gather | solution.py:213
  187.1 21.1 %shard_map.154.refs_0_ = bf16[512,1152]{1,0:T(8,128)(2,1)} custom-call(bf16[512,1152]{1,0:T(8,128)(2,1)} %copy.53.refs_0_, f32[1,1152]{1,0:T(1,128)} %get-tuple-element.64.refs_1_, f32[1,1152]{1,0:T(1,128)} %get-tuple-element.63.refs_2_, f32[4,1,1152]{2,1,0:T(1,128)} %get-tuple-element.68.refs_3_, f32[1,1152]{1,0:T(1,128)} %get-tuple-element.62.refs_4_, ...), custom_call_target="tpu_custom_call" | custom-call | flops 21743271936 | bytes 21233664 | tf_op jit(solution)/shard_map/pallas_call | solution.py:286
  208.2 9.0 %collective-permute-done.1.refs_9_ = bf16[2,4,144,1152]{3,2,1,0:T(8,128)(2,1)} collective-permute-done((bf16[2,4,144,1152]{3,2,1,0:T(8,128)(2,1)}, bf16[2,4,144,1152]{3,2,1,0:T(8,128)(2,1)}, u32[]{:S(2)}, u32[]{:S(2)}) %collective-permute-start.1) | collective-permute-done | bytes 2654240 | tf_op jit(solution)/shard_map/ppermute | solution.py:239
  223.2 19.9 %shard_map.155.refs_0_ = bf16[512,1152]{1,0:T(8,128)(2,1)} custom-call(bf16[512,1152]{1,0:T(8,128)(2,1)} %shard_map.154.refs_0_, f32[1,1152]{1,0:T(1,128)} %get-tuple-element.61.refs_1_, f32[1,1152]{1,0:T(1,128)} %get-tuple-element.60.refs_2_, f32[4,1,1152]{2,1,0:T(1,128)} %get-tuple-element.66.refs_3_, f32[1,1152]{1,0:T(1,128)} %get-tuple-element.59.refs_4_, ...), custom_call_target="tpu_custom_call" | custom-call | flops 21743271936 | bytes 21233664 | tf_op jit(solution)/shard_map/pallas_call | solution.py:296
  243.1 5.3 %all-gather.15.cloned.1.call-done = bf16[4608,1152]{1,0:T(8,128)(2,1)} async-done(((bf16[288,1152]{1,0:T(8,128)(2,1)}), bf16[4608,1152]{1,0:T(8,128)(2,1)}) %all-gather.15.cloned.1.call-update) | async-done | bytes 10616848 | tf_op jit(solution)/shard_map/all_gather | solution.py:213
  248.5 21.1 %shard_map.156.refs_0_ = bf16[512,1152]{1,0:T(8,128)(2,1)} custom-call(bf16[512,1152]{1,0:T(8,128)(2,1)} %shard_map.155.refs_0_, f32[1,1152]{1,0:T(1,128)} %get-tuple-element.58.refs_1_, f32[1,1152]{1,0:T(1,128)} %get-tuple-element.57.refs_2_, f32[4,1,1152]{2,1,0:T(1,128)} %get-tuple-element.67.refs_3_, f32[1,1152]{1,0:T(1,128)} %get-tuple-element.56.refs_4_, ...), custom_call_target="tpu_custom_call" | custom-call | flops 21743271936 | bytes 21233664 | tf_op jit(solution)/shard_map/pallas_call | solution.py:286
  269.6 10.6 %collective-permute-done.refs_5_ = bf16[2,4,144,1152]{3,2,1,0:T(8,128)(2,1)} collective-permute-done((bf16[2,4,144,1152]{3,2,1,0:T(8,128)(2,1)S(1)}, bf16[2,4,144,1152]{3,2,1,0:T(8,128)(2,1)}, u32[]{:S(2)}, u32[]{:S(2)}) %collective-permute-start) | collective-permute-done | bytes 2654240 | tf_op jit(solution)/shard_map/ppermute | solution.py:239
  280.2 5.7 %collective-permute-done.5.refs_6_ = bf16[2,4,144,1152]{3,2,1,0:T(8,128)(2,1)S(1)} collective-permute-done((bf16[2,4,144,1152]{3,2,1,0:T(8,128)(2,1)}, bf16[2,4,144,1152]{3,2,1,0:T(8,128)(2,1)S(1)}, u32[]{:S(2)}, u32[]{:S(2)}) %collective-permute-start.5) | collective-permute-done | bytes 2654240 | tf_op jit(solution)/shard_map/ppermute | solution.py:242
  287.5 12.3 %shard_map.157.refs_2_ = bf16[4,512,1152]{2,1,0:T(8,128)(2,1)} custom-call(bf16[512,1152]{1,0:T(8,128)(2,1)} %shard_map.156.refs_0_, f32[1,1152]{1,0:T(1,128)} %get-tuple-element.54.refs_1_, f32[1,1152]{1,0:T(1,128)} %get-tuple-element.53.refs_2_, f32[4,1,1152]{2,1,0:T(1,128)} %get-tuple-element.65.refs_3_, bf16[4,4,432,1152]{3,2,1,0:T(8,128)(2,1)} %bitcast.150, ...), custom_call_target="tpu_custom_call" | custom-call | flops 10871635968 | bytes 21233664 | tf_op jit(solution)/shard_map/pallas_call | solution.py:301
  299.8 10.2 %all-gather.17.cloned.1.call-done = bf16[4608,1152]{1,0:T(8,128)(2,1)} async-done(((bf16[288,1152]{1,0:T(8,128)(2,1)}), bf16[4608,1152]{1,0:T(8,128)(2,1)}) %all-gather.17.cloned.1.call-update) | async-done | bytes 10616848 | tf_op jit(solution)/shard_map/all_gather | solution.py:213
  309.9 8.5 %shard_map.159 = bf16[4,288,256]{2,1,0:T(8,128)(2,1)} custom-call(bf16[512,1152]{1,0:T(8,128)(2,1)} %shard_map.156.refs_0_, f32[1,1152]{1,0:T(1,128)} %get-tuple-element.55.refs_1_, bf16[4,512,1152]{2,1,0:T(8,128)(2,1)} %shard_map.157.refs_2_, bf16[4,4,288,1152]{3,2,1,0:T(8,128)(2,1)} %bitcast.160), custom_call_target="tpu_custom_call" | custom-call | flops 5435817984 | bytes 21233664 | tf_op jit(solution)/shard_map/pallas_call | solution.py:306
  325.0 8.6 %shard_map.158 = bf16[4,288,256]{2,1,0:T(8,128)(2,1)} custom-call(bf16[512,1152]{1,0:T(8,128)(2,1)} %shard_map.156.refs_0_, f32[1,1152]{1,0:T(1,128)} %get-tuple-element.55.refs_1_, bf16[4,512,1152]{2,1,0:T(8,128)(2,1)} %shard_map.157.refs_2_, bf16[4,4,288,1152]{3,2,1,0:T(8,128)(2,1)} %bitcast.161), custom_call_target="tpu_custom_call" | custom-call | flops 5435817984 | bytes 21233664 | tf_op jit(solution)/shard_map/pallas_call | solution.py:306
  335.9 2.7 collective-permute-start.8
  340.1 3.2 collective-permute-done.6
  343.3 4.8 %collective-permute-done.7 = bf16[288,256]{1,0:T(8,128)(2,1)S(1)} collective-permute-done((bf16[288,256]{1,0:T(8,128)(2,1)S(1)}, bf16[288,256]{1,0:T(8,128)(2,1)S(1)}, u32[]{:S(2)}, u32[]{:S(2)}) %collective-permute-start.7) | collective-permute-done | bytes 147488 | tf_op jit(solution)/shard_map/ppermute | solution.py:319
  350.1 4.8 %collective-permute-done.16.refs_6_ = bf16[4,288,256]{2,1,0:T(8,128)(2,1)S(1)} collective-permute-done((bf16[4,288,256]{2,1,0:T(8,128)(2,1)S(1)}, bf16[4,288,256]{2,1,0:T(8,128)(2,1)S(1)}, u32[]{:S(2)}, u32[]{:S(2)}) %collective-permute-start.16) | collective-permute-done | bytes 589856 | tf_op jit(solution)/shard_map/ppermute | solution.py:323
  354.9 10.5 %collective-permute-done.10.refs_2_ = bf16[4,288,256]{2,1,0:T(8,128)(2,1)S(1)} collective-permute-done((bf16[4,288,256]{2,1,0:T(8,128)(2,1)S(1)}, bf16[4,288,256]{2,1,0:T(8,128)(2,1)S(1)}, u32[]{:S(2)}, u32[]{:S(2)}) %collective-permute-start.10) | collective-permute-done | bytes 589856 | tf_op jit(solution)/shard_map/ppermute | solution.py:323
  367.5 2.4 place.1
  (121 shorter events, 44.9 us)
Async XLA Ops:
  6.5 88.5 %all-gather.13.cloned.1.call-start = ((), (), s32[]{:S(2)}) async-start(), calls=%async_computation.2 | async-start | bytes 11280384 | tf_op jit(solution)/shard_map/all_gather | solution.py:213
  9.4 177.7 %all-gather.11.cloned.1.call-start = ((), (), s32[]{:S(2)}) async-start(), calls=%async_computation.1 | async-start | bytes 16920576 | tf_op jit(solution)/shard_map/all_gather | solution.py:213
  15.7 232.7 %all-gather.15.cloned.1.call-start = ((), (), s32[]{:S(2)}) async-start(), calls=%async_computation.3 | async-start | bytes 11280384 | tf_op jit(solution)/shard_map/all_gather | solution.py:213
  17.8 292.1 %all-gather.17.cloned.1.call-start = ((), (), s32[]{:S(2)}) async-start(), calls=%async_computation.4 | async-start | bytes 11280384 | tf_op jit(solution)/shard_map/all_gather | solution.py:213
  18.9 9.5 %copy-start.5 = (f32[2,4,72]{2,1,0:T(4,128)S(1)}, f32[2,4,72]{2,1,0:T(4,128)}, u32[]{:S(2)}) copy-start(f32[2,4,72]{2,1,0:T(4,128)} %param.23) | copy-start | bytes 6916
  21.3 47.8 %all-to-all-start = ((bf16[8,288,256]{2,1,0:T(8,128)(2,1)}), bf16[8,288,256]{2,1,0:T(8,128)(2,1)S(1)}, u32[]{:S(2)}, u32[]{:S(2)}) async-start(bf16[8,288,256]{2,1,0:T(8,128)(2,1)} %dynamic-slice_bitcast_fusion), calls=%async_computation | async-start | bytes 2359296 | tf_op jit(solution)/shard_map/all_to_all | solution.py:229
  100.3 60.8 %collective-permute-start.2 = (bf16[2,4,144,1152]{3,2,1,0:T(8,128)(2,1)}, bf16[2,4,144,1152]{3,2,1,0:T(8,128)(2,1)}, u32[]{:S(2)}, u32[]{:S(2)}) collective-permute-start(bf16[2,4,144,1152]{3,2,1,0:T(8,128)(2,1)} %get-tuple-element.19), channel_id=1, source_target_pairs={{0,16},{16,0},{1,17},{17,1},{2,18},{18,2},{3,19},{19,3},{4,20},{20... | collective-permute-start | bytes 7962632 | tf_op jit(solution)/shard_map/ppermute | solution.py:239
  127.0 90.2 %collective-permute-start.1 = (bf16[2,4,144,1152]{3,2,1,0:T(8,128)(2,1)}, bf16[2,4,144,1152]{3,2,1,0:T(8,128)(2,1)}, u32[]{:S(2)}, u32[]{:S(2)}) collective-permute-start(bf16[2,4,144,1152]{3,2,1,0:T(8,128)(2,1)} %get-tuple-element.16), channel_id=1, source_target_pairs={{0,16},{16,0},{1,17},{17,1},{2,18},{18,2},{3,19},{19,3},{4,20},{20... | collective-permute-start | bytes 7962632 | tf_op jit(solution)/shard_map/ppermute | solution.py:239
  161.1 60.5 %collective-permute-start.3 = (bf16[2,4,144,1152]{3,2,1,0:T(8,128)(2,1)}, bf16[2,4,144,1152]{3,2,1,0:T(8,128)(2,1)}, u32[]{:S(2)}, u32[]{:S(2)}) collective-permute-start(bf16[2,4,144,1152]{3,2,1,0:T(8,128)(2,1)} %collective-permute-done.2.refs_6_), channel_id=1, source_target_pairs={{0,1},{1,0},{2,3},{3,2},{4,5},{5,4},{6,7},{7,6},{8,9},{9,8},{10,11... | collective-permute-start | bytes 7962632 | tf_op jit(solution)/shard_map/ppermute | solution.py:242
  217.2 6.0 %collective-permute-start.4 = (bf16[2,4,144,1152]{3,2,1,0:T(8,128)(2,1)}, bf16[2,4,144,1152]{3,2,1,0:T(8,128)(2,1)}, u32[]{:S(2)}, u32[]{:S(2)}) collective-permute-start(bf16[2,4,144,1152]{3,2,1,0:T(8,128)(2,1)} %collective-permute-done.1.refs_9_), channel_id=1, source_target_pairs={{0,1},{1,0},{2,3},{3,2},{4,5},{5,4},{6,7},{7,6},{8,9},{9,8},{10,11... | collective-permute-start | bytes 7962632 | tf_op jit(solution)/shard_map/ppermute | solution.py:242
  220.0 60.2 %collective-permute-start = (bf16[2,4,144,1152]{3,2,1,0:T(8,128)(2,1)S(1)}, bf16[2,4,144,1152]{3,2,1,0:T(8,128)(2,1)}, u32[]{:S(2)}, u32[]{:S(2)}) collective-permute-start(bf16[2,4,144,1152]{3,2,1,0:T(8,128)(2,1)S(1)} %constant_dynamic-slice_fusion.4), channel_id=1, source_target_pairs={{0,16},{16,0},{1,17},{17,1},{2,18},{18,2},{3,19},{19,3},{4,20},{20... | collective-permute-start | bytes 7962632 | tf_op jit(solution)/shard_map/ppermute | solution.py:239
  280.2 5.7 %collective-permute-start.5 = (bf16[2,4,144,1152]{3,2,1,0:T(8,128)(2,1)}, bf16[2,4,144,1152]{3,2,1,0:T(8,128)(2,1)S(1)}, u32[]{:S(2)}, u32[]{:S(2)}) collective-permute-start(bf16[2,4,144,1152]{3,2,1,0:T(8,128)(2,1)} %collective-permute-done.refs_5_), channel_id=1, source_target_pairs={{0,1},{1,0},{2,3},{3,2},{4,5},{5,4},{6,7},{7,6},{8,9},{9,8},{10,11... | collective-permute-start | bytes 7962632 | tf_op jit(solution)/shard_map/ppermute | solution.py:242
  319.6 16.3 %collective-permute-start.12 = (bf16[288,256]{1,0:T(8,128)(2,1)S(1)}, bf16[288,256]{1,0:T(8,128)(2,1)S(1)}, u32[]{:S(2)}, u32[]{:S(2)}) collective-permute-start(bf16[288,256]{1,0:T(8,128)(2,1)S(1)} %get-tuple-element.36), channel_id=1, source_target_pairs={{0,4},{4,8},{8,12},{12,0},{1,5},{5,9},{9,13},{13,1},{2,6},{6,10},{... | collective-permute-start | bytes 442376 | tf_op jit(solution)/shard_map/ppermute | solution.py:319
  321.1 17.5 %collective-permute-start.13 = (bf16[288,256]{1,0:T(8,128)(2,1)S(1)}, bf16[288,256]{1,0:T(8,128)(2,1)S(1)}, u32[]{:S(2)}, u32[]{:S(2)}) collective-permute-start(bf16[288,256]{1,0:T(8,128)(2,1)S(1)} %get-tuple-element.35), channel_id=1, source_target_pairs={{0,8},{4,12},{8,0},{12,4},{1,9},{5,13},{9,1},{13,5},{2,10},{6,14},... | collective-permute-start | bytes 442376 | tf_op jit(solution)/shard_map/ppermute | solution.py:319
  323.5 15.1 %collective-permute-start.14 = (bf16[288,256]{1,0:T(8,128)(2,1)S(1)}, bf16[288,256]{1,0:T(8,128)(2,1)S(1)}, u32[]{:S(2)}, u32[]{:S(2)}) collective-permute-start(bf16[288,256]{1,0:T(8,128)(2,1)S(1)} %get-tuple-element.34), channel_id=1, source_target_pairs={{0,12},{4,0},{8,4},{12,8},{1,13},{5,1},{9,5},{13,9},{2,14},{6,2},{... | collective-permute-start | bytes 442376 | tf_op jit(solution)/shard_map/ppermute | solution.py:319
  334.7 8.6 %collective-permute-start.6 = (bf16[288,256]{1,0:T(8,128)(2,1)S(1)}, bf16[288,256]{1,0:T(8,128)(2,1)S(1)}, u32[]{:S(2)}, u32[]{:S(2)}) collective-permute-start(bf16[288,256]{1,0:T(8,128)(2,1)S(1)} %get-tuple-element.40), channel_id=1, source_target_pairs={{0,4},{4,8},{8,12},{12,0},{1,5},{5,9},{9,13},{13,1},{2,6},{6,10},{... | collective-permute-start | bytes 442376 | tf_op jit(solution)/shard_map/ppermute | solution.py:319
  335.3 12.8 %collective-permute-start.7 = (bf16[288,256]{1,0:T(8,128)(2,1)S(1)}, bf16[288,256]{1,0:T(8,128)(2,1)S(1)}, u32[]{:S(2)}, u32[]{:S(2)}) collective-permute-start(bf16[288,256]{1,0:T(8,128)(2,1)S(1)} %get-tuple-element.39), channel_id=1, source_target_pairs={{0,8},{4,12},{8,0},{12,4},{1,9},{5,13},{9,1},{13,5},{2,10},{6,14},... | collective-permute-start | bytes 442376 | tf_op jit(solution)/shard_map/ppermute | solution.py:319
  335.9 12.3 %collective-permute-start.8 = (bf16[288,256]{1,0:T(8,128)(2,1)S(1)}, bf16[288,256]{1,0:T(8,128)(2,1)S(1)}, u32[]{:S(2)}, u32[]{:S(2)}) collective-permute-start(bf16[288,256]{1,0:T(8,128)(2,1)S(1)} %get-tuple-element.38), channel_id=1, source_target_pairs={{0,12},{4,0},{8,4},{12,8},{1,13},{5,1},{9,5},{13,9},{2,14},{6,2},{... | collective-permute-start | bytes 442376 | tf_op jit(solution)/shard_map/ppermute | solution.py:319
  338.7 16.3 %collective-permute-start.16 = (bf16[4,288,256]{2,1,0:T(8,128)(2,1)S(1)}, bf16[4,288,256]{2,1,0:T(8,128)(2,1)S(1)}, u32[]{:S(2)}, u32[]{:S(2)}) collective-permute-start(bf16[4,288,256]{2,1,0:T(8,128)(2,1)S(1)} %pad_maximum_fusion.3.refs_4_), channel_id=1, source_target_pairs={{0,2},{1,3},{2,0},{3,1},{4,6},{5,7},{6,4},{7,5},{8,10},{9,11},{10,... | collective-permute-start | bytes 1769480 | tf_op jit(solution)/shard_map/ppermute | solution.py:323
  348.2 17.2 %collective-permute-start.10 = (bf16[4,288,256]{2,1,0:T(8,128)(2,1)S(1)}, bf16[4,288,256]{2,1,0:T(8,128)(2,1)S(1)}, u32[]{:S(2)}, u32[]{:S(2)}) collective-permute-start(bf16[4,288,256]{2,1,0:T(8,128)(2,1)S(1)} %pad_maximum_fusion.2.refs_0_), channel_id=1, source_target_pairs={{0,2},{1,3},{2,0},{3,1},{4,6},{5,7},{6,4},{7,5},{8,10},{9,11},{10,... | collective-permute-start | bytes 1769480 | tf_op jit(solution)/shard_map/ppermute | solution.py:323
  349.6 15.8 %collective-permute-start.15 = (bf16[4,288,256]{2,1,0:T(8,128)(2,1)S(1)}, bf16[4,288,256]{2,1,0:T(8,128)(2,1)S(1)}, u32[]{:S(2)}, u32[]{:S(2)}) collective-permute-start(bf16[4,288,256]{2,1,0:T(8,128)(2,1)S(1)} %pad_maximum_fusion.3.refs_4_), channel_id=1, source_target_pairs={{0,1},{1,0},{2,3},{3,2},{4,5},{5,4},{6,7},{7,6},{8,9},{9,8},{10,11... | collective-permute-start | bytes 1769480 | tf_op jit(solution)/shard_map/ppermute | solution.py:323
  349.6 15.8 %collective-permute-start.9 = (bf16[4,288,256]{2,1,0:T(8,128)(2,1)S(1)}, bf16[4,288,256]{2,1,0:T(8,128)(2,1)S(1)}, u32[]{:S(2)}, u32[]{:S(2)}) collective-permute-start(bf16[4,288,256]{2,1,0:T(8,128)(2,1)S(1)} %pad_maximum_fusion.2.refs_0_), channel_id=1, source_target_pairs={{0,1},{1,0},{2,3},{3,2},{4,5},{5,4},{6,7},{7,6},{8,9},{9,8},{10,11... | collective-permute-start | bytes 1769480 | tf_op jit(solution)/shard_map/ppermute | solution.py:323
  354.9 10.5 %collective-permute-start.17 = (bf16[4,288,256]{2,1,0:T(8,128)(2,1)S(1)}, bf16[4,288,256]{2,1,0:T(8,128)(2,1)S(1)}, u32[]{:S(2)}, u32[]{:S(2)}) collective-permute-start(bf16[4,288,256]{2,1,0:T(8,128)(2,1)S(1)} %collective-permute-done.16.refs_6_), channel_id=1, source_target_pairs={{0,1},{1,0},{2,3},{3,2},{4,5},{5,4},{6,7},{7,6},{8,9},{9,8},{10,11... | collective-permute-start | bytes 1769480 | tf_op jit(solution)/shard_map/ppermute | solution.py:323
  365.4 2.0 collective-permute-start.11
  (12 other events, 78.7 us)
Sparse Core Ops, SparseCore 0:
  9.5 85.4 all-gather.12
  96.6 90.4 all-gather.10
  188.7 59.6 all-gather.14
  249.9 59.9 all-gather.16

commit v5 on v4

--- a/solution.py
+++ b/solution.py
@@ -89,15 +89,19 @@
 def half_loads(offsets, srcs, bufs, sems):
     plane = lax.axis_index("dp")
     core = lax.rem(lax.axis_index("ty"), 2)
+    per = len(srcs) // len(bufs)
 
     def loads(i, slot):
         copies = []
         for w, buf in enumerate(bufs):
-            own, same, other = srcs[3 * w:3 * w + 3]
-            pair = same.shape[0]
-            parts = [(own.at[:, i, pl.ds(offsets[w], buf.shape[3])], buf.at[slot, :, plane]),
-                     (same.at[:, i], buf.at[slot, pl.ds(core * pair, pair), 1 - plane]),
-                     (other.at[:, i], buf.at[slot, pl.ds((1 - core) * pair, pair), 1 - plane])]
+            own, same, other, *rest = srcs[per * w:per * (w + 1)]
+            pair, size = same.shape[0], same.shape[2]
+            mine = pl.ds(pl.multiple_of(plane * size, 16), size)
+            theirs = pl.ds(pl.multiple_of((1 - plane) * size, 16), size)
+            parts = [(own.at[:, i, pl.ds(offsets[w], size)], buf.at[slot, :, mine]),
+                     (same.at[:, i], buf.at[slot, pl.ds(core * pair, pair), theirs]),
+                     (other.at[:, i], buf.at[slot, pl.ds((1 - core) * pair, pair), theirs])]
+            parts += [(r.at[:, i], buf.at[slot, :, pl.ds(2 * size, r.shape[2])]) for r in rest]
             copies += [pltpu.make_async_copy(src, dst, sems.at[slot, w, j]) for j, (src, dst) in enumerate(parts)]
         return copies
 
@@ -134,17 +138,16 @@
     out_ref[0] = jax.nn.gelu(dot_nn(h_ref[...], up) + bias_ref[0], approximate=True).astype(BF)
 
 
-def down_kernel(order, x_ref, bd_ref, u_ref, down_ref, out_ref, acc_ref):
-    step = pl.program_id(0)
+def down_kernel(order, offsets, x_ref, bd_ref, u_ref, d0, d1, d2, d3, out_ref, acc_ref, down_buf, sems):
     width = x_ref.shape[-1]
 
-    @pl.when(step == 0)
-    def _():
+    def first():
         acc_ref[...] = x_ref[...].astype(F32) + bd_ref[...]
 
-    acc_ref[...] += dot_nt(u_ref[0], down_ref[...].reshape(width, down_ref.shape[-1]))
-
-    @pl.when(step == pl.num_programs(0) - 1)
+    slot = load_ahead(half_loads(offsets, (d0, d1, d2, d3), (down_buf,), sems), first)
+    acc_ref[...] += dot_nt(u_ref[0], down_buf[slot].reshape(width, down_buf.shape[-1]))
+
+    @pl.when(pl.program_id(0) == pl.num_programs(0) - 1)
     def _():
         wl = out_ref.shape[1]
         y_t = acc_ref[...].T.astype(BF)
@@ -213,40 +216,44 @@
             full = lax.all_gather(block, ("tx", "ty"), axis=0, axis_index_groups=groups)
             return full.reshape(tx, ty, *block.shape)
 
-        halves = [("u", 0), ("d", 0), ("u", 1)]
+        halves = [("u", 0), ("d", 0), ("u", 1), ("d", 1)]
+        few = wl // 72 * 16
 
         def half_block(block):
             return lax.dynamic_slice_in_dim(block, plane * half, half, axis=0)
 
         first = gather(jnp.concatenate([half_block(up_block(0)), half_block(down_block(0))], axis=0))
-        second = gather(jnp.concatenate([proj_block(0), half_block(up_block(1))], axis=0))
+        last = down_block(1)
+        few_rows = lax.dynamic_slice_in_dim(last, plane * few, few, axis=0)
+        second = gather(jnp.concatenate([proj_block(0), half_block(up_block(1)), few_rows], axis=0))
         third = gather(proj_block(1))
-        last_down = gather(down_block(1))
+        last_down = gather(last[2 * few:])
         proj = [second, third]
-        split = {("u", 0): (first, 0), ("d", 0): (first, half), ("u", 1): (second, wl)}
-
+        split = {("u", 0): (first, 0, half), ("d", 0): (first, half, half), ("u", 1): (second, wl, half), ("d", 1): (second, wl + half, few)}
+
+        swap = [(i, i ^ 1) for i in range(ty)]
+        got, crossed = {}, {}
+
+        def to_send(key):
+            full, at, size = split[key]
+            return lax.dynamic_slice(full, (core * (tx // 2), 0, at, 0), (tx // 2, ty, size, cols))
+
+        def cross_plane(key, sent):
+            got[key] = lax.ppermute(sent, "dp", [(0, 1), (1, 0)])
+
+        def cross_core(key):
+            crossed[key] = (got[key], lax.ppermute(got[key], "ty", swap))
+
+        sent = {key: to_send(key) for key in halves[:2]}
+        x_in, ln1_gain, sent = lax.optimization_barrier((x_in, ln1_gain, sent))
+        cross_plane(halves[0], sent[halves[0]])
+        cross_plane(halves[1], sent[halves[1]])
         images = lax.dynamic_slice_in_dim(x_in.transpose(0, 2, 1), lax.axis_index("ty") * per, per, axis=0)
         x_t = lax.all_to_all(images, "tx", split_axis=0, concat_axis=0, tiled=True)
         x = blocks(x_t.reshape(tx, nb, wl, toks)).transpose(1, 3, 0, 2).reshape(n, width)
-        swap = [(i, i ^ 1) for i in range(ty)]
-        got, crossed = {}, {}
-
-        def to_send(key):
-            full, at = split[key]
-            return lax.dynamic_slice(full, (core * (tx // 2), 0, at, 0), (tx // 2, ty, half, cols))
-
-        def cross_plane(key, sent):
-            got[key] = lax.ppermute(sent, "dp", [(0, 1), (1, 0)])
-
-        def cross_core(key):
-            crossed[key] = (got[key], lax.ppermute(got[key], "ty", swap))
-
-        first, x = lax.optimization_barrier((first, x))
-        split["u", 0] = (first, 0)
         on_tx = [ln1_gain, ln1_bias, ln2_gain, ln2_bias, b_o, b_down]
         on_ty = [b_q.reshape(layers, hd), b_v.reshape(layers, hd), b_up]
         own = jnp.concatenate([a.reshape(1, -1) for a in on_tx + on_ty], axis=1)
-        own, sent = lax.optimization_barrier((own, to_send(halves[0])))
         vec = lax.all_gather(own, ("tx", "ty"), axis=0)
         vec = blocks(vec.reshape(tx, ty, -1))
         at = len(on_tx) * layers * wl
@@ -259,10 +266,8 @@
         bias_a = jnp.concatenate([vq, gap, vv, gap, tail], axis=2).transpose(1, 0, 2).reshape(layers, ty, 1, cols)
         bias_u = jnp.pad(vu, ((0, 0), (0, 0), (0, cols - fl))).transpose(1, 0, 2).reshape(layers, ty, 1, cols)
 
-        cross_plane(halves[0], sent)
-        for key in halves[1:]:
-            sent, vec = lax.optimization_barrier((to_send(key), vec))
-            cross_plane(key, sent)
+        for key in halves[2:]:
+            cross_plane(key, to_send(key))
         cross_core(halves[0])
 
         whole = pl.BlockSpec((n, width), lambda i: (0, 0))
@@ -273,7 +278,7 @@
 
         anywhere = pl.BlockSpec(memory_space=pl.ANY)
         rows_bf, _ = scratch
-        half_buf = pltpu.VMEM((2, tx, 2, half, cols), BF)
+        half_buf = pltpu.VMEM((2, tx, wl, cols), BF)
         act = jax.ShapeDtypeStruct((n, width), BF)
         dot_flops = 2 * n * width * cols * ty
 
@@ -301,15 +306,19 @@
                 u = kernel(lambda *refs, o=(split["u", l][1],): up_kernel(o, *refs), [whole, row, row, bias] + [anywhere] * 3, hidden,
                            jax.ShapeDtypeStruct((ty, n, cols), BF), [rows_bf, half_buf, pltpu.SemaphoreType.DMA((2, 1, 3))],
                            2 * dot_flops)(x, vt[2, l], vt[3, l], bias_u[l], *up)
+                got["d", l], u = lax.optimization_barrier((got["d", l], u))
+                cross_core(("d", l))
+                down = (split["d", l][0], *crossed["d", l], last_down)
                 outs = []
                 for img in range(nb):
-                    outs.append(kernel(lambda *refs: down_kernel(order, *refs),
+                    outs.append(kernel(lambda *refs, o=(split["d", l][1],): down_kernel(order, o, *refs),
                                        [pl.BlockSpec((toks, width), lambda i, m=img: (m, 0)), row,
                                         pl.BlockSpec((1, toks, cols), lambda i, m=img: (i, m, 0)),
-                                        pl.BlockSpec((tx, 1, wl, cols), lambda i: (0, i, 0, 0))],
+                                        *[anywhere] * 4],
                                        pl.BlockSpec((tx, wl, toks), lambda i: (0, 0, 0)),
-                                       jax.ShapeDtypeStruct((tx, wl, toks), BF), [pltpu.VMEM((toks, width), F32)],
-                                       2 * dot_flops // nb)(x, vt[5, l], u, last_down))
+                                       jax.ShapeDtypeStruct((tx, wl, toks), BF),
+                                       [pltpu.VMEM((toks, width), F32), half_buf, pltpu.SemaphoreType.DMA((2, 1, 4))],
+                                       2 * dot_flops // nb)(x, vt[5, l], u, *down))
         me = lax.axis_index("tx")
         pieces = []
         for y_i in outs:

time: 377 us -> 384 us (1.019)
  blocking collectives: 24.5 us -> 57 us
  waiting for transfers between devices: 189 us -> 157 us
  starting transfers between devices: 22.5 us -> 27.1 us
    all_gather x4, waiting for transfers between devices: 65.7 us -> 115 us  [gather(): full = lax.all_gather(block, ('tx', 'ty'), axis=0, axis_index_groups=groups)]
    all_to_all x1, waiting for transfers between devices: 40.6 us -> 0.01 us  [local_fn(): x_t = lax.all_to_all(images, 'tx', split_axis=0, concat_axis=0, tiled=True)]
    ppermute x3 -> x4, waiting for transfers between devices: 50.1 us -> 11.6 us  [cross_plane(): got[key] = lax.ppermute(sent, 'dp', [(0, 1), (1, 0)])]
    all_gather x1, blocking collectives: 24.5 us -> 57 us  [local_fn(): vec = lax.all_gather(own, ('tx', 'ty'), axis=0)]
    dynamic_slice x2 -> x4, local copies, waits for them, and re-layouts: 7.26 us -> 8.72 us  [the longest x3 8.7 us: to_send(): lax.dynamic_slice(full, (core * (tx // 2), 0, at, 0), (tx // 2, ty, size,...]
  transfers between devices with their start and end apart: 23 -> 25, of which waited for: 15 -> 12; matrix products, arithmetic and copies ran while one was open for 7% -> 7% of each run, Pallas kernels for 22% -> 22%
where the time goes in v5:
time: 384 us; the launch traced here: 383 us
  waiting for transfers between devices  157 us (41%)
  Pallas kernels  95.9 us (25%)
  blocking collectives  57 us (15%)
  local copies, waits for them, and re-layouts  31.1 us (8%)
  starting transfers between devices  27.1 us (7%)
  between operations  13.6 us (4%)
    all_gather x4, waiting for transfers between devices, gather(): full = lax.all_gather(block, ('tx', 'ty'), axis=0, axis_index_groups=groups)  115 us
    all_gather x1, blocking collectives, local_fn(): vec = lax.all_gather(own, ('tx', 'ty'), axis=0)  57 us
    pallas_call x2, Pallas kernels, local_fn(): kernel(lambda *refs: attention_kernel(hl, dim, toks, *refs), [whole, row,...  42.2 us
    pallas_call x1, Pallas kernels, local_fn(): kernel(lambda *refs, o=offsets: mlp_kernel(o, *refs), [whole, row, row, b...  20 us
    pallas_call x2, Pallas kernels, local_fn(): kernel(lambda *refs, o=(split['d', l][1],): down_kernel(order, o, *refs),...  19 us
    ppermute x6, waiting for transfers between devices, local_fn(): lax.ppermute(by_group[dist - bit], 'ty', [(i, i ^ bit) for i in range(ty)])  16.9 us
    pallas_call x1, Pallas kernels, local_fn(): kernel(lambda *refs, o=(split['u', l][1],): up_kernel(o, *refs), [whole,...  12.2 us
    ppermute x4, waiting for transfers between devices, cross_plane(): got[key] = lax.ppermute(sent, 'dp', [(0, 1), (1, 0)])  11.6 us
  transfers between devices with their start and end apart: 25, of which 12 were waited for; matrix products, arithmetic and copies ran while one was open for 7% of the time, Pallas kernels for 22%

profile of v5, /device:TPU:0, one launch (start us, length us, event | category | flops | bytes accessed | tf_op | source)
XLA Modules:
  0.0 383.5 jit_solution(13149664692275301117)
XLA Ops:
  18.4 53.9 %all-gather.13.cloned.1.call-done = bf16[4608,1152]{1,0:T(8,128)(2,1)} async-done(((bf16[288,1152]{1,0:T(8,128)(2,1)}), bf16[4608,1152]{1,0:T(8,128)(2,1)}) %all-gather.13.cloned.1.call-update) | async-done | bytes 10616848 | tf_op jit(solution)/shard_map/all_gather | solution.py:216
  72.3 5.4 %constant_dynamic-slice_fusion.3 = (bf16[2,4,144,1152]{3,2,1,0:T(8,128)(2,1)}, bf16[2,4,144,1152]{3,2,1,0:T(8,128)(2,1)}) fusion(bf16[4,4,288,1152]{3,2,1,0:T(8,128)(2,1)} %bitcast.136, s32[]{:T(128)S(6)} %select_n.68), kind=kLoop, calls=%fused_computation.55 | loop fusion | bytes 10616836 | tf_op jit(solution)/shard_map/dynamic_slice | solution.py:239
  77.7 2.3 dynamic-slice_bitcast_fusion
  80.1 4.6 %all-to-all-start = ((bf16[8,288,256]{2,1,0:T(8,128)(2,1)}), bf16[8,288,256]{2,1,0:T(8,128)(2,1)S(1)}, u32[]{:S(2)}, u32[]{:S(2)}) async-start(bf16[8,288,256]{2,1,0:T(8,128)(2,1)} %dynamic-slice_bitcast_fusion), calls=%async_computation | async-start | bytes 2359296 | tf_op jit(solution)/shard_map/all_to_all | solution.py:252
  86.3 57.0 %all-gather.5 = f32[16,1,6760]{2,1,0:T(1,128)S(1)} all-gather(f32[1,1,6760]{2,1,0:T(1,128)S(1)} %bitcast.157), channel_id=4, replica_groups=mesh['dp'=2,'tx'=4,'ty'=4] {'tx','ty'}, dimensions={0}, use_global_device_ids=true | all-gather | bytes 459680 | tf_op jit(solution)/shard_map/all_gather | solution.py:257
  150.4 40.3 %all-gather.11.cloned.1.call-done = bf16[7936,1152]{1,0:T(8,128)(2,1)} async-done(((bf16[496,1152]{1,0:T(8,128)(2,1)}), bf16[7936,1152]{1,0:T(8,128)(2,1)}) %all-gather.11.cloned.1.call-update) | async-done | bytes 18284560 | tf_op jit(solution)/shard_map/all_gather | solution.py:216
  190.7 21.1 %shard_map.154.refs_0_ = bf16[512,1152]{1,0:T(8,128)(2,1)} custom-call(bf16[512,1152]{1,0:T(8,128)(2,1)} %reshape.123.refs_0_, f32[1,1152]{1,0:T(1,128)} %get-tuple-element.68.refs_1_, f32[1,1152]{1,0:T(1,128)} %get-tuple-element.67.refs_2_, f32[4,1,1152]{2,1,0:T(1,128)} %get-tuple-element.72.refs_3_, f32[1,1152]{1,0:T(1,128)} %get-tuple-element.66.refs_4_, ...), custom_call_target="tpu_custom_call" | custom-call | flops 21743271936 | bytes 21233664 | tf_op jit(solution)/shard_map/pallas_call | solution.py:291
  217.6 20.0 %shard_map.155.refs_0_ = bf16[512,1152]{1,0:T(8,128)(2,1)} custom-call(bf16[512,1152]{1,0:T(8,128)(2,1)} %shard_map.154.refs_0_, f32[1,1152]{1,0:T(1,128)} %get-tuple-element.65.refs_1_, f32[1,1152]{1,0:T(1,128)} %get-tuple-element.64.refs_2_, f32[4,1,1152]{2,1,0:T(1,128)} %get-tuple-element.70.refs_3_, f32[1,1152]{1,0:T(1,128)} %get-tuple-element.63.refs_4_, ...), custom_call_target="tpu_custom_call" | custom-call | flops 21743271936 | bytes 21233664 | tf_op jit(solution)/shard_map/pallas_call | solution.py:301
  237.6 20.7 %all-gather.15.cloned.1.call-done = bf16[4608,1152]{1,0:T(8,128)(2,1)} async-done(((bf16[288,1152]{1,0:T(8,128)(2,1)}), bf16[4608,1152]{1,0:T(8,128)(2,1)}) %all-gather.15.cloned.1.call-update) | async-done | bytes 10616848 | tf_op jit(solution)/shard_map/all_gather | solution.py:216
  258.3 21.1 %shard_map.156.refs_0_ = bf16[512,1152]{1,0:T(8,128)(2,1)} custom-call(bf16[512,1152]{1,0:T(8,128)(2,1)} %shard_map.155.refs_0_, f32[1,1152]{1,0:T(1,128)} %get-tuple-element.62.refs_1_, f32[1,1152]{1,0:T(1,128)} %get-tuple-element.61.refs_2_, f32[4,1,1152]{2,1,0:T(1,128)} %get-tuple-element.71.refs_3_, f32[1,1152]{1,0:T(1,128)} %get-tuple-element.60.refs_4_, ...), custom_call_target="tpu_custom_call" | custom-call | flops 21743271936 | bytes 21233664 | tf_op jit(solution)/shard_map/pallas_call | solution.py:291
  282.6 2.8 collective-permute-done.6.refs_6_
  285.4 12.2 %shard_map.157.refs_2_ = bf16[4,512,1152]{2,1,0:T(8,128)(2,1)} custom-call(bf16[512,1152]{1,0:T(8,128)(2,1)} %shard_map.156.refs_0_, f32[1,1152]{1,0:T(1,128)} %get-tuple-element.58.refs_1_, f32[1,1152]{1,0:T(1,128)} %get-tuple-element.57.refs_2_, f32[4,1,1152]{2,1,0:T(1,128)} %get-tuple-element.69.refs_3_, bf16[4,4,496,1152]{3,2,1,0:T(8,128)(2,1)} %bitcast.131, ...), custom_call_target="tpu_custom_call" | custom-call | flops 10871635968 | bytes 21233664 | tf_op jit(solution)/shard_map/pallas_call | solution.py:306
  297.7 11.6 %collective-permute-done.5.refs_4_ = bf16[2,4,64,1152]{3,2,1,0:T(8,128)(2,1)S(1)} collective-permute-done((bf16[2,4,64,1152]{3,2,1,0:T(8,128)(2,1)S(1)}, bf16[2,4,64,1152]{3,2,1,0:T(8,128)(2,1)S(1)}, u32[]{:S(2)}, u32[]{:S(2)}) %collective-permute-start.5) | collective-permute-done | bytes 1179680 | tf_op jit(solution)/shard_map/ppermute | solution.py:242
  309.3 2.8 collective-permute-done.7.refs_5_
  313.2 9.5 %shard_map.159 = bf16[4,288,256]{2,1,0:T(8,128)(2,1)} custom-call(bf16[512,1152]{1,0:T(8,128)(2,1)} %shard_map.156.refs_0_, f32[1,1152]{1,0:T(1,128)} %get-tuple-element.59.refs_1_, bf16[4,512,1152]{2,1,0:T(8,128)(2,1)} %shard_map.157.refs_2_, bf16[4,4,496,1152]{3,2,1,0:T(8,128)(2,1)} %bitcast.132, bf16[2,4,64,1152]{3,2,1,0:T(8,128)(2,1)} %copy-done, ...), custom_call_target="tpu_custom_call" | custom-call | flops 5435817984 | bytes 21233664 | tf_op jit(solution)/shard_map/pallas_call | solution.py:314
  323.9 4.0 %collective-permute-start.14 = (bf16[288,256]{1,0:T(8,128)(2,1)S(1)}, bf16[288,256]{1,0:T(8,128)(2,1)S(1)}, u32[]{:S(2)}, u32[]{:S(2)}) collective-permute-start(bf16[288,256]{1,0:T(8,128)(2,1)S(1)} %get-tuple-element.40), channel_id=1, source_target_pairs={{0,4},{4,8},{8,12},{12,0},{1,5},{5,9},{9,13},{13,1},{2,6},{6,10},{... | collective-permute-start | bytes 442376 | tf_op jit(solution)/shard_map/ppermute | solution.py:328
  327.9 2.8 collective-permute-start.16
  330.7 9.5 %shard_map.158 = bf16[4,288,256]{2,1,0:T(8,128)(2,1)} custom-call(bf16[512,1152]{1,0:T(8,128)(2,1)} %shard_map.156.refs_0_, f32[1,1152]{1,0:T(1,128)} %get-tuple-element.59.refs_1_, bf16[4,512,1152]{2,1,0:T(8,128)(2,1)} %shard_map.157.refs_2_, bf16[4,4,496,1152]{3,2,1,0:T(8,128)(2,1)} %bitcast.133, bf16[2,4,64,1152]{3,2,1,0:T(8,128)(2,1)} %copy-done, ...), custom_call_target="tpu_custom_call" | custom-call | flops 5435817984 | bytes 21233664 | tf_op jit(solution)/shard_map/pallas_call | solution.py:314
  347.6 2.3 collective-permute-done.8
  349.9 4.7 %collective-permute-done.9 = bf16[288,256]{1,0:T(8,128)(2,1)S(1)} collective-permute-done((bf16[288,256]{1,0:T(8,128)(2,1)S(1)}, bf16[288,256]{1,0:T(8,128)(2,1)S(1)}, u32[]{:S(2)}, u32[]{:S(2)}) %collective-permute-start.9) | collective-permute-done | bytes 147488 | tf_op jit(solution)/shard_map/ppermute | solution.py:328
  354.7 2.3 collective-permute-start.12
  357.5 4.2 %collective-permute-done.18.refs_6_ = bf16[4,288,256]{2,1,0:T(8,128)(2,1)S(1)} collective-permute-done((bf16[4,288,256]{2,1,0:T(8,128)(2,1)S(1)}, bf16[4,288,256]{2,1,0:T(8,128)(2,1)S(1)}, u32[]{:S(2)}, u32[]{:S(2)}) %collective-permute-start.18) | collective-permute-done | bytes 589856 | tf_op jit(solution)/shard_map/ppermute | solution.py:332
  361.8 10.7 %collective-permute-done.12.refs_2_ = bf16[4,288,256]{2,1,0:T(8,128)(2,1)S(1)} collective-permute-done((bf16[4,288,256]{2,1,0:T(8,128)(2,1)S(1)}, bf16[4,288,256]{2,1,0:T(8,128)(2,1)S(1)}, u32[]{:S(2)}, u32[]{:S(2)}) %collective-permute-start.12) | collective-permute-done | bytes 589856 | tf_op jit(solution)/shard_map/ppermute | solution.py:332
  374.5 2.4 place.1
  (129 shorter events, 41.6 us)
Async XLA Ops:
  6.5 65.7 %all-gather.13.cloned.1.call-start = ((), (), s32[]{:S(2)}) async-start(), calls=%async_computation.2 | async-start | bytes 11280384 | tf_op jit(solution)/shard_map/all_gather | solution.py:216
  9.4 181.3 %all-gather.11.cloned.1.call-start = ((), (), s32[]{:S(2)}) async-start(), calls=%async_computation.1 | async-start | bytes 19427328 | tf_op jit(solution)/shard_map/all_gather | solution.py:216
  15.4 242.9 %all-gather.15.cloned.1.call-start = ((), (), s32[]{:S(2)}) async-start(), calls=%async_computation.3 | async-start | bytes 11280384 | tf_op jit(solution)/shard_map/all_gather | solution.py:216
  80.1 66.9 %all-to-all-start = ((bf16[8,288,256]{2,1,0:T(8,128)(2,1)}), bf16[8,288,256]{2,1,0:T(8,128)(2,1)S(1)}, u32[]{:S(2)}, u32[]{:S(2)}) async-start(bf16[8,288,256]{2,1,0:T(8,128)(2,1)} %dynamic-slice_bitcast_fusion), calls=%async_computation | async-start | bytes 2359296 | tf_op jit(solution)/shard_map/all_to_all | solution.py:252
  84.7 224.6 %all-gather.17.cloned.1.call-start = ((), (), s32[]{:S(2)}) async-start(), calls=%async_computation.4 | async-start | bytes 6266880 | tf_op jit(solution)/shard_map/all_gather | solution.py:216
  84.7 65.7 %collective-permute-start.2 = (bf16[2,4,144,1152]{3,2,1,0:T(8,128)(2,1)}, bf16[2,4,144,1152]{3,2,1,0:T(8,128)(2,1)}, u32[]{:S(2)}, u32[]{:S(2)}) collective-permute-start(bf16[2,4,144,1152]{3,2,1,0:T(8,128)(2,1)} %get-tuple-element.19), channel_id=1, source_target_pairs={{0,16},{16,0},{1,17},{17,1},{2,18},{18,2},{3,19},{19,3},{4,20},{20... | collective-permute-start | bytes 7962632 | tf_op jit(solution)/shard_map/ppermute | solution.py:242
  143.9 67.9 %collective-permute-start.1 = (bf16[2,4,144,1152]{3,2,1,0:T(8,128)(2,1)}, bf16[2,4,144,1152]{3,2,1,0:T(8,128)(2,1)}, u32[]{:S(2)}, u32[]{:S(2)}) collective-permute-start(bf16[2,4,144,1152]{3,2,1,0:T(8,128)(2,1)} %get-tuple-element.15), channel_id=1, source_target_pairs={{0,16},{16,0},{1,17},{17,1},{2,18},{18,2},{3,19},{19,3},{4,20},{20... | collective-permute-start | bytes 7962632 | tf_op jit(solution)/shard_map/ppermute | solution.py:242
  150.4 66.9 %collective-permute-start.3 = (bf16[2,4,144,1152]{3,2,1,0:T(8,128)(2,1)}, bf16[2,4,144,1152]{3,2,1,0:T(8,128)(2,1)}, u32[]{:S(2)}, u32[]{:S(2)}) collective-permute-start(bf16[2,4,144,1152]{3,2,1,0:T(8,128)(2,1)} %collective-permute-done.2.refs_6_), channel_id=1, source_target_pairs={{0,1},{1,0},{2,3},{3,2},{4,5},{5,4},{6,7},{7,6},{8,9},{9,8},{10,11... | collective-permute-start | bytes 7962632 | tf_op jit(solution)/shard_map/ppermute | solution.py:245
  211.8 5.8 %collective-permute-start.4 = (bf16[2,4,144,1152]{3,2,1,0:T(8,128)(2,1)}, bf16[2,4,144,1152]{3,2,1,0:T(8,128)(2,1)}, u32[]{:S(2)}, u32[]{:S(2)}) collective-permute-start(bf16[2,4,144,1152]{3,2,1,0:T(8,128)(2,1)} %collective-permute-done.1.refs_9_), channel_id=1, source_target_pairs={{0,1},{1,0},{2,3},{3,2},{4,5},{5,4},{6,7},{7,6},{8,9},{9,8},{10,11... | collective-permute-start | bytes 7962632 | tf_op jit(solution)/shard_map/ppermute | solution.py:245
  215.7 63.7 %collective-permute-start = (bf16[2,4,144,1152]{3,2,1,0:T(8,128)(2,1)S(1)}, bf16[2,4,144,1152]{3,2,1,0:T(8,128)(2,1)}, u32[]{:S(2)}, u32[]{:S(2)}) collective-permute-start(bf16[2,4,144,1152]{3,2,1,0:T(8,128)(2,1)S(1)} %constant_dynamic-slice_fusion.5), channel_id=1, source_target_pairs={{0,16},{16,0},{1,17},{17,1},{2,18},{18,2},{3,19},{19,3},{4,20},{20... | collective-permute-start | bytes 7962632 | tf_op jit(solution)/shard_map/ppermute | solution.py:242
  279.5 6.0 %collective-permute-start.6 = (bf16[2,4,144,1152]{3,2,1,0:T(8,128)(2,1)}, bf16[2,4,144,1152]{3,2,1,0:T(8,128)(2,1)}, u32[]{:S(2)}, u32[]{:S(2)}) collective-permute-start(bf16[2,4,144,1152]{3,2,1,0:T(8,128)(2,1)} %collective-permute-done.refs_5_), channel_id=1, source_target_pairs={{0,1},{1,0},{2,3},{3,2},{4,5},{5,4},{6,7},{7,6},{8,9},{9,8},{10,11... | collective-permute-start | bytes 7962632 | tf_op jit(solution)/shard_map/ppermute | solution.py:245
  281.1 28.2 %collective-permute-start.5 = (bf16[2,4,64,1152]{3,2,1,0:T(8,128)(2,1)S(1)}, bf16[2,4,64,1152]{3,2,1,0:T(8,128)(2,1)S(1)}, u32[]{:S(2)}, u32[]{:S(2)}) collective-permute-start(bf16[2,4,64,1152]{3,2,1,0:T(8,128)(2,1)S(1)} %constant_dynamic-slice_fusion.2), channel_id=1, source_target_pairs={{0,16},{16,0},{1,17},{17,1},{2,18},{18,2},{3,19},{19,3},{4,20},{20... | collective-permute-start | bytes 3538952 | tf_op jit(solution)/shard_map/ppermute | solution.py:242
  309.3 2.8 collective-permute-start.7
  323.9 19.7 %collective-permute-start.14 = (bf16[288,256]{1,0:T(8,128)(2,1)S(1)}, bf16[288,256]{1,0:T(8,128)(2,1)S(1)}, u32[]{:S(2)}, u32[]{:S(2)}) collective-permute-start(bf16[288,256]{1,0:T(8,128)(2,1)S(1)} %get-tuple-element.40), channel_id=1, source_target_pairs={{0,4},{4,8},{8,12},{12,0},{1,5},{5,9},{9,13},{13,1},{2,6},{6,10},{... | collective-permute-start | bytes 442376 | tf_op jit(solution)/shard_map/ppermute | solution.py:328
  327.9 17.3 %collective-permute-start.15 = (bf16[288,256]{1,0:T(8,128)(2,1)S(1)}, bf16[288,256]{1,0:T(8,128)(2,1)S(1)}, u32[]{:S(2)}, u32[]{:S(2)}) collective-permute-start(bf16[288,256]{1,0:T(8,128)(2,1)S(1)} %get-tuple-element.39), channel_id=1, source_target_pairs={{0,8},{4,12},{8,0},{12,4},{1,9},{5,13},{9,1},{13,5},{2,10},{6,14},... | collective-permute-start | bytes 442376 | tf_op jit(solution)/shard_map/ppermute | solution.py:328
  327.9 17.3 %collective-permute-start.16 = (bf16[288,256]{1,0:T(8,128)(2,1)S(1)}, bf16[288,256]{1,0:T(8,128)(2,1)S(1)}, u32[]{:S(2)}, u32[]{:S(2)}) collective-permute-start(bf16[288,256]{1,0:T(8,128)(2,1)S(1)} %get-tuple-element.38), channel_id=1, source_target_pairs={{0,12},{4,0},{8,4},{12,8},{1,13},{5,1},{9,5},{13,9},{2,14},{6,2},{... | collective-permute-start | bytes 442376 | tf_op jit(solution)/shard_map/ppermute | solution.py:328
  341.3 8.6 %collective-permute-start.8 = (bf16[288,256]{1,0:T(8,128)(2,1)S(1)}, bf16[288,256]{1,0:T(8,128)(2,1)S(1)}, u32[]{:S(2)}, u32[]{:S(2)}) collective-permute-start(bf16[288,256]{1,0:T(8,128)(2,1)S(1)} %get-tuple-element.44), channel_id=1, source_target_pairs={{0,4},{4,8},{8,12},{12,0},{1,5},{5,9},{9,13},{13,1},{2,6},{6,10},{... | collective-permute-start | bytes 442376 | tf_op jit(solution)/shard_map/ppermute | solution.py:328
  341.4 13.3 %collective-permute-start.9 = (bf16[288,256]{1,0:T(8,128)(2,1)S(1)}, bf16[288,256]{1,0:T(8,128)(2,1)S(1)}, u32[]{:S(2)}, u32[]{:S(2)}) collective-permute-start(bf16[288,256]{1,0:T(8,128)(2,1)S(1)} %get-tuple-element.43), channel_id=1, source_target_pairs={{0,8},{4,12},{8,0},{12,4},{1,9},{5,13},{9,1},{13,5},{2,10},{6,14},... | collective-permute-start | bytes 442376 | tf_op jit(solution)/shard_map/ppermute | solution.py:328
  343.5 11.1 %collective-permute-start.10 = (bf16[288,256]{1,0:T(8,128)(2,1)S(1)}, bf16[288,256]{1,0:T(8,128)(2,1)S(1)}, u32[]{:S(2)}, u32[]{:S(2)}) collective-permute-start(bf16[288,256]{1,0:T(8,128)(2,1)S(1)} %get-tuple-element.42), channel_id=1, source_target_pairs={{0,12},{4,0},{8,4},{12,8},{1,13},{5,1},{9,5},{13,9},{2,14},{6,2},{... | collective-permute-start | bytes 442376 | tf_op jit(solution)/shard_map/ppermute | solution.py:328
  345.3 16.5 %collective-permute-start.18 = (bf16[4,288,256]{2,1,0:T(8,128)(2,1)S(1)}, bf16[4,288,256]{2,1,0:T(8,128)(2,1)S(1)}, u32[]{:S(2)}, u32[]{:S(2)}) collective-permute-start(bf16[4,288,256]{2,1,0:T(8,128)(2,1)S(1)} %pad_maximum_fusion.3.refs_4_), channel_id=1, source_target_pairs={{0,2},{1,3},{2,0},{3,1},{4,6},{5,7},{6,4},{7,5},{8,10},{9,11},{10,... | collective-permute-start | bytes 1769480 | tf_op jit(solution)/shard_map/ppermute | solution.py:332
  354.7 17.8 %collective-permute-start.12 = (bf16[4,288,256]{2,1,0:T(8,128)(2,1)S(1)}, bf16[4,288,256]{2,1,0:T(8,128)(2,1)S(1)}, u32[]{:S(2)}, u32[]{:S(2)}) collective-permute-start(bf16[4,288,256]{2,1,0:T(8,128)(2,1)S(1)} %pad_maximum_fusion.2.refs_0_), channel_id=1, source_target_pairs={{0,2},{1,3},{2,0},{3,1},{4,6},{5,7},{6,4},{7,5},{8,10},{9,11},{10,... | collective-permute-start | bytes 1769480 | tf_op jit(solution)/shard_map/ppermute | solution.py:332
  357.0 15.4 %collective-permute-start.17 = (bf16[4,288,256]{2,1,0:T(8,128)(2,1)S(1)}, bf16[4,288,256]{2,1,0:T(8,128)(2,1)S(1)}, u32[]{:S(2)}, u32[]{:S(2)}) collective-permute-start(bf16[4,288,256]{2,1,0:T(8,128)(2,1)S(1)} %pad_maximum_fusion.3.refs_4_), channel_id=1, source_target_pairs={{0,1},{1,0},{2,3},{3,2},{4,5},{5,4},{6,7},{7,6},{8,9},{9,8},{10,11... | collective-permute-start | bytes 1769480 | tf_op jit(solution)/shard_map/ppermute | solution.py:332
  357.0 15.4 %collective-permute-start.11 = (bf16[4,288,256]{2,1,0:T(8,128)(2,1)S(1)}, bf16[4,288,256]{2,1,0:T(8,128)(2,1)S(1)}, u32[]{:S(2)}, u32[]{:S(2)}) collective-permute-start(bf16[4,288,256]{2,1,0:T(8,128)(2,1)S(1)} %pad_maximum_fusion.2.refs_0_), channel_id=1, source_target_pairs={{0,1},{1,0},{2,3},{3,2},{4,5},{5,4},{6,7},{7,6},{8,9},{9,8},{10,11... | collective-permute-start | bytes 1769480 | tf_op jit(solution)/shard_map/ppermute | solution.py:332
  361.8 10.7 %collective-permute-start.19 = (bf16[4,288,256]{2,1,0:T(8,128)(2,1)S(1)}, bf16[4,288,256]{2,1,0:T(8,128)(2,1)S(1)}, u32[]{:S(2)}, u32[]{:S(2)}) collective-permute-start(bf16[4,288,256]{2,1,0:T(8,128)(2,1)S(1)} %collective-permute-done.18.refs_6_), channel_id=1, source_target_pairs={{0,1},{1,0},{2,3},{3,2},{4,5},{5,4},{6,7},{7,6},{8,9},{9,8},{10,11... | collective-permute-start | bytes 1769480 | tf_op jit(solution)/shard_map/ppermute | solution.py:332
  (16 other events, 31.7 us)
Sparse Core Ops, SparseCore 0:
  9.5 62.7 all-gather.12
  73.9 116.8 all-gather.10
  192.3 65.9 all-gather.14
  259.8 38.5 all-gather.16

commit v6 on v5

--- a/solution.py
+++ b/solution.py
@@ -138,7 +138,8 @@
     out_ref[0] = jax.nn.gelu(dot_nn(h_ref[...], up) + bias_ref[0], approximate=True).astype(BF)
 
 
-def down_kernel(order, offsets, x_ref, bd_ref, u_ref, d0, d1, d2, d3, out_ref, acc_ref, down_buf, sems):
+def down_kernel(order, offsets, x_ref, bd_ref, u_ref, d0, d1, d2, d3, *rest):
+    *outs, acc_ref, down_buf, sems = rest
     width = x_ref.shape[-1]
 
     def first():
@@ -149,10 +150,11 @@
 
     @pl.when(pl.program_id(0) == pl.num_programs(0) - 1)
     def _():
-        wl = out_ref.shape[1]
         y_t = acc_ref[...].T.astype(BF)
-        for i, block in enumerate(order):
-            out_ref[block] = y_t[i * wl:(i + 1) * wl]
+        for img, out_ref in enumerate(outs):
+            _, wl, toks = out_ref.shape
+            for i, block in enumerate(order):
+                out_ref[block] = y_t[i * wl:(i + 1) * wl, img * toks:(img + 1) * toks]
 
 
 def place_kernel(tx, ty, per, nb, *refs):
@@ -277,7 +279,7 @@
         params = pltpu.CompilerParams(vmem_limit_bytes=VMEM_BYTES, dimension_semantics=("arbitrary",))
 
         anywhere = pl.BlockSpec(memory_space=pl.ANY)
-        rows_bf, _ = scratch
+        rows_bf, rows_f = scratch
         half_buf = pltpu.VMEM((2, tx, wl, cols), BF)
         act = jax.ShapeDtypeStruct((n, width), BF)
         dot_flops = 2 * n * width * cols * ty
@@ -288,10 +290,13 @@
                                   cost_estimate=pl.CostEstimate(flops=flops, bytes_accessed=width * cols * ty * 4, transcendentals=n * cols * ty))
 
         for l in range(layers):
+            if l:
+                got["u", l], x = lax.optimization_barrier((got["u", l], x))
+                cross_core(("u", l))
             x = kernel(lambda *refs: attention_kernel(hl, dim, toks, *refs),
                        [whole, row, row, bias, row, pl.BlockSpec((tx, 1, wl, cols), lambda i: (0, i, 0, 0))],
                        whole, act, scratch, 4 * dot_flops)(x, vt[0, l], vt[1, l], bias_a[l], vt[4, l], proj[l])
-            late = halves[l + 1]
+            late = halves[2 * l + 1]
             got[late], x = lax.optimization_barrier((got[late], x))
             cross_core(late)
             up = (split["u", l][0], *crossed["u", l])
@@ -306,19 +311,12 @@
                 u = kernel(lambda *refs, o=(split["u", l][1],): up_kernel(o, *refs), [whole, row, row, bias] + [anywhere] * 3, hidden,
                            jax.ShapeDtypeStruct((ty, n, cols), BF), [rows_bf, half_buf, pltpu.SemaphoreType.DMA((2, 1, 3))],
                            2 * dot_flops)(x, vt[2, l], vt[3, l], bias_u[l], *up)
-                got["d", l], u = lax.optimization_barrier((got["d", l], u))
-                cross_core(("d", l))
                 down = (split["d", l][0], *crossed["d", l], last_down)
-                outs = []
-                for img in range(nb):
-                    outs.append(kernel(lambda *refs, o=(split["d", l][1],): down_kernel(order, o, *refs),
-                                       [pl.BlockSpec((toks, width), lambda i, m=img: (m, 0)), row,
-                                        pl.BlockSpec((1, toks, cols), lambda i, m=img: (i, m, 0)),
-                                        *[anywhere] * 4],
-                                       pl.BlockSpec((tx, wl, toks), lambda i: (0, 0, 0)),
-                                       jax.ShapeDtypeStruct((tx, wl, toks), BF),
-                                       [pltpu.VMEM((toks, width), F32), half_buf, pltpu.SemaphoreType.DMA((2, 1, 4))],
-                                       2 * dot_flops // nb)(x, vt[5, l], u, *down))
+                outs = kernel(lambda *refs, o=(split["d", l][1],): down_kernel(order, o, *refs),
+                              [whole, row, hidden] + [anywhere] * 4,
+                              [pl.BlockSpec((tx, wl, toks), lambda i: (0, 0, 0))] * nb,
+                              [jax.ShapeDtypeStruct((tx, wl, toks), BF)] * nb,
+                              [rows_f, half_buf, pltpu.SemaphoreType.DMA((2, 1, 4))], 2 * dot_flops)(x, vt[5, l], u, *down)
         me = lax.axis_index("tx")
         pieces = []
         for y_i in outs:

time: 384 us -> 406 us (1.057); the launches traced: 383 us -> 399 us
  waiting for transfers between devices: 157 us -> 221 us
  blocking collectives: 57 us -> 24.4 us
  starting transfers between devices: 27.1 us -> 18.2 us
  Pallas kernels: 95.9 us -> 90 us
    ppermute x4, waiting for transfers between devices: 11.6 us -> 71.9 us  [cross_plane(): got[key] = lax.ppermute(sent, 'dp', [(0, 1), (1, 0)])]
    all_gather x4, waiting for transfers between devices: 115 us -> 74.3 us  [gather(): full = lax.all_gather(block, ('tx', 'ty'), axis=0, axis_index_groups=groups)]
    all_to_all x1, waiting for transfers between devices: 0.01 us -> 37.2 us  [local_fn(): x_t = lax.all_to_all(images, 'tx', split_axis=0, concat_axis=0, tiled=True)]
    all_gather x1, blocking collectives: 57 us -> 24.4 us  [local_fn(): vec = lax.all_gather(own, ('tx', 'ty'), axis=0)]
    ppermute x6, waiting for transfers between devices: 7.06 us -> 18.1 us  [local_fn(): lax.ppermute(part, 'tx', [(i, (i + k) % tx) for i in range(tx)])]
    pallas_call x2 -> x1, Pallas kernels: 19 us -> 12.7 us  [local_fn(): kernel(lambda *refs, o=(split['d', l][1],): down_kernel(order, o, *refs),...]
    ppermute x6, starting transfers between devices: 5.12 us -> 0.72 us  [local_fn(): lax.ppermute(by_group[dist - bit], 'ty', [(i, i ^ bit) for i in range(ty)])]
    ppermute x4, waiting for transfers between devices: 5.97 us -> 1.64 us  [cross_core(): crossed[key] = (got[key], lax.ppermute(got[key], 'ty', swap))]
  transfers between devices with their start and end apart: 25 -> 25, of which waited for: 12 -> 16; matrix products, arithmetic and copies ran while one was open for 7% -> 7% of each run, Pallas kernels for 22% -> 19%
where the time goes in v6:
time: 406 us; the launch traced here: 399 us
  waiting for transfers between devices  221 us (54%)
  Pallas kernels  90 us (22%)
  local copies, waits for them, and re-layouts  30.1 us (7%)
  blocking collectives  24.4 us (6%)
  starting transfers between devices  18.2 us (4%)
  between operations  13.6 us (3%)
    all_gather x4, waiting for transfers between devices, gather(): full = lax.all_gather(block, ('tx', 'ty'), axis=0, axis_index_groups=groups)  74.3 us
    ppermute x4, waiting for transfers between devices, cross_plane(): got[key] = lax.ppermute(sent, 'dp', [(0, 1), (1, 0)])  71.9 us
    pallas_call x2, Pallas kernels, local_fn(): kernel(lambda *refs: attention_kernel(hl, dim, toks, *refs), [whole, row,...  42.3 us
    all_to_all x1, waiting for transfers between devices, local_fn(): x_t = lax.all_to_all(images, 'tx', split_axis=0, concat_axis=0, tiled=True)  37.2 us
    all_gather x1, blocking collectives, local_fn(): vec = lax.all_gather(own, ('tx', 'ty'), axis=0)  24.4 us
    pallas_call x1, Pallas kernels, local_fn(): kernel(lambda *refs, o=offsets: mlp_kernel(o, *refs), [whole, row, row, b...  20 us
    ppermute x6, waiting for transfers between devices, local_fn(): lax.ppermute(part, 'tx', [(i, (i + k) % tx) for i in range(tx)])  18.1 us
    ppermute x6, waiting for transfers between devices, local_fn(): lax.ppermute(by_group[dist - bit], 'ty', [(i, i ^ bit) for i in range(ty)])  17.3 us
  transfers between devices with their start and end apart: 25, of which 16 were waited for; matrix products, arithmetic and copies ran while one was open for 7% of the time, Pallas kernels for 19%

profile of v6, /device:TPU:0, one launch (start us, length us, event | category | flops | bytes accessed | tf_op | source)
XLA Modules:
  0.0 399.2 jit_solution(10498809724761886801)
XLA Ops:
  19.3 53.0 %all-gather.13.cloned.1.call-done = bf16[4608,1152]{1,0:T(8,128)(2,1)} async-done(((bf16[288,1152]{1,0:T(8,128)(2,1)}), bf16[4608,1152]{1,0:T(8,128)(2,1)}) %all-gather.13.cloned.1.call-update) | async-done | bytes 10616848 | tf_op jit(solution)/shard_map/all_gather | solution.py:218
  72.3 5.4 %constant_dynamic-slice_fusion.2 = (bf16[2,4,144,1152]{3,2,1,0:T(8,128)(2,1)}, bf16[2,4,144,1152]{3,2,1,0:T(8,128)(2,1)}) fusion(bf16[4,4,288,1152]{3,2,1,0:T(8,128)(2,1)} %bitcast.128, s32[]{:T(128)S(6)} %select_n.68), kind=kLoop, calls=%fused_computation.54 | loop fusion | bytes 10616836 | tf_op jit(solution)/shard_map/dynamic_slice | solution.py:241
  77.9 24.4 %all-gather.5 = f32[16,1,6760]{2,1,0:T(1,128)S(1)} all-gather(f32[1,1,6760]{2,1,0:T(1,128)S(1)} %bitcast.154), channel_id=4, replica_groups=mesh['dp'=2,'tx'=4,'ty'=4] {'tx','ty'}, dimensions={0}, use_global_device_ids=true | all-gather | bytes 459680 | tf_op jit(solution)/shard_map/all_gather | solution.py:259
  102.3 2.4 dynamic-slice_bitcast_fusion
  104.7 3.7 all-to-all-start
  112.7 37.2 %all-to-all-done = bf16[8,288,256]{2,1,0:T(8,128)(2,1)S(1)} async-done(((bf16[8,288,256]{2,1,0:T(8,128)(2,1)}), bf16[8,288,256]{2,1,0:T(8,128)(2,1)S(1)}, u32[]{:S(2)}, u32[]{:S(2)}) %all-to-all-start) | async-done | bytes 1179680 | tf_op jit(solution)/shard_map/all_to_all | solution.py:254
  153.3 15.9 %collective-permute-done.3.refs_6_ = bf16[2,4,144,1152]{3,2,1,0:T(8,128)(2,1)} collective-permute-done((bf16[2,4,144,1152]{3,2,1,0:T(8,128)(2,1)}, bf16[2,4,144,1152]{3,2,1,0:T(8,128)(2,1)}, u32[]{:S(2)}, u32[]{:S(2)}) %collective-permute-start.3) | collective-permute-done | bytes 2654240 | tf_op jit(solution)/shard_map/ppermute | solution.py:244
  169.2 21.3 %all-gather.11.cloned.1.call-done = bf16[7936,1152]{1,0:T(8,128)(2,1)} async-done(((bf16[496,1152]{1,0:T(8,128)(2,1)}), bf16[7936,1152]{1,0:T(8,128)(2,1)}) %all-gather.11.cloned.1.call-update) | async-done | bytes 18284560 | tf_op jit(solution)/shard_map/all_gather | solution.py:218
  190.5 21.1 %shard_map.154.refs_0_ = bf16[512,1152]{1,0:T(8,128)(2,1)} custom-call(bf16[512,1152]{1,0:T(8,128)(2,1)} %reshape.123.refs_0_, f32[1,1152]{1,0:T(1,128)} %get-tuple-element.72.refs_1_, f32[1,1152]{1,0:T(1,128)} %get-tuple-element.71.refs_2_, f32[4,1,1152]{2,1,0:T(1,128)} %get-tuple-element.76.refs_3_, f32[1,1152]{1,0:T(1,128)} %get-tuple-element.70.refs_4_, ...), custom_call_target="tpu_custom_call" | custom-call | flops 21743271936 | bytes 21233664 | tf_op jit(solution)/shard_map/pallas_call | solution.py:296
  211.6 13.9 %collective-permute-done.2.refs_9_ = bf16[2,4,144,1152]{3,2,1,0:T(8,128)(2,1)} collective-permute-done((bf16[2,4,144,1152]{3,2,1,0:T(8,128)(2,1)}, bf16[2,4,144,1152]{3,2,1,0:T(8,128)(2,1)}, u32[]{:S(2)}, u32[]{:S(2)}) %collective-permute-start.2) | collective-permute-done | bytes 2654240 | tf_op jit(solution)/shard_map/ppermute | solution.py:244
  225.7 2.0 constant_dynamic-slice_fusion.4
  231.5 20.0 %shard_map.155.refs_0_ = bf16[512,1152]{1,0:T(8,128)(2,1)} custom-call(bf16[512,1152]{1,0:T(8,128)(2,1)} %shard_map.154.refs_0_, f32[1,1152]{1,0:T(1,128)} %get-tuple-element.69.refs_1_, f32[1,1152]{1,0:T(1,128)} %get-tuple-element.68.refs_2_, f32[4,1,1152]{2,1,0:T(1,128)} %get-tuple-element.74.refs_3_, f32[1,1152]{1,0:T(1,128)} %get-tuple-element.67.refs_4_, ...), custom_call_target="tpu_custom_call" | custom-call | flops 21743271936 | bytes 21233664 | tf_op jit(solution)/shard_map/pallas_call | solution.py:306
  251.5 36.4 %collective-permute-done.1.refs_5_ = bf16[2,4,144,1152]{3,2,1,0:T(8,128)(2,1)} collective-permute-done((bf16[2,4,144,1152]{3,2,1,0:T(8,128)(2,1)S(1)}, bf16[2,4,144,1152]{3,2,1,0:T(8,128)(2,1)}, u32[]{:S(2)}, u32[]{:S(2)}) %collective-permute-start.1) | collective-permute-done | bytes 2654240 | tf_op jit(solution)/shard_map/ppermute | solution.py:244
  290.8 21.2 %shard_map.156.refs_0_ = bf16[512,1152]{1,0:T(8,128)(2,1)} custom-call(bf16[512,1152]{1,0:T(8,128)(2,1)} %shard_map.155.refs_0_, f32[1,1152]{1,0:T(1,128)} %get-tuple-element.66.refs_1_, f32[1,1152]{1,0:T(1,128)} %get-tuple-element.65.refs_2_, f32[4,1,1152]{2,1,0:T(1,128)} %get-tuple-element.75.refs_3_, f32[1,1152]{1,0:T(1,128)} %get-tuple-element.64.refs_4_, ...), custom_call_target="tpu_custom_call" | custom-call | flops 21743271936 | bytes 21233664 | tf_op jit(solution)/shard_map/pallas_call | solution.py:296
  312.0 5.7 %collective-permute-done.refs_4_ = bf16[2,4,64,1152]{3,2,1,0:T(8,128)(2,1)S(1)} collective-permute-done((bf16[2,4,64,1152]{3,2,1,0:T(8,128)(2,1)S(1)}, bf16[2,4,64,1152]{3,2,1,0:T(8,128)(2,1)S(1)}, u32[]{:S(2)}, u32[]{:S(2)}) %collective-permute-start) | collective-permute-done | bytes 1179680 | tf_op jit(solution)/shard_map/ppermute | solution.py:244
  317.7 12.5 %shard_map.157.refs_2_ = bf16[4,512,1152]{2,1,0:T(8,128)(2,1)} custom-call(bf16[512,1152]{1,0:T(8,128)(2,1)} %shard_map.156.refs_0_, f32[1,1152]{1,0:T(1,128)} %get-tuple-element.62.refs_1_, f32[1,1152]{1,0:T(1,128)} %get-tuple-element.61.refs_2_, f32[4,1,1152]{2,1,0:T(1,128)} %get-tuple-element.73.refs_3_, bf16[4,4,496,1152]{3,2,1,0:T(8,128)(2,1)} %bitcast.144, ...), custom_call_target="tpu_custom_call" | custom-call | flops 10871635968 | bytes 21233664 | tf_op jit(solution)/shard_map/pallas_call | solution.py:311
  331.4 12.7 %shard_map.158 = (bf16[4,288,256]{2,1,0:T(8,128)(2,1)}, bf16[4,288,256]{2,1,0:T(8,128)(2,1)}) custom-call(bf16[512,1152]{1,0:T(8,128)(2,1)} %shard_map.156.refs_0_, f32[1,1152]{1,0:T(1,128)} %get-tuple-element.63.refs_1_, bf16[4,512,1152]{2,1,0:T(8,128)(2,1)} %shard_map.157.refs_2_, bf16[4,4,496,1152]{3,2,1,0:T(8,128)(2,1)} %bitcast.145, ...), custom_call_target="tpu_custom_call" | custom-call | flops 10871635968 | bytes 21233664 | tf_op jit(solution)/shard_map/pallas_call | solution.py:315
  346.9 2.3 collective-permute-start.15
  351.9 2.1 collective-permute-done.14
  355.9 4.5 %collective-permute-done.15 = bf16[288,256]{1,0:T(8,128)(2,1)S(1)} collective-permute-done((bf16[288,256]{1,0:T(8,128)(2,1)S(1)}, bf16[288,256]{1,0:T(8,128)(2,1)S(1)}, u32[]{:S(2)}, u32[]{:S(2)}) %collective-permute-start.15) | collective-permute-done | bytes 147488 | tf_op jit(solution)/shard_map/ppermute | solution.py:326
  363.5 8.6 %collective-permute-done.9 = bf16[288,256]{1,0:T(8,128)(2,1)S(1)} collective-permute-done((bf16[288,256]{1,0:T(8,128)(2,1)S(1)}, bf16[288,256]{1,0:T(8,128)(2,1)S(1)}, u32[]{:S(2)}, u32[]{:S(2)}) %collective-permute-start.9) | collective-permute-done | bytes 147488 | tf_op jit(solution)/shard_map/ppermute | solution.py:326
  372.9 3.5 collective-permute-done.18.refs_6_
  376.4 11.8 %collective-permute-done.12.refs_2_ = bf16[4,288,256]{2,1,0:T(8,128)(2,1)S(1)} collective-permute-done((bf16[4,288,256]{2,1,0:T(8,128)(2,1)S(1)}, bf16[4,288,256]{2,1,0:T(8,128)(2,1)S(1)}, u32[]{:S(2)}, u32[]{:S(2)}) %collective-permute-start.12) | collective-permute-done | bytes 589856 | tf_op jit(solution)/shard_map/ppermute | solution.py:330
  390.2 2.4 place.1
  (130 shorter events, 41.6 us)
Async XLA Ops:
  6.5 65.7 %all-gather.13.cloned.1.call-start = ((), (), s32[]{:S(2)}) async-start(), calls=%async_computation.2 | async-start | bytes 11280384 | tf_op jit(solution)/shard_map/all_gather | solution.py:218
  9.4 181.1 %all-gather.11.cloned.1.call-start = ((), (), s32[]{:S(2)}) async-start(), calls=%async_computation.1 | async-start | bytes 19427328 | tf_op jit(solution)/shard_map/all_gather | solution.py:218
  15.5 275.3 %all-gather.15.cloned.1.call-start = ((), (), s32[]{:S(2)}) async-start(), calls=%async_computation.3 | async-start | bytes 11280384 | tf_op jit(solution)/shard_map/all_gather | solution.py:218
  17.7 312.6 %all-gather.17.cloned.1.call-start = ((), (), s32[]{:S(2)}) async-start(), calls=%async_computation.4 | async-start | bytes 6266880 | tf_op jit(solution)/shard_map/all_gather | solution.py:218
  104.7 45.2 %all-to-all-start = ((bf16[8,288,256]{2,1,0:T(8,128)(2,1)}), bf16[8,288,256]{2,1,0:T(8,128)(2,1)S(1)}, u32[]{:S(2)}, u32[]{:S(2)}) async-start(bf16[8,288,256]{2,1,0:T(8,128)(2,1)} %dynamic-slice_bitcast_fusion), calls=%async_computation | async-start | bytes 2359296 | tf_op jit(solution)/shard_map/all_to_all | solution.py:254
  108.4 60.8 %collective-permute-start.3 = (bf16[2,4,144,1152]{3,2,1,0:T(8,128)(2,1)}, bf16[2,4,144,1152]{3,2,1,0:T(8,128)(2,1)}, u32[]{:S(2)}, u32[]{:S(2)}) collective-permute-start(bf16[2,4,144,1152]{3,2,1,0:T(8,128)(2,1)} %get-tuple-element.21), channel_id=1, source_target_pairs={{0,16},{16,0},{1,17},{17,1},{2,18},{18,2},{3,19},{19,3},{4,20},{20... | collective-permute-start | bytes 7962632 | tf_op jit(solution)/shard_map/ppermute | solution.py:244
  110.6 114.9 %collective-permute-start.2 = (bf16[2,4,144,1152]{3,2,1,0:T(8,128)(2,1)}, bf16[2,4,144,1152]{3,2,1,0:T(8,128)(2,1)}, u32[]{:S(2)}, u32[]{:S(2)}) collective-permute-start(bf16[2,4,144,1152]{3,2,1,0:T(8,128)(2,1)} %get-tuple-element.17), channel_id=1, source_target_pairs={{0,16},{16,0},{1,17},{17,1},{2,18},{18,2},{3,19},{19,3},{4,20},{20... | collective-permute-start | bytes 7962632 | tf_op jit(solution)/shard_map/ppermute | solution.py:244
  169.2 60.6 %collective-permute-start.4 = (bf16[2,4,144,1152]{3,2,1,0:T(8,128)(2,1)}, bf16[2,4,144,1152]{3,2,1,0:T(8,128)(2,1)}, u32[]{:S(2)}, u32[]{:S(2)}) collective-permute-start(bf16[2,4,144,1152]{3,2,1,0:T(8,128)(2,1)} %collective-permute-done.3.refs_6_), channel_id=1, source_target_pairs={{0,1},{1,0},{2,3},{3,2},{4,5},{5,4},{6,7},{7,6},{8,9},{9,8},{10,11... | collective-permute-start | bytes 7962632 | tf_op jit(solution)/shard_map/ppermute | solution.py:247
  225.5 6.0 %collective-permute-start.5 = (bf16[2,4,144,1152]{3,2,1,0:T(8,128)(2,1)}, bf16[2,4,144,1152]{3,2,1,0:T(8,128)(2,1)}, u32[]{:S(2)}, u32[]{:S(2)}) collective-permute-start(bf16[2,4,144,1152]{3,2,1,0:T(8,128)(2,1)} %collective-permute-done.2.refs_9_), channel_id=1, source_target_pairs={{0,1},{1,0},{2,3},{3,2},{4,5},{5,4},{6,7},{7,6},{8,9},{9,8},{10,11... | collective-permute-start | bytes 7962632 | tf_op jit(solution)/shard_map/ppermute | solution.py:247
  227.7 60.2 %collective-permute-start.1 = (bf16[2,4,144,1152]{3,2,1,0:T(8,128)(2,1)S(1)}, bf16[2,4,144,1152]{3,2,1,0:T(8,128)(2,1)}, u32[]{:S(2)}, u32[]{:S(2)}) collective-permute-start(bf16[2,4,144,1152]{3,2,1,0:T(8,128)(2,1)S(1)} %constant_dynamic-slice_fusion.4), channel_id=1, source_target_pairs={{0,16},{16,0},{1,17},{17,1},{2,18},{18,2},{3,19},{19,3},{4,20},{20... | collective-permute-start | bytes 7962632 | tf_op jit(solution)/shard_map/ppermute | solution.py:244
  287.9 29.9 %collective-permute-start.6 = (bf16[2,4,144,1152]{3,2,1,0:T(8,128)(2,1)}, bf16[2,4,144,1152]{3,2,1,0:T(8,128)(2,1)}, u32[]{:S(2)}, u32[]{:S(2)}) collective-permute-start(bf16[2,4,144,1152]{3,2,1,0:T(8,128)(2,1)} %collective-permute-done.1.refs_5_), channel_id=1, source_target_pairs={{0,1},{1,0},{2,3},{3,2},{4,5},{5,4},{6,7},{7,6},{8,9},{9,8},{10,11... | collective-permute-start | bytes 7962632 | tf_op jit(solution)/shard_map/ppermute | solution.py:247
  289.3 28.5 %collective-permute-start = (bf16[2,4,64,1152]{3,2,1,0:T(8,128)(2,1)S(1)}, bf16[2,4,64,1152]{3,2,1,0:T(8,128)(2,1)S(1)}, u32[]{:S(2)}, u32[]{:S(2)}) collective-permute-start(bf16[2,4,64,1152]{3,2,1,0:T(8,128)(2,1)S(1)} %constant_dynamic-slice_fusion.5), channel_id=1, source_target_pairs={{0,16},{16,0},{1,17},{17,1},{2,18},{18,2},{3,19},{19,3},{4,20},{20... | collective-permute-start | bytes 3538952 | tf_op jit(solution)/shard_map/ppermute | solution.py:244
  317.7 12.6 %collective-permute-start.7 = (bf16[2,4,64,1152]{3,2,1,0:T(8,128)(2,1)S(1)}, bf16[2,4,64,1152]{3,2,1,0:T(8,128)(2,1)S(1)}, u32[]{:S(2)}, u32[]{:S(2)}) collective-permute-start(bf16[2,4,64,1152]{3,2,1,0:T(8,128)(2,1)S(1)} %collective-permute-done.refs_4_), channel_id=1, source_target_pairs={{0,1},{1,0},{2,3},{3,2},{4,5},{5,4},{6,7},{7,6},{8,9},{9,8},{10,11... | collective-permute-start | bytes 3538952 | tf_op jit(solution)/shard_map/ppermute | solution.py:247
  345.3 8.7 %collective-permute-start.14 = (bf16[288,256]{1,0:T(8,128)(2,1)S(1)}, bf16[288,256]{1,0:T(8,128)(2,1)S(1)}, u32[]{:S(2)}, u32[]{:S(2)}) collective-permute-start(bf16[288,256]{1,0:T(8,128)(2,1)S(1)} %get-tuple-element.44), channel_id=1, source_target_pairs={{0,4},{4,8},{8,12},{12,0},{1,5},{5,9},{9,13},{13,1},{2,6},{6,10},{... | collective-permute-start | bytes 442376 | tf_op jit(solution)/shard_map/ppermute | solution.py:326
  346.9 13.5 %collective-permute-start.15 = (bf16[288,256]{1,0:T(8,128)(2,1)S(1)}, bf16[288,256]{1,0:T(8,128)(2,1)S(1)}, u32[]{:S(2)}, u32[]{:S(2)}) collective-permute-start(bf16[288,256]{1,0:T(8,128)(2,1)S(1)} %get-tuple-element.43), channel_id=1, source_target_pairs={{0,8},{4,12},{8,0},{12,4},{1,9},{5,13},{9,1},{13,5},{2,10},{6,14},... | collective-permute-start | bytes 442376 | tf_op jit(solution)/shard_map/ppermute | solution.py:326
  349.2 12.8 %collective-permute-start.16 = (bf16[288,256]{1,0:T(8,128)(2,1)S(1)}, bf16[288,256]{1,0:T(8,128)(2,1)S(1)}, u32[]{:S(2)}, u32[]{:S(2)}) collective-permute-start(bf16[288,256]{1,0:T(8,128)(2,1)S(1)} %get-tuple-element.42), channel_id=1, source_target_pairs={{0,12},{4,0},{8,4},{12,8},{1,13},{5,1},{9,5},{13,9},{2,14},{6,2},{... | collective-permute-start | bytes 442376 | tf_op jit(solution)/shard_map/ppermute | solution.py:326
  350.7 12.8 %collective-permute-start.8 = (bf16[288,256]{1,0:T(8,128)(2,1)S(1)}, bf16[288,256]{1,0:T(8,128)(2,1)S(1)}, u32[]{:S(2)}, u32[]{:S(2)}) collective-permute-start(bf16[288,256]{1,0:T(8,128)(2,1)S(1)} %get-tuple-element.48), channel_id=1, source_target_pairs={{0,4},{4,8},{8,12},{12,0},{1,5},{5,9},{9,13},{13,1},{2,6},{6,10},{... | collective-permute-start | bytes 442376 | tf_op jit(solution)/shard_map/ppermute | solution.py:326
  351.4 20.8 %collective-permute-start.9 = (bf16[288,256]{1,0:T(8,128)(2,1)S(1)}, bf16[288,256]{1,0:T(8,128)(2,1)S(1)}, u32[]{:S(2)}, u32[]{:S(2)}) collective-permute-start(bf16[288,256]{1,0:T(8,128)(2,1)S(1)} %get-tuple-element.47), channel_id=1, source_target_pairs={{0,8},{4,12},{8,0},{12,4},{1,9},{5,13},{9,1},{13,5},{2,10},{6,14},... | collective-permute-start | bytes 442376 | tf_op jit(solution)/shard_map/ppermute | solution.py:326
  354.0 18.1 %collective-permute-start.10 = (bf16[288,256]{1,0:T(8,128)(2,1)S(1)}, bf16[288,256]{1,0:T(8,128)(2,1)S(1)}, u32[]{:S(2)}, u32[]{:S(2)}) collective-permute-start(bf16[288,256]{1,0:T(8,128)(2,1)S(1)} %get-tuple-element.46), channel_id=1, source_target_pairs={{0,12},{4,0},{8,4},{12,8},{1,13},{5,1},{9,5},{13,9},{2,14},{6,2},{... | collective-permute-start | bytes 442376 | tf_op jit(solution)/shard_map/ppermute | solution.py:326
  362.1 14.3 %collective-permute-start.18 = (bf16[4,288,256]{2,1,0:T(8,128)(2,1)S(1)}, bf16[4,288,256]{2,1,0:T(8,128)(2,1)S(1)}, u32[]{:S(2)}, u32[]{:S(2)}) collective-permute-start(bf16[4,288,256]{2,1,0:T(8,128)(2,1)S(1)} %pad_maximum_fusion.3.refs_4_), channel_id=1, source_target_pairs={{0,2},{1,3},{2,0},{3,1},{4,6},{5,7},{6,4},{7,5},{8,10},{9,11},{10,... | collective-permute-start | bytes 1769480 | tf_op jit(solution)/shard_map/ppermute | solution.py:330
  372.2 16.0 %collective-permute-start.12 = (bf16[4,288,256]{2,1,0:T(8,128)(2,1)S(1)}, bf16[4,288,256]{2,1,0:T(8,128)(2,1)S(1)}, u32[]{:S(2)}, u32[]{:S(2)}) collective-permute-start(bf16[4,288,256]{2,1,0:T(8,128)(2,1)S(1)} %pad_maximum_fusion.2.refs_0_), channel_id=1, source_target_pairs={{0,2},{1,3},{2,0},{3,1},{4,6},{5,7},{6,4},{7,5},{8,10},{9,11},{10,... | collective-permute-start | bytes 1769480 | tf_op jit(solution)/shard_map/ppermute | solution.py:330
  372.3 15.9 %collective-permute-start.17 = (bf16[4,288,256]{2,1,0:T(8,128)(2,1)S(1)}, bf16[4,288,256]{2,1,0:T(8,128)(2,1)S(1)}, u32[]{:S(2)}, u32[]{:S(2)}) collective-permute-start(bf16[4,288,256]{2,1,0:T(8,128)(2,1)S(1)} %pad_maximum_fusion.3.refs_4_), channel_id=1, source_target_pairs={{0,1},{1,0},{2,3},{3,2},{4,5},{5,4},{6,7},{7,6},{8,9},{9,8},{10,11... | collective-permute-start | bytes 1769480 | tf_op jit(solution)/shard_map/ppermute | solution.py:330
  372.4 15.9 %collective-permute-start.11 = (bf16[4,288,256]{2,1,0:T(8,128)(2,1)S(1)}, bf16[4,288,256]{2,1,0:T(8,128)(2,1)S(1)}, u32[]{:S(2)}, u32[]{:S(2)}) collective-permute-start(bf16[4,288,256]{2,1,0:T(8,128)(2,1)S(1)} %pad_maximum_fusion.2.refs_0_), channel_id=1, source_target_pairs={{0,1},{1,0},{2,3},{3,2},{4,5},{5,4},{6,7},{7,6},{8,9},{9,8},{10,11... | collective-permute-start | bytes 1769480 | tf_op jit(solution)/shard_map/ppermute | solution.py:330
  376.4 11.9 %collective-permute-start.19 = (bf16[4,288,256]{2,1,0:T(8,128)(2,1)S(1)}, bf16[4,288,256]{2,1,0:T(8,128)(2,1)S(1)}, u32[]{:S(2)}, u32[]{:S(2)}) collective-permute-start(bf16[4,288,256]{2,1,0:T(8,128)(2,1)S(1)} %collective-permute-done.18.refs_6_), channel_id=1, source_target_pairs={{0,1},{1,0},{2,3},{3,2},{4,5},{5,4},{6,7},{7,6},{8,9},{9,8},{10,11... | collective-permute-start | bytes 1769480 | tf_op jit(solution)/shard_map/ppermute | solution.py:330
  (17 other events, 42.7 us)
Sparse Core Ops, SparseCore 0:
  9.5 62.7 all-gather.12
  73.9 116.5 all-gather.10
  192.1 66.0 all-gather.14
  259.7 38.5 all-gather.16

commit v7 on v5

--- a/solution.py
+++ b/solution.py
@@ -288,10 +288,13 @@
                                   cost_estimate=pl.CostEstimate(flops=flops, bytes_accessed=width * cols * ty * 4, transcendentals=n * cols * ty))
 
         for l in range(layers):
+            if l:
+                got["u", l], x = lax.optimization_barrier((got["u", l], x))
+                cross_core(("u", l))
             x = kernel(lambda *refs: attention_kernel(hl, dim, toks, *refs),
                        [whole, row, row, bias, row, pl.BlockSpec((tx, 1, wl, cols), lambda i: (0, i, 0, 0))],
                        whole, act, scratch, 4 * dot_flops)(x, vt[0, l], vt[1, l], bias_a[l], vt[4, l], proj[l])
-            late = halves[l + 1]
+            late = halves[2 * l + 1]
             got[late], x = lax.optimization_barrier((got[late], x))
             cross_core(late)
             up = (split["u", l][0], *crossed["u", l])
@@ -306,8 +309,6 @@
                 u = kernel(lambda *refs, o=(split["u", l][1],): up_kernel(o, *refs), [whole, row, row, bias] + [anywhere] * 3, hidden,
                            jax.ShapeDtypeStruct((ty, n, cols), BF), [rows_bf, half_buf, pltpu.SemaphoreType.DMA((2, 1, 3))],
                            2 * dot_flops)(x, vt[2, l], vt[3, l], bias_u[l], *up)
-                got["d", l], u = lax.optimization_barrier((got["d", l], u))
-                cross_core(("d", l))
                 down = (split["d", l][0], *crossed["d", l], last_down)
                 outs = []
                 for img in range(nb):

time: 384 us -> 400 us (1.042)
  waiting for transfers between devices: 157 us -> 213 us
  blocking collectives: 57 us -> 24.4 us
  starting transfers between devices: 27.1 us -> 19 us
    ppermute x4, waiting for transfers between devices: 11.6 us -> 71.9 us  [cross_plane(): got[key] = lax.ppermute(sent, 'dp', [(0, 1), (1, 0)])]
    all_gather x4, waiting for transfers between devices: 115 us -> 74.3 us  [gather(): full = lax.all_gather(block, ('tx', 'ty'), axis=0, axis_index_groups=groups)]
    all_to_all x1, waiting for transfers between devices: 0.01 us -> 37.1 us  [local_fn(): x_t = lax.all_to_all(images, 'tx', split_axis=0, concat_axis=0, tiled=True)]
    all_gather x1, blocking collectives: 57 us -> 24.4 us  [local_fn(): vec = lax.all_gather(own, ('tx', 'ty'), axis=0)]
    ppermute x6, starting transfers between devices: 5.12 us -> 0.72 us  [local_fn(): lax.ppermute(by_group[dist - bit], 'ty', [(i, i ^ bit) for i in range(ty)])]
    ppermute x4, waiting for transfers between devices: 5.97 us -> 1.65 us  [cross_core(): crossed[key] = (got[key], lax.ppermute(got[key], 'ty', swap))]
  transfers between devices with their start and end apart: 25 -> 25, of which waited for: 12 -> 13; matrix products, arithmetic and copies ran while one was open for 7% -> 7% of each run, Pallas kernels for 22% -> 21%
where the time goes in v7:
time: 400 us
  waiting for transfers between devices  213 us (53%)
  Pallas kernels  96.2 us (24%)
  local copies, waits for them, and re-layouts  31.2 us (8%)
  blocking collectives  24.4 us (6%)
  starting transfers between devices  19 us (5%)
  between operations  13.6 us (3%)
    all_gather x4, waiting for transfers between devices, gather(): full = lax.all_gather(block, ('tx', 'ty'), axis=0, axis_index_groups=groups)  74.3 us
    ppermute x4, waiting for transfers between devices, cross_plane(): got[key] = lax.ppermute(sent, 'dp', [(0, 1), (1, 0)])  71.9 us
    pallas_call x2, Pallas kernels, local_fn(): kernel(lambda *refs: attention_kernel(hl, dim, toks, *refs), [whole, row,...  42.3 us
    all_to_all x1, waiting for transfers between devices, local_fn(): x_t = lax.all_to_all(images, 'tx', split_axis=0, concat_axis=0, tiled=True)  37.1 us
    all_gather x1, blocking collectives, local_fn(): vec = lax.all_gather(own, ('tx', 'ty'), axis=0)  24.4 us
    pallas_call x1, Pallas kernels, local_fn(): kernel(lambda *refs, o=offsets: mlp_kernel(o, *refs), [whole, row, row, b...  20 us
    pallas_call x2, Pallas kernels, local_fn(): kernel(lambda *refs, o=(split['d', l][1],): down_kernel(order, o, *refs),...  18.9 us
    ppermute x6, waiting for transfers between devices, local_fn(): lax.ppermute(by_group[dist - bit], 'ty', [(i, i ^ bit) for i in range(ty)])  18.6 us
  transfers between devices with their start and end apart: 25, of which 13 were waited for; matrix products, arithmetic and copies ran while one was open for 7% of the time, Pallas kernels for 21%

profile of v7, /device:TPU:0, one launch (start us, length us, event | category | flops | bytes accessed | tf_op | source)
XLA Modules:
  0.0 399.6 jit_solution(13996231391744799039)
XLA Ops:
  19.3 53.0 %all-gather.13.cloned.1.call-done = bf16[4608,1152]{1,0:T(8,128)(2,1)} async-done(((bf16[288,1152]{1,0:T(8,128)(2,1)}), bf16[4608,1152]{1,0:T(8,128)(2,1)}) %all-gather.13.cloned.1.call-update) | async-done | bytes 10616848 | tf_op jit(solution)/shard_map/all_gather | solution.py:216
  72.3 5.4 %constant_dynamic-slice_fusion.2 = (bf16[2,4,144,1152]{3,2,1,0:T(8,128)(2,1)}, bf16[2,4,144,1152]{3,2,1,0:T(8,128)(2,1)}) fusion(bf16[4,4,288,1152]{3,2,1,0:T(8,128)(2,1)} %bitcast.136, s32[]{:T(128)S(6)} %select_n.68), kind=kLoop, calls=%fused_computation.54 | loop fusion | bytes 10616836 | tf_op jit(solution)/shard_map/dynamic_slice | solution.py:239
  77.9 24.4 %all-gather.5 = f32[16,1,6760]{2,1,0:T(1,128)S(1)} all-gather(f32[1,1,6760]{2,1,0:T(1,128)S(1)} %bitcast.157), channel_id=4, replica_groups=mesh['dp'=2,'tx'=4,'ty'=4] {'tx','ty'}, dimensions={0}, use_global_device_ids=true | all-gather | bytes 459680 | tf_op jit(solution)/shard_map/all_gather | solution.py:257
  102.2 2.4 dynamic-slice_bitcast_fusion
  104.7 3.7 all-to-all-start
  112.7 37.1 %all-to-all-done = bf16[8,288,256]{2,1,0:T(8,128)(2,1)S(1)} async-done(((bf16[8,288,256]{2,1,0:T(8,128)(2,1)}), bf16[8,288,256]{2,1,0:T(8,128)(2,1)S(1)}, u32[]{:S(2)}, u32[]{:S(2)}) %all-to-all-start) | async-done | bytes 1179680 | tf_op jit(solution)/shard_map/all_to_all | solution.py:252
  153.3 15.9 %collective-permute-done.3.refs_6_ = bf16[2,4,144,1152]{3,2,1,0:T(8,128)(2,1)} collective-permute-done((bf16[2,4,144,1152]{3,2,1,0:T(8,128)(2,1)}, bf16[2,4,144,1152]{3,2,1,0:T(8,128)(2,1)}, u32[]{:S(2)}, u32[]{:S(2)}) %collective-permute-start.3) | collective-permute-done | bytes 2654240 | tf_op jit(solution)/shard_map/ppermute | solution.py:242
  169.2 21.3 %all-gather.11.cloned.1.call-done = bf16[7936,1152]{1,0:T(8,128)(2,1)} async-done(((bf16[496,1152]{1,0:T(8,128)(2,1)}), bf16[7936,1152]{1,0:T(8,128)(2,1)}) %all-gather.11.cloned.1.call-update) | async-done | bytes 18284560 | tf_op jit(solution)/shard_map/all_gather | solution.py:216
  190.5 21.1 %shard_map.154.refs_0_ = bf16[512,1152]{1,0:T(8,128)(2,1)} custom-call(bf16[512,1152]{1,0:T(8,128)(2,1)} %reshape.123.refs_0_, f32[1,1152]{1,0:T(1,128)} %get-tuple-element.68.refs_1_, f32[1,1152]{1,0:T(1,128)} %get-tuple-element.67.refs_2_, f32[4,1,1152]{2,1,0:T(1,128)} %get-tuple-element.72.refs_3_, f32[1,1152]{1,0:T(1,128)} %get-tuple-element.66.refs_4_, ...), custom_call_target="tpu_custom_call" | custom-call | flops 21743271936 | bytes 21233664 | tf_op jit(solution)/shard_map/pallas_call | solution.py:294
  211.6 13.8 %collective-permute-done.2.refs_9_ = bf16[2,4,144,1152]{3,2,1,0:T(8,128)(2,1)} collective-permute-done((bf16[2,4,144,1152]{3,2,1,0:T(8,128)(2,1)}, bf16[2,4,144,1152]{3,2,1,0:T(8,128)(2,1)}, u32[]{:S(2)}, u32[]{:S(2)}) %collective-permute-start.2) | collective-permute-done | bytes 2654240 | tf_op jit(solution)/shard_map/ppermute | solution.py:242
  231.5 20.0 %shard_map.155.refs_0_ = bf16[512,1152]{1,0:T(8,128)(2,1)} custom-call(bf16[512,1152]{1,0:T(8,128)(2,1)} %shard_map.154.refs_0_, f32[1,1152]{1,0:T(1,128)} %get-tuple-element.65.refs_1_, f32[1,1152]{1,0:T(1,128)} %get-tuple-element.64.refs_2_, f32[4,1,1152]{2,1,0:T(1,128)} %get-tuple-element.70.refs_3_, f32[1,1152]{1,0:T(1,128)} %get-tuple-element.63.refs_4_, ...), custom_call_target="tpu_custom_call" | custom-call | flops 21743271936 | bytes 21233664 | tf_op jit(solution)/shard_map/pallas_call | solution.py:304
  251.5 36.4 %collective-permute-done.1.refs_5_ = bf16[2,4,144,1152]{3,2,1,0:T(8,128)(2,1)} collective-permute-done((bf16[2,4,144,1152]{3,2,1,0:T(8,128)(2,1)S(1)}, bf16[2,4,144,1152]{3,2,1,0:T(8,128)(2,1)}, u32[]{:S(2)}, u32[]{:S(2)}) %collective-permute-start.1) | collective-permute-done | bytes 2654240 | tf_op jit(solution)/shard_map/ppermute | solution.py:242
  290.8 21.2 %shard_map.156.refs_0_ = bf16[512,1152]{1,0:T(8,128)(2,1)} custom-call(bf16[512,1152]{1,0:T(8,128)(2,1)} %shard_map.155.refs_0_, f32[1,1152]{1,0:T(1,128)} %get-tuple-element.62.refs_1_, f32[1,1152]{1,0:T(1,128)} %get-tuple-element.61.refs_2_, f32[4,1,1152]{2,1,0:T(1,128)} %get-tuple-element.71.refs_3_, f32[1,1152]{1,0:T(1,128)} %get-tuple-element.60.refs_4_, ...), custom_call_target="tpu_custom_call" | custom-call | flops 21743271936 | bytes 21233664 | tf_op jit(solution)/shard_map/pallas_call | solution.py:294
  312.0 5.7 %collective-permute-done.refs_4_ = bf16[2,4,64,1152]{3,2,1,0:T(8,128)(2,1)S(1)} collective-permute-done((bf16[2,4,64,1152]{3,2,1,0:T(8,128)(2,1)S(1)}, bf16[2,4,64,1152]{3,2,1,0:T(8,128)(2,1)S(1)}, u32[]{:S(2)}, u32[]{:S(2)}) %collective-permute-start) | collective-permute-done | bytes 1179680 | tf_op jit(solution)/shard_map/ppermute | solution.py:242
  317.7 12.5 %shard_map.157.refs_2_ = bf16[4,512,1152]{2,1,0:T(8,128)(2,1)} custom-call(bf16[512,1152]{1,0:T(8,128)(2,1)} %shard_map.156.refs_0_, f32[1,1152]{1,0:T(1,128)} %get-tuple-element.58.refs_1_, f32[1,1152]{1,0:T(1,128)} %get-tuple-element.57.refs_2_, f32[4,1,1152]{2,1,0:T(1,128)} %get-tuple-element.69.refs_3_, bf16[4,4,496,1152]{3,2,1,0:T(8,128)(2,1)} %bitcast.131, ...), custom_call_target="tpu_custom_call" | custom-call | flops 10871635968 | bytes 21233664 | tf_op jit(solution)/shard_map/pallas_call | solution.py:309
  331.4 9.5 %shard_map.159 = bf16[4,288,256]{2,1,0:T(8,128)(2,1)} custom-call(bf16[512,1152]{1,0:T(8,128)(2,1)} %shard_map.156.refs_0_, f32[1,1152]{1,0:T(1,128)} %get-tuple-element.59.refs_1_, bf16[4,512,1152]{2,1,0:T(8,128)(2,1)} %shard_map.157.refs_2_, bf16[4,4,496,1152]{3,2,1,0:T(8,128)(2,1)} %bitcast.132, bf16[2,4,64,1152]{3,2,1,0:T(8,128)(2,1)} %copy-done, ...), custom_call_target="tpu_custom_call" | custom-call | flops 5435817984 | bytes 21233664 | tf_op jit(solution)/shard_map/pallas_call | solution.py:315
  343.6 2.3 collective-permute-start.15
  347.3 9.5 %shard_map.158 = bf16[4,288,256]{2,1,0:T(8,128)(2,1)} custom-call(bf16[512,1152]{1,0:T(8,128)(2,1)} %shard_map.156.refs_0_, f32[1,1152]{1,0:T(1,128)} %get-tuple-element.59.refs_1_, bf16[4,512,1152]{2,1,0:T(8,128)(2,1)} %shard_map.157.refs_2_, bf16[4,4,496,1152]{3,2,1,0:T(8,128)(2,1)} %bitcast.133, bf16[2,4,64,1152]{3,2,1,0:T(8,128)(2,1)} %copy-done, ...), custom_call_target="tpu_custom_call" | custom-call | flops 5435817984 | bytes 21233664 | tf_op jit(solution)/shard_map/pallas_call | solution.py:315
  359.2 2.7 collective-permute-start.10
  362.1 4.5 %collective-permute-done.8 = bf16[288,256]{1,0:T(8,128)(2,1)S(1)} collective-permute-done((bf16[288,256]{1,0:T(8,128)(2,1)S(1)}, bf16[288,256]{1,0:T(8,128)(2,1)S(1)}, u32[]{:S(2)}, u32[]{:S(2)}) %collective-permute-start.8) | collective-permute-done | bytes 147488 | tf_op jit(solution)/shard_map/ppermute | solution.py:329
  366.6 4.7 %collective-permute-done.9 = bf16[288,256]{1,0:T(8,128)(2,1)S(1)} collective-permute-done((bf16[288,256]{1,0:T(8,128)(2,1)S(1)}, bf16[288,256]{1,0:T(8,128)(2,1)S(1)}, u32[]{:S(2)}, u32[]{:S(2)}) %collective-permute-start.9) | collective-permute-done | bytes 147488 | tf_op jit(solution)/shard_map/ppermute | solution.py:329
  372.0 6.3 %collective-permute-done.18.refs_6_ = bf16[4,288,256]{2,1,0:T(8,128)(2,1)S(1)} collective-permute-done((bf16[4,288,256]{2,1,0:T(8,128)(2,1)S(1)}, bf16[4,288,256]{2,1,0:T(8,128)(2,1)S(1)}, u32[]{:S(2)}, u32[]{:S(2)}) %collective-permute-start.18) | collective-permute-done | bytes 589856 | tf_op jit(solution)/shard_map/ppermute | solution.py:333
  378.3 10.3 %collective-permute-done.12.refs_2_ = bf16[4,288,256]{2,1,0:T(8,128)(2,1)S(1)} collective-permute-done((bf16[4,288,256]{2,1,0:T(8,128)(2,1)S(1)}, bf16[4,288,256]{2,1,0:T(8,128)(2,1)S(1)}, u32[]{:S(2)}, u32[]{:S(2)}) %collective-permute-start.12) | collective-permute-done | bytes 589856 | tf_op jit(solution)/shard_map/ppermute | solution.py:333
  390.6 2.4 place.1
  (129 shorter events, 39.8 us)
Async XLA Ops:
  6.5 65.7 %all-gather.13.cloned.1.call-start = ((), (), s32[]{:S(2)}) async-start(), calls=%async_computation.2 | async-start | bytes 11280384 | tf_op jit(solution)/shard_map/all_gather | solution.py:216
  9.4 181.1 %all-gather.11.cloned.1.call-start = ((), (), s32[]{:S(2)}) async-start(), calls=%async_computation.1 | async-start | bytes 19427328 | tf_op jit(solution)/shard_map/all_gather | solution.py:216
  15.5 275.2 %all-gather.15.cloned.1.call-start = ((), (), s32[]{:S(2)}) async-start(), calls=%async_computation.3 | async-start | bytes 11280384 | tf_op jit(solution)/shard_map/all_gather | solution.py:216
  17.7 312.6 %all-gather.17.cloned.1.call-start = ((), (), s32[]{:S(2)}) async-start(), calls=%async_computation.4 | async-start | bytes 6266880 | tf_op jit(solution)/shard_map/all_gather | solution.py:216
  104.7 45.2 %all-to-all-start = ((bf16[8,288,256]{2,1,0:T(8,128)(2,1)}), bf16[8,288,256]{2,1,0:T(8,128)(2,1)S(1)}, u32[]{:S(2)}, u32[]{:S(2)}) async-start(bf16[8,288,256]{2,1,0:T(8,128)(2,1)} %dynamic-slice_bitcast_fusion), calls=%async_computation | async-start | bytes 2359296 | tf_op jit(solution)/shard_map/all_to_all | solution.py:252
  108.4 60.8 %collective-permute-start.3 = (bf16[2,4,144,1152]{3,2,1,0:T(8,128)(2,1)}, bf16[2,4,144,1152]{3,2,1,0:T(8,128)(2,1)}, u32[]{:S(2)}, u32[]{:S(2)}) collective-permute-start(bf16[2,4,144,1152]{3,2,1,0:T(8,128)(2,1)} %get-tuple-element.19), channel_id=1, source_target_pairs={{0,16},{16,0},{1,17},{17,1},{2,18},{18,2},{3,19},{19,3},{4,20},{20... | collective-permute-start | bytes 7962632 | tf_op jit(solution)/shard_map/ppermute | solution.py:242
  110.6 114.9 %collective-permute-start.2 = (bf16[2,4,144,1152]{3,2,1,0:T(8,128)(2,1)}, bf16[2,4,144,1152]{3,2,1,0:T(8,128)(2,1)}, u32[]{:S(2)}, u32[]{:S(2)}) collective-permute-start(bf16[2,4,144,1152]{3,2,1,0:T(8,128)(2,1)} %get-tuple-element.15), channel_id=1, source_target_pairs={{0,16},{16,0},{1,17},{17,1},{2,18},{18,2},{3,19},{19,3},{4,20},{20... | collective-permute-start | bytes 7962632 | tf_op jit(solution)/shard_map/ppermute | solution.py:242
  169.2 60.6 %collective-permute-start.4 = (bf16[2,4,144,1152]{3,2,1,0:T(8,128)(2,1)}, bf16[2,4,144,1152]{3,2,1,0:T(8,128)(2,1)}, u32[]{:S(2)}, u32[]{:S(2)}) collective-permute-start(bf16[2,4,144,1152]{3,2,1,0:T(8,128)(2,1)} %collective-permute-done.3.refs_6_), channel_id=1, source_target_pairs={{0,1},{1,0},{2,3},{3,2},{4,5},{5,4},{6,7},{7,6},{8,9},{9,8},{10,11... | collective-permute-start | bytes 7962632 | tf_op jit(solution)/shard_map/ppermute | solution.py:245
  225.4 6.0 %collective-permute-start.5 = (bf16[2,4,144,1152]{3,2,1,0:T(8,128)(2,1)}, bf16[2,4,144,1152]{3,2,1,0:T(8,128)(2,1)}, u32[]{:S(2)}, u32[]{:S(2)}) collective-permute-start(bf16[2,4,144,1152]{3,2,1,0:T(8,128)(2,1)} %collective-permute-done.2.refs_9_), channel_id=1, source_target_pairs={{0,1},{1,0},{2,3},{3,2},{4,5},{5,4},{6,7},{7,6},{8,9},{9,8},{10,11... | collective-permute-start | bytes 7962632 | tf_op jit(solution)/shard_map/ppermute | solution.py:245
  227.6 60.2 %collective-permute-start.1 = (bf16[2,4,144,1152]{3,2,1,0:T(8,128)(2,1)S(1)}, bf16[2,4,144,1152]{3,2,1,0:T(8,128)(2,1)}, u32[]{:S(2)}, u32[]{:S(2)}) collective-permute-start(bf16[2,4,144,1152]{3,2,1,0:T(8,128)(2,1)S(1)} %constant_dynamic-slice_fusion.4), channel_id=1, source_target_pairs={{0,16},{16,0},{1,17},{17,1},{2,18},{18,2},{3,19},{19,3},{4,20},{20... | collective-permute-start | bytes 7962632 | tf_op jit(solution)/shard_map/ppermute | solution.py:242
  287.9 29.9 %collective-permute-start.6 = (bf16[2,4,144,1152]{3,2,1,0:T(8,128)(2,1)}, bf16[2,4,144,1152]{3,2,1,0:T(8,128)(2,1)}, u32[]{:S(2)}, u32[]{:S(2)}) collective-permute-start(bf16[2,4,144,1152]{3,2,1,0:T(8,128)(2,1)} %collective-permute-done.1.refs_5_), channel_id=1, source_target_pairs={{0,1},{1,0},{2,3},{3,2},{4,5},{5,4},{6,7},{7,6},{8,9},{9,8},{10,11... | collective-permute-start | bytes 7962632 | tf_op jit(solution)/shard_map/ppermute | solution.py:245
  289.3 28.5 %collective-permute-start = (bf16[2,4,64,1152]{3,2,1,0:T(8,128)(2,1)S(1)}, bf16[2,4,64,1152]{3,2,1,0:T(8,128)(2,1)S(1)}, u32[]{:S(2)}, u32[]{:S(2)}) collective-permute-start(bf16[2,4,64,1152]{3,2,1,0:T(8,128)(2,1)S(1)} %constant_dynamic-slice_fusion.5), channel_id=1, source_target_pairs={{0,16},{16,0},{1,17},{17,1},{2,18},{18,2},{3,19},{19,3},{4,20},{20... | collective-permute-start | bytes 3538952 | tf_op jit(solution)/shard_map/ppermute | solution.py:242
  317.7 12.6 %collective-permute-start.7 = (bf16[2,4,64,1152]{3,2,1,0:T(8,128)(2,1)S(1)}, bf16[2,4,64,1152]{3,2,1,0:T(8,128)(2,1)S(1)}, u32[]{:S(2)}, u32[]{:S(2)}) collective-permute-start(bf16[2,4,64,1152]{3,2,1,0:T(8,128)(2,1)S(1)} %collective-permute-done.refs_4_), channel_id=1, source_target_pairs={{0,1},{1,0},{2,3},{3,2},{4,5},{5,4},{6,7},{7,6},{8,9},{9,8},{10,11... | collective-permute-start | bytes 3538952 | tf_op jit(solution)/shard_map/ppermute | solution.py:245
  342.0 17.2 %collective-permute-start.14 = (bf16[288,256]{1,0:T(8,128)(2,1)S(1)}, bf16[288,256]{1,0:T(8,128)(2,1)S(1)}, u32[]{:S(2)}, u32[]{:S(2)}) collective-permute-start(bf16[288,256]{1,0:T(8,128)(2,1)S(1)} %get-tuple-element.40), channel_id=1, source_target_pairs={{0,4},{4,8},{8,12},{12,0},{1,5},{5,9},{9,13},{13,1},{2,6},{6,10},{... | collective-permute-start | bytes 442376 | tf_op jit(solution)/shard_map/ppermute | solution.py:329
  343.6 18.3 %collective-permute-start.15 = (bf16[288,256]{1,0:T(8,128)(2,1)S(1)}, bf16[288,256]{1,0:T(8,128)(2,1)S(1)}, u32[]{:S(2)}, u32[]{:S(2)}) collective-permute-start(bf16[288,256]{1,0:T(8,128)(2,1)S(1)} %get-tuple-element.39), channel_id=1, source_target_pairs={{0,8},{4,12},{8,0},{12,4},{1,9},{5,13},{9,1},{13,5},{2,10},{6,14},... | collective-permute-start | bytes 442376 | tf_op jit(solution)/shard_map/ppermute | solution.py:329
  345.9 16.0 %collective-permute-start.16 = (bf16[288,256]{1,0:T(8,128)(2,1)S(1)}, bf16[288,256]{1,0:T(8,128)(2,1)S(1)}, u32[]{:S(2)}, u32[]{:S(2)}) collective-permute-start(bf16[288,256]{1,0:T(8,128)(2,1)S(1)} %get-tuple-element.38), channel_id=1, source_target_pairs={{0,12},{4,0},{8,4},{12,8},{1,13},{5,1},{9,5},{13,9},{2,14},{6,2},{... | collective-permute-start | bytes 442376 | tf_op jit(solution)/shard_map/ppermute | solution.py:329
  358.0 8.6 %collective-permute-start.8 = (bf16[288,256]{1,0:T(8,128)(2,1)S(1)}, bf16[288,256]{1,0:T(8,128)(2,1)S(1)}, u32[]{:S(2)}, u32[]{:S(2)}) collective-permute-start(bf16[288,256]{1,0:T(8,128)(2,1)S(1)} %get-tuple-element.44), channel_id=1, source_target_pairs={{0,4},{4,8},{8,12},{12,0},{1,5},{5,9},{9,13},{13,1},{2,6},{6,10},{... | collective-permute-start | bytes 442376 | tf_op jit(solution)/shard_map/ppermute | solution.py:329
  358.6 12.7 %collective-permute-start.9 = (bf16[288,256]{1,0:T(8,128)(2,1)S(1)}, bf16[288,256]{1,0:T(8,128)(2,1)S(1)}, u32[]{:S(2)}, u32[]{:S(2)}) collective-permute-start(bf16[288,256]{1,0:T(8,128)(2,1)S(1)} %get-tuple-element.43), channel_id=1, source_target_pairs={{0,8},{4,12},{8,0},{12,4},{1,9},{5,13},{9,1},{13,5},{2,10},{6,14},... | collective-permute-start | bytes 442376 | tf_op jit(solution)/shard_map/ppermute | solution.py:329
  359.2 12.0 %collective-permute-start.10 = (bf16[288,256]{1,0:T(8,128)(2,1)S(1)}, bf16[288,256]{1,0:T(8,128)(2,1)S(1)}, u32[]{:S(2)}, u32[]{:S(2)}) collective-permute-start(bf16[288,256]{1,0:T(8,128)(2,1)S(1)} %get-tuple-element.42), channel_id=1, source_target_pairs={{0,12},{4,0},{8,4},{12,8},{1,13},{5,1},{9,5},{13,9},{2,14},{6,2},{... | collective-permute-start | bytes 442376 | tf_op jit(solution)/shard_map/ppermute | solution.py:329
  362.0 16.3 %collective-permute-start.18 = (bf16[4,288,256]{2,1,0:T(8,128)(2,1)S(1)}, bf16[4,288,256]{2,1,0:T(8,128)(2,1)S(1)}, u32[]{:S(2)}, u32[]{:S(2)}) collective-permute-start(bf16[4,288,256]{2,1,0:T(8,128)(2,1)S(1)} %pad_maximum_fusion.3.refs_4_), channel_id=1, source_target_pairs={{0,2},{1,3},{2,0},{3,1},{4,6},{5,7},{6,4},{7,5},{8,10},{9,11},{10,... | collective-permute-start | bytes 1769480 | tf_op jit(solution)/shard_map/ppermute | solution.py:333
  371.3 17.2 %collective-permute-start.12 = (bf16[4,288,256]{2,1,0:T(8,128)(2,1)S(1)}, bf16[4,288,256]{2,1,0:T(8,128)(2,1)S(1)}, u32[]{:S(2)}, u32[]{:S(2)}) collective-permute-start(bf16[4,288,256]{2,1,0:T(8,128)(2,1)S(1)} %pad_maximum_fusion.2.refs_0_), channel_id=1, source_target_pairs={{0,2},{1,3},{2,0},{3,1},{4,6},{5,7},{6,4},{7,5},{8,10},{9,11},{10,... | collective-permute-start | bytes 1769480 | tf_op jit(solution)/shard_map/ppermute | solution.py:333
  371.4 17.2 %collective-permute-start.17 = (bf16[4,288,256]{2,1,0:T(8,128)(2,1)S(1)}, bf16[4,288,256]{2,1,0:T(8,128)(2,1)S(1)}, u32[]{:S(2)}, u32[]{:S(2)}) collective-permute-start(bf16[4,288,256]{2,1,0:T(8,128)(2,1)S(1)} %pad_maximum_fusion.3.refs_4_), channel_id=1, source_target_pairs={{0,1},{1,0},{2,3},{3,2},{4,5},{5,4},{6,7},{7,6},{8,9},{9,8},{10,11... | collective-permute-start | bytes 1769480 | tf_op jit(solution)/shard_map/ppermute | solution.py:333
  371.5 17.1 %collective-permute-start.11 = (bf16[4,288,256]{2,1,0:T(8,128)(2,1)S(1)}, bf16[4,288,256]{2,1,0:T(8,128)(2,1)S(1)}, u32[]{:S(2)}, u32[]{:S(2)}) collective-permute-start(bf16[4,288,256]{2,1,0:T(8,128)(2,1)S(1)} %pad_maximum_fusion.2.refs_0_), channel_id=1, source_target_pairs={{0,1},{1,0},{2,3},{3,2},{4,5},{5,4},{6,7},{7,6},{8,9},{9,8},{10,11... | collective-permute-start | bytes 1769480 | tf_op jit(solution)/shard_map/ppermute | solution.py:333
  378.3 10.4 %collective-permute-start.19 = (bf16[4,288,256]{2,1,0:T(8,128)(2,1)S(1)}, bf16[4,288,256]{2,1,0:T(8,128)(2,1)S(1)}, u32[]{:S(2)}, u32[]{:S(2)}) collective-permute-start(bf16[4,288,256]{2,1,0:T(8,128)(2,1)S(1)} %collective-permute-done.18.refs_6_), channel_id=1, source_target_pairs={{0,1},{1,0},{2,3},{3,2},{4,5},{5,4},{6,7},{7,6},{8,9},{9,8},{10,11... | collective-permute-start | bytes 1769480 | tf_op jit(solution)/shard_map/ppermute | solution.py:333
  (16 other events, 36.3 us)
Sparse Core Ops, SparseCore 0:
  9.5 62.7 all-gather.12
  73.9 116.5 all-gather.10
  192.1 66.0 all-gather.14
  259.6 38.5 all-gather.16
